TPU v7x, 32 devices: a whole 2x2x4 slice. The times are simulated.
32 devices in a mesh: dp: 4 (over z), expert: 8 (over y, x, core).
Axes of the slice: x: 2, y: 2, z: 4, core: 2. Of those that a mesh axis runs over, the one named last changes fastest.
Arguments:
- layer_input: bfloat16 [8192, 768], P(('dp', 'expert')), may hold values from -6 to 6
- prev_logits: float32 [8192, 12], P(('dp', 'expert')), may hold values from -3 to 3
- segments: int32 [32, 256], P(('dp', 'expert')), may hold values from 0 to 3, never falling along the last dimension, each value on 1 to 128 neighbouring positions
- routes: int32 [8192, 2], P(('dp', 'expert')), may hold values from 0 to 11, all different within a row; in each aligned block of 256 rows (0 to 255, 256 to 511, ...) at most 64 rows name the same one
- cotangent: bfloat16 [8192, 768], P(('dp', 'expert')), may hold values from -6 to 6
- gain_attn: bfloat16 [768], P('dp'), may hold values from 0.5 to 1.5
- qkv_weight: bfloat16 [768, 2304], P('dp'), may hold values from -0.21875 to 0.21875
- out_weight: bfloat16 [768, 768], P('dp'), may hold values from -1.75 to 1.75
- gain_moe: bfloat16 [768], P('dp'), may hold values from 0.5 to 1.5
- router: bfloat16 [768, 12], P('dp'), may hold values from -0.109375 to 0.109375
- const_w: bfloat16 [768, 4], P('dp'), may hold values from -0.21875 to 0.21875
- const_v: bfloat16 [2, 768], P(None, 'dp'), may hold values from -24 to 24
- exp_gate: bfloat16 [768, 16384], P('dp', 'expert'), may hold values from -0.21875 to 0.21875
- exp_up: bfloat16 [768, 16384], P('dp', 'expert'), may hold values from -0.21875 to 0.21875
- exp_down: bfloat16 [16384, 768], P('expert', 'dp'), may hold values from -1 to 1
Outputs:
- layer_output: bfloat16 [8192, 768], P(('dp', 'expert'))
- grad_input: float32 [8192, 768], P(('dp', 'expert'))
- grad_prev: float32 [8192, 12], P(('dp', 'expert'))
- grad_gain_attn: float32 [768], P('dp')
- grad_qkv_weight: float32 [768, 2304], P('dp')
- grad_out_weight: float32 [768, 768], P('dp')
- grad_gain_moe: float32 [768], P('dp')
- grad_router: float32 [768, 12], P('dp')
- grad_const_w: float32 [768, 4], P('dp')
- grad_const_v: float32 [2, 768], P(None, 'dp')
- grad_exp_gate: float32 [768, 16384], P('dp', 'expert')
- grad_exp_up: float32 [768, 16384], P('dp', 'expert')
- grad_exp_down: float32 [16384, 768], P('expert', 'dp')
Inputs may be any that keep to these rules, and one draw needn't show every extreme that they name: `routes`: in the 256 rows of one device no id is named by more than 64 rows, a bound that some block reaches; a row's two ids differ. Ids below 8 are feed-forward experts, 8 is the zero expert, 9 the copy expert, the last 2 the constant experts. `segments`: along a sequence the ids never fall.
All inputs are finite; a program needn't handle non-finite values.
Results may differ from a plain program's by a relative error of at most 0.019.
Values may be sent and summed in bfloat16 or wider, within the bound.
A program may use at most 128 MiB of HBM per device.

v0:
```python
import math

import jax
import jax.numpy as jnp
from jax import lax
from jax.sharding import PartitionSpec as P

HEADS = 12
EXPERTS = 8
NC = 2
NR = 12
CAP = 64


EPSILON = 1e-06
NEGATIVE = -1e30
FULL_PRECISION = lax.Precision.HIGHEST


def rope_tables(length, head_dim):
    half_dim = head_dim // 2
    places = jnp.arange(length, dtype=jnp.float32)
    inv_rates = jnp.exp(
        jnp.arange(half_dim, dtype=jnp.float32) * (-2.0 * math.log(10000.0) / head_dim)
    )
    angles = places[:, None] * inv_rates[None, :]
    return (jnp.cos(angles), jnp.sin(angles))


def rotate(vectors, cosine, sine_table):
    half_dim = vectors.shape[-1] // 2
    first_half = vectors[..., :half_dim]
    second_half = vectors[..., half_dim:]
    cos_wide = cosine[:, None, :]
    sin_wide = sine_table[:, None, :]
    return jnp.concatenate(
        [
            first_half * cos_wide - second_half * sin_wide,
            second_half * cos_wide + first_half * sin_wide,
        ],
        axis=-1,
    )


def unrotate(gradients, cosine, sine_table):
    half_dim = gradients.shape[-1] // 2
    first_half = gradients[..., :half_dim]
    second_half = gradients[..., half_dim:]
    cos_wide = cosine[:, None, :]
    sin_wide = sine_table[:, None, :]
    return jnp.concatenate(
        [
            first_half * cos_wide + second_half * sin_wide,
            second_half * cos_wide - first_half * sin_wide,
        ],
        axis=-1,
    )


def norm_forward(values, gain_values):
    inverse = lax.rsqrt(jnp.mean(values * values, axis=-1) + EPSILON)
    return (values * inverse[:, None] * gain_values, inverse)


def norm_back(values, inverse, gain_values, gradients):
    scaled = gradients * gain_values
    inner_mean = jnp.mean(values * scaled, axis=-1)
    grad_values = (
        inverse[:, None] * scaled - values * (inverse * inverse * inverse * inner_mean)[:, None]
    )
    grad_gain = jnp.sum(gradients * values * inverse[:, None], axis=0)
    return (grad_values, grad_gain)


def route_slots(routes):
    assigned = routes.shape[0] * routes.shape[1]
    flat_routes = routes.reshape(assigned)
    onehot = (flat_routes[:, None] == jnp.arange(NR, dtype=jnp.int32)[None, :]).astype(jnp.int32)
    before = jnp.cumsum(onehot, axis=0) - onehot
    slot_ids = jnp.sum(before * onehot, axis=1)
    target = jnp.where(flat_routes < EXPERTS, flat_routes * CAP + slot_ids, EXPERTS * CAP)
    slot_table = (
        jnp.full((EXPERTS * CAP + 1,), assigned, jnp.int32)
        .at[target]
        .set(jnp.arange(assigned, dtype=jnp.int32))
    )
    return (target, slot_table[: EXPERTS * CAP])


def block_scores(query_rows, key_rows, query_segments, segment_ids, offset, score_scale):
    block_rows = query_rows.shape[0]
    places = jnp.arange(key_rows.shape[0])
    scores = (
        jnp.einsum("qd,kd->qk", query_rows, key_rows, preferred_element_type=jnp.float32)
        * score_scale
    )
    allowed = (query_segments[:, None] == segment_ids[None, :]) & (
        (offset + jnp.arange(block_rows))[:, None] >= places[None, :]
    )
    return jnp.where(allowed, scores, NEGATIVE)


def head_forward(queries, key_rows, values, segment_ids, score_scale):
    length = key_rows.shape[0]
    block_rows = min(512, length)

    def one_block(block_id):
        offset = block_id * block_rows
        scores = block_scores(queries, key_rows, segment_ids, segment_ids, offset, score_scale)
        highest = jnp.max(scores, axis=1, keepdims=True)
        weights = jnp.exp(scores - highest)
        totals = jnp.sum(weights, axis=1, keepdims=True)
        mixed_rows = jnp.dot(
            (weights / totals).astype(jnp.bfloat16), values, preferred_element_type=jnp.float32
        )
        return (mixed_rows, (highest + jnp.log(totals))[:, 0])

    outputs, log_sums = lax.map(one_block, jnp.arange(length // block_rows))
    return (outputs.reshape(length, -1), log_sums.reshape(length))


def head_backward(queries, key_rows, values, log_sums, gradients, segment_ids, score_scale):
    length = key_rows.shape[0]
    block_rows = min(512, length)

    def one_block(carried, block_id):
        grad_keys, grad_values = carried
        offset = block_id * block_rows
        scores = block_scores(queries, key_rows, segment_ids, segment_ids, offset, score_scale)
        weights = jnp.exp(scores - log_sums[:, None])
        grad_weights = jnp.einsum(
            "qd,kd->qk", gradients, values, preferred_element_type=jnp.float32
        )
        inner_sum = jnp.sum(weights * grad_weights, axis=1, keepdims=True)
        grad_scores = (weights * (grad_weights - inner_sum)).astype(jnp.bfloat16)
        grad_queries = (
            jnp.einsum("qk,kd->qd", grad_scores, key_rows, preferred_element_type=jnp.float32)
            * score_scale
        )
        grad_keys = (
            grad_keys
            + jnp.einsum("qk,qd->kd", grad_scores, queries, preferred_element_type=jnp.float32)
            * score_scale
        )
        grad_values = grad_values + jnp.einsum(
            "qk,qd->kd", weights.astype(jnp.bfloat16), gradients, preferred_element_type=jnp.float32
        )
        return ((grad_keys, grad_values), grad_queries)

    zero_rows = jnp.zeros((length, key_rows.shape[1]), jnp.float32)
    (grad_keys, grad_values), grad_queries = lax.scan(
        one_block, (zero_rows, zero_rows), jnp.arange(length // block_rows)
    )
    return (grad_queries.reshape(length, -1), grad_keys, grad_values)


def expert_forward(received, gate_weight, up_weight, down_weight, windows):
    sources, slot_count, features = received.shape
    row_count = sources * slot_count
    block_rows = 2048 if row_count % 2048 == 0 else row_count
    blocked = received.reshape(row_count // block_rows, block_rows, features)
    window_width = gate_weight.shape[1] // windows
    down_windows = down_weight.reshape(windows, window_width, features)

    def one_block(token_rows):
        gate_pre = jnp.dot(token_rows, gate_weight, preferred_element_type=jnp.float32)
        up_pre = jnp.dot(token_rows, up_weight, preferred_element_type=jnp.float32)
        hidden_rows = (
            (jax.nn.silu(gate_pre) * up_pre)
            .astype(jnp.bfloat16)
            .reshape(block_rows, windows, window_width)
        )
        window_rows = jnp.einsum(
            "rwf,wfd->rwd", hidden_rows, down_windows, preferred_element_type=jnp.float32
        ).astype(jnp.bfloat16)
        return jnp.sum(window_rows.astype(jnp.float32), axis=1)

    return lax.map(one_block, blocked).reshape(sources, slot_count, features)


def expert_backward(token_rows_all, grad_all, gate_weight, up_weight, down_weight, windows):
    sources, slot_count, features = token_rows_all.shape
    row_count = sources * slot_count
    block_rows = 2048 if row_count % 2048 == 0 else row_count
    block_count = row_count // block_rows
    blocked_rows = token_rows_all.reshape(block_count, block_rows, features)
    blocked_grads = grad_all.reshape(block_count, block_rows, features)
    hidden_dim = gate_weight.shape[1]
    window_width = hidden_dim // windows
    gate_windows = gate_weight.reshape(features, windows, window_width)
    up_windows = up_weight.reshape(features, windows, window_width)
    start_sums = (
        jnp.zeros((features, hidden_dim), jnp.float32),
        jnp.zeros((features, hidden_dim), jnp.float32),
        jnp.zeros((hidden_dim, features), jnp.float32),
    )

    def one_block(carried, block_items):
        token_rows, grad_rows = block_items
        gate_pre = jnp.dot(token_rows, gate_weight, preferred_element_type=jnp.float32)
        up_pre = jnp.dot(token_rows, up_weight, preferred_element_type=jnp.float32)
        sigmoid_gate = jax.nn.sigmoid(gate_pre)
        silu_gate = gate_pre * sigmoid_gate
        hidden_rows = (silu_gate * up_pre).astype(jnp.bfloat16)
        grad_hidden = jnp.einsum(
            "rd,fd->rf", grad_rows, down_weight, preferred_element_type=jnp.float32
        )
        grad_up_pre = (grad_hidden * silu_gate).astype(jnp.bfloat16)
        grad_gate_pre = (
            grad_hidden * up_pre * sigmoid_gate * (1.0 + gate_pre * (1.0 - sigmoid_gate))
        ).astype(jnp.bfloat16)
        sum_gate = carried[0] + jnp.einsum(
            "rd,rf->df", token_rows, grad_gate_pre, preferred_element_type=jnp.float32
        )
        sum_up = carried[1] + jnp.einsum(
            "rd,rf->df", token_rows, grad_up_pre, preferred_element_type=jnp.float32
        )
        sum_down = carried[2] + jnp.einsum(
            "rf,rd->fd", hidden_rows, grad_rows, preferred_element_type=jnp.float32
        )
        gate_split = grad_gate_pre.reshape(block_rows, windows, window_width)
        up_split = grad_up_pre.reshape(block_rows, windows, window_width)
        window_grads = jnp.einsum(
            "rwf,dwf->rwd", gate_split, gate_windows, preferred_element_type=jnp.float32
        ) + jnp.einsum("rwf,dwf->rwd", up_split, up_windows, preferred_element_type=jnp.float32)
        grad_tokens = jnp.sum(window_grads.astype(jnp.bfloat16).astype(jnp.float32), axis=1)
        return ((sum_gate, sum_up, sum_down), grad_tokens)

    weight_sums, grad_tokens = lax.scan(one_block, start_sums, (blocked_rows, blocked_grads))
    return (
        grad_tokens.reshape(sources, slot_count, features),
        weight_sums[0],
        weight_sums[1],
        weight_sums[2],
    )


def reduce_owners(pieces):
    return (
        lax.psum_scatter(
            pieces[0].astype(jnp.bfloat16), "dp", scatter_dimension=0, tiled=True
        ).astype(jnp.float32),
        lax.psum_scatter(
            pieces[1].astype(jnp.bfloat16), "dp", scatter_dimension=0, tiled=True
        ).astype(jnp.float32),
        lax.psum_scatter(
            pieces[2].astype(jnp.bfloat16), "dp", scatter_dimension=0, tiled=True
        ).astype(jnp.float32),
        lax.psum_scatter(
            pieces[3].astype(jnp.bfloat16), "dp", scatter_dimension=0, tiled=True
        ).astype(jnp.float32),
        lax.psum_scatter(
            pieces[4].astype(jnp.bfloat16), "dp", scatter_dimension=0, tiled=True
        ).astype(jnp.float32),
        lax.psum_scatter(
            pieces[5].astype(jnp.bfloat16), "dp", scatter_dimension=0, tiled=True
        ).astype(jnp.float32),
        lax.psum_scatter(
            pieces[6].astype(jnp.bfloat16), "dp", scatter_dimension=1, tiled=True
        ).astype(jnp.float32),
        lax.psum_scatter(
            pieces[7].astype(jnp.bfloat16), "dp", scatter_dimension=0, tiled=True
        ).astype(jnp.float32),
        lax.psum_scatter(
            pieces[8].astype(jnp.bfloat16), "dp", scatter_dimension=0, tiled=True
        ).astype(jnp.float32),
        lax.psum_scatter(
            pieces[9].astype(jnp.bfloat16), "dp", scatter_dimension=1, tiled=True
        ).astype(jnp.float32),
    )


def sum_replicas(pieces):
    return (
        lax.psum(pieces[0].astype(jnp.bfloat16), "expert").astype(jnp.float32),
        lax.psum(pieces[1].astype(jnp.bfloat16), "expert").astype(jnp.float32),
        lax.psum(pieces[2].astype(jnp.bfloat16), "expert").astype(jnp.float32),
        lax.psum(pieces[3].astype(jnp.bfloat16), "expert").astype(jnp.float32),
        lax.psum(pieces[4].astype(jnp.bfloat16), "expert").astype(jnp.float32),
        lax.psum(pieces[5].astype(jnp.bfloat16), "expert").astype(jnp.float32),
        lax.psum(pieces[6].astype(jnp.bfloat16), "expert").astype(jnp.float32),
    )


def local(
    layer_input,
    prev_logits,
    segments,
    routes,
    cotangent,
    gain_attn,
    qkv_weight,
    out_weight,
    gain_moe,
    router,
    const_w,
    const_v,
    exp_gate,
    exp_up,
    exp_down,
):
    gathered = (
        lax.all_gather(gain_attn, "dp", axis=0, tiled=True),
        lax.all_gather(qkv_weight, "dp", axis=0, tiled=True),
        lax.all_gather(out_weight, "dp", axis=0, tiled=True),
        lax.all_gather(gain_moe, "dp", axis=0, tiled=True),
        lax.all_gather(router, "dp", axis=0, tiled=True),
        lax.all_gather(const_w, "dp", axis=0, tiled=True),
        lax.all_gather(const_v, "dp", axis=1, tiled=True),
        lax.all_gather(exp_gate, "dp", axis=0, tiled=True),
        lax.all_gather(exp_up, "dp", axis=0, tiled=True),
        lax.all_gather(exp_down, "dp", axis=1, tiled=True),
    )
    gain_one = gathered[0].astype(jnp.float32)
    qkv_full = gathered[1]
    out_full = gathered[2]
    gain_two = gathered[3].astype(jnp.float32)
    router_full = gathered[4].astype(jnp.float32)
    const_full = gathered[5].astype(jnp.float32)
    vectors_full = gathered[6].astype(jnp.float32)
    gate_full = gathered[7]
    up_full = gathered[8]
    down_full = gathered[9]
    tokens = layer_input.shape[0]
    features = layer_input.shape[1]
    head_dim = features // HEADS
    score_scale = head_dim ** (-0.5)
    windows = lax.axis_size("expert") // EXPERTS
    segment_ids = segments.reshape(tokens)
    inputs = layer_input.astype(jnp.float32)
    normed_one, inverse_one = norm_forward(inputs, gain_one)
    normed_low = normed_one.astype(jnp.bfloat16)
    projected = jnp.dot(normed_low, qkv_full, preferred_element_type=jnp.float32)
    cosine, sine_table = rope_tables(tokens, head_dim)
    queries = rotate(
        projected[:, :features].reshape(tokens, HEADS, head_dim), cosine, sine_table
    ).astype(jnp.bfloat16)
    key_rows = rotate(
        projected[:, features : 2 * features].reshape(tokens, HEADS, head_dim), cosine, sine_table
    ).astype(jnp.bfloat16)
    values = projected[:, 2 * features :].reshape(tokens, HEADS, head_dim).astype(jnp.bfloat16)
    head_queries = jnp.swapaxes(queries, 0, 1)
    head_keys = jnp.swapaxes(key_rows, 0, 1)
    head_values = jnp.swapaxes(values, 0, 1)

    def forward_head(head_items):
        return head_forward(head_items[0], head_items[1], head_items[2], segment_ids, score_scale)

    head_outputs, log_sums = lax.map(forward_head, (head_queries, head_keys, head_values))
    attended = jnp.swapaxes(head_outputs, 0, 1).reshape(tokens, features).astype(jnp.bfloat16)
    hidden = inputs + jnp.dot(attended, out_full, preferred_element_type=jnp.float32)
    normed_two, inverse_two = norm_forward(hidden, gain_two)
    moe_low = normed_two.astype(jnp.bfloat16)
    moe_in = moe_low.astype(jnp.float32)
    logits = jnp.dot(moe_in, router_full, precision=FULL_PRECISION) + prev_logits
    route_probs = jax.nn.softmax(logits, axis=-1)
    route_hot = (routes[:, :, None] == jnp.arange(NR, dtype=jnp.int32)[None, None, :]).astype(
        jnp.float32
    )
    chosen = jnp.sum(route_probs[:, None, :] * route_hot, axis=-1)
    const_mix = jax.nn.softmax(
        jnp.dot(moe_in, const_full, precision=FULL_PRECISION).reshape(tokens, NC, 2), axis=-1
    )
    is_copy = (routes == EXPERTS + 1).astype(jnp.float32)
    const_hot = (
        routes[:, :, None] == (EXPERTS + 2 + jnp.arange(NC, dtype=jnp.int32))[None, None, :]
    ).astype(jnp.float32)
    const_gate = jnp.sum(chosen[:, :, None] * const_hot, axis=1)
    copy_gate = jnp.sum(chosen * is_copy, axis=1) + jnp.sum(const_gate * const_mix[:, :, 0], axis=1)
    vector_gate = const_gate * const_mix[:, :, 1]
    target, slot_table = route_slots(routes)
    slot_tokens = slot_table // 2
    moe_padded = jnp.concatenate([moe_low, jnp.zeros((1, features), jnp.bfloat16)], axis=0)
    slot_rows = jnp.take(moe_padded, slot_tokens, axis=0)
    gate_use, up_use, down_use = (gate_full, up_full, down_full)
    local_windows = 1
    outgoing = jnp.broadcast_to(
        slot_rows.reshape(EXPERTS, 1, CAP, features), (EXPERTS, windows, CAP, features)
    ).reshape(EXPERTS * windows, CAP, features)
    received = lax.all_to_all(outgoing, "expert", split_axis=0, concat_axis=0, tiled=True)
    window_out = expert_forward(received, gate_use, up_use, down_use, local_windows)
    returned = lax.all_to_all(
        window_out.astype(jnp.bfloat16), "expert", split_axis=0, concat_axis=0, tiled=True
    )
    expert_out = jnp.sum(
        returned.astype(jnp.float32).reshape(EXPERTS, windows, CAP, features), axis=1
    ).reshape(EXPERTS * CAP, features)
    expert_padded = jnp.concatenate([expert_out, jnp.zeros((1, features), jnp.float32)], axis=0)
    assigned = jnp.take(expert_padded, target, axis=0).reshape(tokens, 2, features)
    moe_out = (
        jnp.sum(chosen[:, :, None] * assigned, axis=1)
        + copy_gate[:, None] * moe_in
        + jnp.dot(vector_gate, vectors_full, precision=FULL_PRECISION)
    )
    result = (hidden + moe_out).astype(jnp.bfloat16)
    grad_out = cotangent.astype(jnp.float32)
    grad_norm_dot = jnp.sum(grad_out * moe_in, axis=1)
    grad_vector_dot = jnp.dot(grad_out, vectors_full.T, precision=FULL_PRECISION)
    grad_chosen = (
        jnp.sum(grad_out[:, None, :] * assigned, axis=-1)
        + is_copy * grad_norm_dot[:, None]
        + jnp.sum(
            const_hot
            * (
                const_mix[:, None, :, 0] * grad_norm_dot[:, None, None]
                + const_mix[:, None, :, 1] * grad_vector_dot[:, None, :]
            ),
            axis=-1,
        )
    )
    grad_mix = jnp.stack(
        [const_gate * grad_norm_dot[:, None], const_gate * grad_vector_dot], axis=-1
    )
    grad_const_logits = (
        const_mix * (grad_mix - jnp.sum(const_mix * grad_mix, axis=-1, keepdims=True))
    ).reshape(tokens, 2 * NC)
    grad_vectors = jnp.dot(vector_gate.T, grad_out, precision=FULL_PRECISION)
    grad_probs = jnp.sum(grad_chosen[:, :, None] * route_hot, axis=1)
    grad_logits = route_probs * (
        grad_probs - jnp.sum(route_probs * grad_probs, axis=-1, keepdims=True)
    )
    grad_router = jnp.dot(moe_in.T, grad_logits, precision=FULL_PRECISION)
    grad_const = jnp.dot(moe_in.T, grad_const_logits, precision=FULL_PRECISION)
    grad_moe = (
        copy_gate[:, None] * grad_out
        + jnp.dot(grad_logits, router_full.T, precision=FULL_PRECISION)
        + jnp.dot(grad_const_logits, const_full.T, precision=FULL_PRECISION)
    )
    gate_padded = jnp.concatenate([chosen.reshape(2 * tokens), jnp.zeros((1,), jnp.float32)])
    grad_padded = jnp.concatenate([grad_out, jnp.zeros((1, features), jnp.float32)], axis=0)
    grad_slots = (
        jnp.take(gate_padded, slot_table)[:, None] * jnp.take(grad_padded, slot_tokens, axis=0)
    ).astype(jnp.bfloat16)
    grad_outgoing = jnp.broadcast_to(
        grad_slots.reshape(EXPERTS, 1, CAP, features), (EXPERTS, windows, CAP, features)
    ).reshape(EXPERTS * windows, CAP, features)
    rows_again, grad_received = (
        lax.all_to_all(outgoing, "expert", split_axis=0, concat_axis=0, tiled=True),
        lax.all_to_all(grad_outgoing, "expert", split_axis=0, concat_axis=0, tiled=True),
    )
    grad_rows, grad_gate, grad_up, grad_down = expert_backward(
        rows_again, grad_received, gate_use, up_use, down_use, local_windows
    )
    grad_returned = lax.all_to_all(
        grad_rows.astype(jnp.bfloat16), "expert", split_axis=0, concat_axis=0, tiled=True
    )
    grad_expert_rows = jnp.sum(
        grad_returned.astype(jnp.float32).reshape(EXPERTS, windows, CAP, features), axis=1
    ).reshape(EXPERTS * CAP, features)
    grad_moe = (
        grad_moe
        + jnp.zeros((tokens + 1, features), jnp.float32)
        .at[slot_tokens]
        .add(grad_expert_rows)[:tokens]
    )
    grad_norm_two, grad_gain_two = norm_back(hidden, inverse_two, gain_two, grad_moe)
    grad_hidden = grad_out + grad_norm_two
    grad_branch = grad_hidden.astype(jnp.bfloat16)
    grad_out_matrix = jnp.dot(attended.T, grad_branch, preferred_element_type=jnp.float32)
    grad_attended = (
        jnp.dot(grad_branch, out_full.T, preferred_element_type=jnp.float32)
        .astype(jnp.bfloat16)
        .reshape(tokens, HEADS, head_dim)
    )

    def backward_head(head_items):
        return head_backward(
            head_items[0],
            head_items[1],
            head_items[2],
            head_items[3],
            head_items[4],
            segment_ids,
            score_scale,
        )

    grad_head_q, grad_head_k, grad_head_v = lax.map(
        backward_head,
        (head_queries, head_keys, head_values, log_sums, jnp.swapaxes(grad_attended, 0, 1)),
    )
    grad_q_rows = unrotate(jnp.swapaxes(grad_head_q, 0, 1), cosine, sine_table).reshape(
        tokens, features
    )
    grad_k_rows = unrotate(jnp.swapaxes(grad_head_k, 0, 1), cosine, sine_table).reshape(
        tokens, features
    )
    grad_v_rows = jnp.swapaxes(grad_head_v, 0, 1).reshape(tokens, features)
    grad_projected = jnp.concatenate([grad_q_rows, grad_k_rows, grad_v_rows], axis=1).astype(
        jnp.bfloat16
    )
    grad_qkv_matrix = jnp.dot(normed_low.T, grad_projected, preferred_element_type=jnp.float32)
    grad_normed_one = jnp.dot(grad_projected, qkv_full.T, preferred_element_type=jnp.float32)
    grad_norm_one, grad_gain_one = norm_back(inputs, inverse_one, gain_one, grad_normed_one)
    grad_inputs = grad_hidden + grad_norm_one
    shared = (
        grad_gain_one,
        grad_qkv_matrix,
        grad_out_matrix,
        grad_gain_two,
        grad_router,
        grad_const,
        grad_vectors,
    )
    owned = (grad_gate, grad_up, grad_down)
    summed = tuple(sum_replicas(shared))
    reduced = tuple(reduce_owners(summed + owned))
    return (
        result,
        grad_inputs,
        grad_logits,
        reduced[0],
        reduced[1],
        reduced[2],
        reduced[3],
        reduced[4],
        reduced[5],
        reduced[6],
        reduced[7],
        reduced[8],
        reduced[9],
    )


def solution(mesh):
    placed = (
        P(("dp", "expert"), None),
        P(("dp", "expert"), None),
        P(("dp", "expert"), None),
        P(("dp", "expert"), None),
        P(("dp", "expert"), None),
        P("dp"),
        P("dp", None),
        P("dp", None),
        P("dp"),
        P("dp", None),
        P("dp", None),
        P(None, "dp"),
        P("dp", "expert"),
        P("dp", "expert"),
        P("expert", "dp"),
    )
    return jax.shard_map(
        local,
        mesh=mesh,
        in_specs=placed,
        out_specs=(
            P(("dp", "expert"), None),
            P(("dp", "expert"), None),
            P(("dp", "expert"), None),
            P("dp"),
            P("dp", None),
            P("dp", None),
            P("dp"),
            P("dp", None),
            P("dp", None),
            P(None, "dp"),
            P("dp", "expert"),
            P("dp", "expert"),
            P("expert", "dp"),
        ),
        check_vma=False,
    )
```

profile of v0, /device:TPU:9, one launch (start us, length us, event | category | flops | bytes accessed | tf_op | source)
XLA Modules:
  0.0 791.0 jit_solution(5274287071500031300)
XLA Ops:
  13.5 7.2 all-reduce.10
  21.4 10.7 %all-gather = bf16[4,192,12]{1,2,0:T(8,128)(2,1)S(1)} all-gather(bf16[1,192,12]{1,2,0:T(8,128)(2,1)S(1)} %bitcast.282), channel_id=1, replica_groups=mesh['dp'=4,'expert'=8] {'dp'}, dimensions={0}, use_global_device_ids=true | all-gather | bytes 23040 | tf_op jit(solution)/shard_map/all_gather | solution.py:307
  38.7 11.0 %all-gather.1 = bf16[4,192,4]{1,2,0:T(4,128)(2,1)S(1)} all-gather(bf16[1,192,4]{1,2,0:T(4,128)(2,1)S(1)} %bitcast.285), channel_id=1, replica_groups=mesh['dp'=4,'expert'=8] {'dp'}, dimensions={0}, use_global_device_ids=true | all-gather | bytes 7680 | tf_op jit(solution)/shard_map/all_gather | solution.py:308
  49.8 9.9 %all-gather.2 = bf16[4,192,2]{1,2,0:T(2,128)(2,1)S(1)} all-gather(bf16[1,192,2]{1,2,0:T(2,128)(2,1)S(1)} %bitcast.286), channel_id=1, replica_groups=mesh['dp'=4,'expert'=8] {'dp'}, dimensions={0}, use_global_device_ids=true | all-gather | bytes 3840 | tf_op jit(solution)/shard_map/all_gather | solution.py:309
  69.0 9.9 %all-gather.9.cloned.1.call-done = bf16[768,2304]{1,0:T(8,128)(2,1)} async-done(((bf16[192,2304]{1,0:T(8,128)(2,1)}), bf16[768,2304]{1,0:T(8,128)(2,1)}) %all-gather.9.cloned.1.call-update) | async-done | bytes 3538960 | tf_op jit(solution)/shard_map/all_gather | solution.py:304
  86.1 41.1 %while.26 = (s32[]{:T(128)}, bf16[12,256,64]{1,2,0:T(8,128)(2,1)S(1)}, f32[12,256]{1,0:T(8,128)}, s32[1,256]{1,0:T(1,128)}, bf16[12,256,64]{2,1,0:T(8,128)(2,1)S...) while((s32[]{:T(128)}, bf16[12,256,64]{1,2,0:T(8,128)(2,1)S(1)}, ...), condition=%wide.region_4.5_spmd.clone, body=%wide.region_1.4_spmd.sunk.clone | while | flops 17497856 | bytes 1062993 | solution.py:349
  148.0 7.1 all-to-all-start.2
  155.1 18.5 %all-gather.13.cloned.1.call-done = bf16[768,2048]{1,0:T(8,128)(2,1)} async-done(((bf16[192,2048]{1,0:T(8,128)(2,1)}), bf16[768,2048]{1,0:T(8,128)(2,1)}) %all-gather.13.cloned.1.call-update) | async-done | bytes 3145744 | tf_op jit(solution)/shard_map/all_gather | solution.py:310
  173.6 5.9 fusion.96
  179.5 57.6 %all-gather.15.cloned.1.call-done = bf16[768,2048]{1,0:T(8,128)(2,1)} async-done(((bf16[192,2048]{1,0:T(8,128)(2,1)}), bf16[768,2048]{1,0:T(8,128)(2,1)}) %all-gather.15.cloned.1.call-update) | async-done | bytes 3145744 | tf_op jit(solution)/shard_map/all_gather | solution.py:311
  237.1 6.0 fusion.97
  243.1 57.6 %all-gather.17.cloned.1.call-done = bf16[2048,768]{0,1:T(8,128)(2,1)} async-done(((bf16[2048,192]{0,1:T(8,128)(2,1)}), bf16[2048,768]{0,1:T(8,128)(2,1)}) %all-gather.17.cloned.1.call-update) | async-done | bytes 3145744 | tf_op jit(solution)/shard_map/all_gather | solution.py:312
  300.7 8.1 %multiply_convert_fusion.1 = (bf16[512,2048]{1,0:T(8,128)(2,1)}, bf16[512,2048]{1,0:T(8,128)(2,1)}, bf16[512,2048]{1,0:T(8,128)(2,1)S(1)}) fusion(f32[512,2048]{1,0:T(8,128)} %fusion.96, f32[512,2048]{1,0:T(8,128)} %fusion.97, bf16[512,768]{1,0:T(8,128)(2,1)S(1)} %bitcast.267, bf16[2048,768]{0,1:T(8,128)(2,1)} %all-gather.17.cloned.1.call-done), kind=kOutput, calls=%fused_computation.65 | convolution fusion | flops 1626341376 | bytes 18612224 | tf_op jit(solution)/shard_map/while/body/eval_jaxpr/rd,fd->rf/dot_general | solution.py:205
  325.4 7.5 all-to-all-start.3
  351.9 86.5 %while.27 = (s32[]{:T(128)}, f32[12,256,64]{1,2,0:T(8,128)}, f32[12,256,64]{1,2,0:T(8,128)}, bf16[12,256,64]{1,2,0:T(8,128)(2,1)}, s32[1,256]{1,0:T(1,128)}, /*i...) while((s32[]{:T(128)}, f32[12,256,64]{1,2,0:T(8,128)}, ...), condition=%wide.region_29.30_spmd.clone, body=%wide.region_27.29_spmd.sunk.clone | while | flops 42761984 | bytes 5714081 | solution.py:477
  450.8 5.3 convolution_convert_fusion.3
  476.4 35.9 %reduce-scatter.21.cloned.1.call-done = bf16[192,2304]{1,0:T(8,128)(2,1)} async-done(((bf16[768,2304]{1,0:T(8,128)(2,1)}), bf16[192,2304]{1,0:T(8,128)(2,1)}) %reduce-scatter.21.cloned.1.call-update) | async-done | bytes 884752 | tf_op jit(solution)/shard_map/reduce_scatter | solution.py:243
  513.0 7.5 all-reduce.9
  523.9 6.6 reduce-scatter.25.cloned.1.call-done
  531.4 21.5 %all-reduce.7 = (bf16[192]{0:T(256)(128)(2,1)S(1)}, bf16[192]{0:T(256)(128)(2,1)S(1)}, bf16[192,12]{0,1:T(8,128)(2,1)S(1)}, bf16[192,4]{0,1:T(4,128)(2,1)S(1)}, bf16[2,192]{1,0:T(2,128)(2,1)S(1)}) all-reduce(bf16[192]{0:T(256)(128)(2,1)S(1)} %dynamic-slice.3, ...), channel_id=1, replica_groups=mesh['dp'=4,'expert'=8] {'expert'}, use_global_device_ids=true, to_apply=%region_32.33 | all-reduce | flops 3840 | bytes 15360 | tf_op jit(solution)/shard_map/psum | solution.py:275
  555.9 39.5 %reduce-scatter.19.cloned.1.call-done = bf16[2048,192]{0,1:T(8,128)(2,1)} async-done(((bf16[2048,768]{0,1:T(8,128)(2,1)}), bf16[2048,192]{0,1:T(8,128)(2,1)}) %reduce-scatter.19.cloned.1.call-update) | async-done | bytes 786448 | tf_op jit(solution)/shard_map/reduce_scatter | solution.py:267
  597.9 60.0 %reduce-scatter.15.cloned.1.call-done = bf16[192,2048]{1,0:T(8,128)(2,1)} async-done(((bf16[768,2048]{1,0:T(8,128)(2,1)}), bf16[192,2048]{1,0:T(8,128)(2,1)}) %reduce-scatter.15.cloned.1.call-update) | async-done | bytes 786448 | tf_op jit(solution)/shard_map/reduce_scatter | solution.py:261
  660.4 60.2 %reduce-scatter.17.cloned.1.call-done = bf16[192,2048]{1,0:T(8,128)(2,1)} async-done(((bf16[768,2048]{1,0:T(8,128)(2,1)}), bf16[192,2048]{1,0:T(8,128)(2,1)}) %reduce-scatter.17.cloned.1.call-update) | async-done | bytes 786448 | tf_op jit(solution)/shard_map/reduce_scatter | solution.py:264
  723.0 57.6 %all-reduce.13.cloned.1.call-done = (bf16[192,2304]{1,0:T(8,128)(2,1)}, bf16[192,768]{1,0:T(8,128)(2,1)}) async-done(((bf16[192,2304]{1,0:T(8,128)(2,1)}, bf16[192,768]{1,0:T(8,128)(2,1)}), (bf16[192,2304]{1,0:T(8,128)(2,1)}, bf16[192,768]{1,0:T(8,128)(2,1)})) %all-reduce.13.cloned.1.call-update) | async-done | bytes 1179664 | tf_op jit(solution)/shard_map/psum | solution.py:276
  (547 shorter events, 262.2 us)
Async XLA Ops:
  7.2 71.8 %all-gather.9.cloned.1.call-start = ((), (), s32[]{:S(2)}) async-start(), calls=%async_computation.12 | async-start | bytes 4423680 | tf_op jit(solution)/shard_map/all_gather | solution.py:304
  8.0 119.3 %all-gather.11.cloned.1.call-start = ((), (), s32[]{:S(2)}) async-start(), calls=%async_computation.13 | async-start | bytes 1474560 | tf_op jit(solution)/shard_map/all_gather | solution.py:305
  8.7 164.9 %all-gather.13.cloned.1.call-start = ((), (), s32[]{:S(2)}) async-start(), calls=%async_computation.14 | async-start | bytes 3932160 | tf_op jit(solution)/shard_map/all_gather | solution.py:310
  9.5 227.7 %all-gather.15.cloned.1.call-start = ((), (), s32[]{:S(2)}) async-start(), calls=%async_computation.15 | async-start | bytes 3932160 | tf_op jit(solution)/shard_map/all_gather | solution.py:311
  10.1 290.6 %all-gather.17.cloned.1.call-start = ((), (), s32[]{:S(2)}) async-start(), calls=%async_computation.16 | async-start | bytes 3932160 | tf_op jit(solution)/shard_map/all_gather | solution.py:312
  21.1 62.5 %copy-start.27 = (f32[256,32]{0,1:T(8,128)}, f32[256,32]{0,1:T(8,128)S(1)}, u32[]{:S(2)}) copy-start(f32[256,32]{0,1:T(8,128)S(1)} %get-tuple-element.495) | copy-start | bytes 98308
  21.4 108.5 %copy-start.35 = (f32[768]{0:T(1024)}, f32[768]{0:T(1024)S(1)}, u32[]{:S(2)}) copy-start(f32[768]{0:T(1024)S(1)} %convert_element_type.219) | copy-start | bytes 9220
  49.8 89.4 %copy-start.38 = (bf16[768,4]{0,1:T(4,128)(2,1)}, bf16[768,4]{0,1:T(4,128)(2,1)S(1)}, u32[]{:S(2)}) copy-start(bf16[768,4]{0,1:T(4,128)(2,1)S(1)} %reshape.489) | copy-start | bytes 18436
  134.1 13.9 %all-to-all-start = ((bf16[8,64,768]{2,1,0:T(8,128)(2,1)}), bf16[8,64,768]{2,1,0:T(8,128)(2,1)}, u32[]{:S(2)}, u32[]{:S(2)}) async-start(bf16[8,64,768]{2,1,0:T(8,128)(2,1)} %broadcast_select_fusion), calls=%async_computation | async-start | bytes 1572864 | tf_op jit(solution)/shard_map/all_to_all | solution.py:380
  138.9 323.4 %reduce-scatter.29.cloned.1.call-start = ((), (), s32[]{:S(2)}) async-start(), calls=%async_computation.24 | async-start | bytes 245760
  142.2 321.5 %reduce-scatter.27.cloned.1.call-start = ((), (), s32[]{:S(2)}) async-start(), calls=%async_computation.23 | async-start | bytes 245760
  148.0 152.7 %all-to-all-start.2 = ((bf16[8,64,768]{2,1,0:T(8,128)(2,1)}), bf16[8,64,768]{2,1,0:T(8,128)(2,1)S(1)}, u32[]{:S(2)}, u32[]{:S(2)}) async-start(bf16[8,64,768]{2,1,0:T(8,128)(2,1)} %multiply_convert_fusion.4), calls=%async_computation.2 | async-start | bytes 1572864 | tf_op jit(solution)/shard_map/all_to_all | solution.py:439
  311.6 13.8 %all-to-all-start.1 = ((bf16[8,64,768]{2,1,0:T(8,128)(2,1)}), bf16[8,64,768]{2,1,0:T(8,128)(2,1)S(1)}, u32[]{:S(2)}, u32[]{:S(2)}) async-start(bf16[8,64,768]{2,1,0:T(8,128)(2,1)} %bitcast.33), calls=%async_computation.1 | async-start | bytes 1572864 | tf_op jit(solution)/shard_map/all_to_all | solution.py:382
  325.4 16.6 %all-to-all-start.3 = ((bf16[8,64,768]{2,1,0:T(8,128)(2,1)}), bf16[8,64,768]{2,1,0:T(8,128)(2,1)}, u32[]{:S(2)}, u32[]{:S(2)}) async-start(bf16[8,64,768]{2,1,0:T(8,128)(2,1)} %bitcast.47), calls=%async_computation.3 | async-start | bytes 1572864 | tf_op jit(solution)/shard_map/all_to_all | solution.py:444
  332.9 143.5 %reduce-scatter.23.cloned.1.call-start = ((), (), s32[]{:S(2)}) async-start(), calls=%async_computation.21 | async-start | bytes 1474560 | tf_op jit(solution)/shard_map/reduce_scatter | solution.py:246
  339.6 104.6 %copy-start.34 = (f32[256,12]{0,1:T(8,128)}, f32[256,12]{0,1:T(8,128)S(1)}, u32[]{:S(2)}) copy-start(f32[256,12]{0,1:T(8,128)S(1)} %subtract_multiply_fusion) | copy-start | bytes 36868
  351.8 160.5 %reduce-scatter.21.cloned.1.call-start = ((), (), s32[]{:S(2)}) async-start(), calls=%async_computation.20 | async-start | bytes 4423680 | tf_op jit(solution)/shard_map/reduce_scatter | solution.py:243
  351.9 86.6 %copy-start.28 = (f32[256,32]{0,1:T(8,128)S(1)}, f32[256,32]{0,1:T(8,128)}, u32[]{:S(2)}) copy-start(f32[256,32]{0,1:T(8,128)} %copy-done.27) | copy-start | bytes 98308
  351.9 86.6 %copy-start.30 = (f32[256,32]{0,1:T(8,128)S(1)}, f32[256,32]{0,1:T(8,128)}, u32[]{:S(2)}) copy-start(f32[256,32]{0,1:T(8,128)} %copy-done.29) | copy-start | bytes 98308
  444.1 86.5 %reduce-scatter.25.cloned.1.call-start = ((), (), s32[]{:S(2)}) async-start(), calls=%async_computation.22 | async-start | bytes 245760
  445.3 150.1 %reduce-scatter.19.cloned.1.call-start = ((), (), s32[]{:S(2)}) async-start(), calls=%async_computation.19 | async-start | bytes 3932160 | tf_op jit(solution)/shard_map/reduce_scatter | solution.py:267
  450.5 207.4 %reduce-scatter.15.cloned.1.call-start = ((), (), s32[]{:S(2)}) async-start(), calls=%async_computation.17 | async-start | bytes 3932160 | tf_op jit(solution)/shard_map/reduce_scatter | solution.py:261
  456.1 264.4 %reduce-scatter.17.cloned.1.call-start = ((), (), s32[]{:S(2)}) async-start(), calls=%async_computation.18 | async-start | bytes 3932160 | tf_op jit(solution)/shard_map/reduce_scatter | solution.py:264
  461.5 319.1 %all-reduce.13.cloned.1.call-start = ((), (), s32[]{:S(2)}) async-start(), calls=%async_computation.25 | async-start | bytes 2359296 | tf_op jit(solution)/shard_map/psum | solution.py:276
  (100 other events, 1029.6 us)
Sparse Core Ops, SparseCore 0:
  9.6 69.3 all-gather.8
  80.5 30.3 all-gather.10
  112.5 61.0 all-gather.12
  175.0 62.0 all-gather.14
  238.6 62.0 all-gather.16
  302.8 16.1 reduce-scatter.28
  321.2 17.8 reduce-scatter.26
  351.9 29.0 reduce-scatter.22
  444.2 68.0 reduce-scatter.20
  515.0 15.5 reduce-scatter.24
  532.9 62.5 reduce-scatter.18
  597.6 60.3 reduce-scatter.14
  660.2 60.2 reduce-scatter.16
  723.6 56.9 all-reduce.12
where the time goes:
time: 806 us; the launch traced here: 791 us
  waiting for transfers between devices  412 us (51%)
  matrix products  158 us (20%)
  local copies, waits for them, and re-layouts  70.3 us (9%)
  blocking collectives  67.9 us (8%)
  other arithmetic  39.2 us (5%)
  starting transfers between devices  25.2 us (3%)
  between operations  17 us (2%)
    reduce_scatter x1, waiting for transfers between devices, reduce_owners(): lax.psum_scatter(pieces[8].astype(jnp.bfloat16), 'dp', scatter_dimension=...  60.2 us
    reduce_scatter x1, waiting for transfers between devices, reduce_owners(): lax.psum_scatter(pieces[7].astype(jnp.bfloat16), 'dp', scatter_dimension=...  60 us
    all_gather x1, waiting for transfers between devices, local(): lax.all_gather(exp_up, 'dp', axis=0, tiled=True)  57.6 us
    psum x1, waiting for transfers between devices, sum_replicas(): lax.psum(pieces[1].astype(jnp.bfloat16), 'expert').astype(jnp.float32)  57.6 us
    all_gather x1, waiting for transfers between devices, local(): lax.all_gather(exp_down, 'dp', axis=1, tiled=True)  57.6 us
    reduce_scatter x1, waiting for transfers between devices, reduce_owners(): lax.psum_scatter(pieces[9].astype(jnp.bfloat16), 'dp', scatter_dimension=...  39.5 us
    reduce_scatter x1, waiting for transfers between devices, reduce_owners(): lax.psum_scatter(pieces[1].astype(jnp.bfloat16), 'dp', scatter_dimension=...  35.9 us
    dot_general x24, matrix products, block_scores(): jnp.einsum('qd,kd->qk', query_rows, key_rows, preferred_element_type=jnp....  25.1 us
  transfers between devices with their start and end apart: 18, of which 13 were waited for; matrix products, arithmetic and copies ran while one was open for 32% of the time, Pallas kernels for 0%

commit v1 on v0

--- a/solution.py
+++ b/solution.py
@@ -3,6 +3,8 @@
 import jax
 import jax.numpy as jnp
 from jax import lax
+from jax.experimental import pallas as pl
+from jax.experimental.pallas import tpu as pltpu
 from jax.sharding import PartitionSpec as P
 
 HEADS = 12
@@ -282,7 +284,7 @@
     )
 
 
-def local(
+def local_general(
     layer_input,
     prev_logits,
     segments,
@@ -521,6 +523,552 @@
     )
 
 
+ROW_ROUTER = 0
+ROW_EVEN = 16
+ROW_ODD = 32
+ROW_GAIN_ONE = 48
+ROW_GAIN_TWO = 64
+ROW_VECTORS = 80
+SMALL_ROWS = 96
+LANES = 128
+VMEM_BYTES = 60 * 1024 * 1024
+
+
+def dot_nn(left, right):
+    return jnp.dot(left, right, preferred_element_type=jnp.float32)
+
+
+def dot_nt(left, right):
+    return lax.dot_general(
+        left, right, (((1,), (1,)), ((), ())), preferred_element_type=jnp.float32
+    )
+
+
+def dot_tn(left, right):
+    return lax.dot_general(
+        left, right, (((0,), (0,)), ((), ())), preferred_element_type=jnp.float32
+    )
+
+
+def pack_small(router, const_w, gain_attn, gain_moe, const_v):
+    width = router.shape[0]
+
+    def group(rows):
+        return jnp.concatenate([rows, jnp.zeros((16 - rows.shape[0], width), rows.dtype)], axis=0)
+
+    return jnp.concatenate(
+        [
+            group(router.T),
+            group(const_w[:, 0::2].T),
+            group(const_w[:, 1::2].T),
+            group(gain_attn[None, :]),
+            group(gain_moe[None, :]),
+            group(const_v),
+        ],
+        axis=0,
+    )
+
+
+def rotary_tables(length, head_dim):
+    cosine, sine = rope_tables(length, head_dim)
+    pairs = LANES // head_dim
+    cos_wide = jnp.tile(jnp.concatenate([cosine, cosine], axis=1), (1, pairs))
+    sin_wide = jnp.tile(jnp.concatenate([-sine, sine], axis=1), (1, pairs))
+    return cos_wide, sin_wide
+
+
+def swap_halves(values, head_dim):
+    half_dim = head_dim // 2
+    lane = lax.broadcasted_iota(jnp.int32, values.shape, 1)
+    after = pltpu.roll(values, LANES - half_dim, 1)
+    before = pltpu.roll(values, half_dim, 1)
+    return jnp.where(lane % head_dim < half_dim, after, before)
+
+
+def routing_terms(moe_low, small_ref, prev, routes):
+    logits = dot_nt(moe_low, small_ref[ROW_ROUTER : ROW_ROUTER + 16, :])[:, :NR] + prev
+    spread = jnp.exp(logits - jnp.max(logits, axis=1, keepdims=True))
+    probs = spread / jnp.sum(spread, axis=1, keepdims=True)
+    even = dot_nt(moe_low, small_ref[ROW_EVEN : ROW_EVEN + 16, :])
+    odd = dot_nt(moe_low, small_ref[ROW_ODD : ROW_ODD + 16, :])
+    gap = (even - odd)[:, :NC]
+    mix_first = 1.0 / (1.0 + jnp.exp(-gap))
+    mix_second = 1.0 / (1.0 + jnp.exp(gap))
+    ids = lax.broadcasted_iota(jnp.int32, probs.shape, 1)
+    hots = [(ids == routes[:, k : k + 1]).astype(jnp.float32) for k in range(2)]
+    chosen = [jnp.sum(probs * hot, axis=1, keepdims=True) for hot in hots]
+    return probs, mix_first, mix_second, hots, chosen
+
+
+def slot_hots(hots, routes):
+    tokens = routes.shape[0]
+    rows = lax.broadcasted_iota(jnp.int32, (tokens, tokens), 0)
+    columns = lax.broadcasted_iota(jnp.int32, (tokens, tokens), 1)
+    earlier = jnp.where(columns < rows, 1.0, 0.0).astype(jnp.bfloat16)
+    before = dot_nn(earlier, (hots[0] + hots[1]).astype(jnp.bfloat16))
+    places = lax.broadcasted_iota(jnp.int32, (tokens, EXPERTS * CAP), 1)
+    picks = []
+    for k in range(2):
+        slot = jnp.sum(before * hots[k], axis=1, keepdims=True).astype(jnp.int32)
+        route = routes[:, k : k + 1]
+        target = jnp.where(route < EXPERTS, route * CAP + slot, -1)
+        picks.append(jnp.where(places == target, 1.0, 0.0).astype(jnp.bfloat16))
+    return picks
+
+
+def fill_mask(mask_ref, column_segments, row_segments):
+    shape = mask_ref.shape
+    rows = lax.broadcasted_iota(jnp.int32, shape, 0)
+    columns = lax.broadcasted_iota(jnp.int32, shape, 1)
+    allowed = (column_segments == row_segments) & (rows >= columns)
+    mask_ref[...] = jnp.where(allowed, 0.0, NEGATIVE)
+
+
+def head_probs(query_pair, key_pair, keep, mask, score_scale):
+    zero = jnp.zeros_like(query_pair)
+    scores = dot_nt(jnp.where(keep, query_pair, zero), key_pair) * score_scale + mask
+    weights = jnp.exp(scores - jnp.max(scores, axis=1, keepdims=True))
+    return weights / jnp.sum(weights, axis=1, keepdims=True)
+
+
+def before_kernel(
+    input_ref,
+    prev_ref,
+    routes_ref,
+    column_ref,
+    row_ref,
+    grad_ref,
+    small_ref,
+    weight_ref,
+    cos_ref,
+    sin_ref,
+    query_ref,
+    key_ref,
+    value_ref,
+    attended_ref,
+    hidden_ref,
+    moe_ref,
+    rows_ref,
+    projected,
+    mask,
+):
+    tokens, features = input_ref.shape
+    head_dim = features // HEADS
+    score_scale = head_dim ** (-0.5)
+    part = weight_ref.shape[2]
+    inputs = input_ref[...].astype(jnp.float32)
+    inverse_one = lax.rsqrt(jnp.mean(inputs * inputs, axis=1, keepdims=True) + EPSILON)
+    gain_one = small_ref[ROW_GAIN_ONE : ROW_GAIN_ONE + 1, :].astype(jnp.float32)
+    normed = (inputs * inverse_one * gain_one).astype(jnp.bfloat16)
+    fill_mask(mask, column_ref[...], row_ref[...])
+
+    def project(step, carry):
+        at = pl.multiple_of(step * part, LANES)
+        projected[:, pl.ds(at, part)] = dot_nn(normed, weight_ref[step])
+        return carry
+
+    lax.fori_loop(0, 3 * features // part, project, 0)
+    lane = lax.broadcasted_iota(jnp.int32, (tokens, LANES), 1)
+
+    def pair_step(pair, carry):
+        at = pl.multiple_of(pair * LANES, LANES)
+        cosine, sine = cos_ref[...], sin_ref[...]
+        query = projected[:, pl.ds(at, LANES)]
+        key = projected[:, pl.ds(features + at, LANES)]
+        query = (query * cosine + swap_halves(query, head_dim) * sine).astype(jnp.bfloat16)
+        key = (key * cosine + swap_halves(key, head_dim) * sine).astype(jnp.bfloat16)
+        value = projected[:, pl.ds(2 * features + at, LANES)].astype(jnp.bfloat16)
+        query_ref[:, pl.ds(at, LANES)] = query
+        key_ref[:, pl.ds(at, LANES)] = key
+        value_ref[:, pl.ds(at, LANES)] = value
+        mixed = None
+        for head in range(LANES // head_dim):
+            keep = lane // head_dim == head
+            probs = head_probs(query, key, keep, mask[...], score_scale)
+            out = dot_nn(probs.astype(jnp.bfloat16), value)
+            mixed = out if mixed is None else jnp.where(keep, out, mixed)
+        attended_ref[:, pl.ds(at, LANES)] = mixed.astype(jnp.bfloat16)
+        return carry
+
+    lax.fori_loop(0, features // LANES, pair_step, 0)
+    attended = attended_ref[...]
+    first = 3 * features // part
+    for step in range(features // part):
+        columns = pl.ds(step * part, part)
+        hidden_ref[:, columns] = input_ref[:, columns].astype(jnp.float32) + dot_nn(
+            attended, weight_ref[first + step]
+        )
+    hidden = hidden_ref[...]
+    inverse_two = lax.rsqrt(jnp.mean(hidden * hidden, axis=1, keepdims=True) + EPSILON)
+    gain_two = small_ref[ROW_GAIN_TWO : ROW_GAIN_TWO + 1, :].astype(jnp.float32)
+    moe_low = (hidden * inverse_two * gain_two).astype(jnp.bfloat16)
+    moe_ref[...] = moe_low
+    routes = routes_ref[...]
+    _, _, _, hots, chosen = routing_terms(moe_low, small_ref, prev_ref[...], routes)
+    picks = slot_hots(hots, routes)
+    slots = EXPERTS * CAP
+    token_rows = dot_tn(picks[0] + picks[1], moe_low).astype(jnp.bfloat16)
+    grad = grad_ref[...].astype(jnp.float32)
+    grad_rows = (
+        dot_tn(picks[0], (chosen[0] * grad).astype(jnp.bfloat16))
+        + dot_tn(picks[1], (chosen[1] * grad).astype(jnp.bfloat16))
+    ).astype(jnp.bfloat16)
+    for expert in range(EXPERTS):
+        rows_ref[expert, 0] = token_rows[expert * CAP : (expert + 1) * CAP]
+        rows_ref[expert, 1] = grad_rows[expert * CAP : (expert + 1) * CAP]
+
+
+def after_kernel(
+    input_ref,
+    prev_ref,
+    routes_ref,
+    column_ref,
+    row_ref,
+    grad_ref,
+    small_ref,
+    weight_ref,
+    cos_ref,
+    sin_ref,
+    query_ref,
+    key_ref,
+    value_ref,
+    attended_ref,
+    hidden_ref,
+    moe_ref,
+    back_ref,
+    result_ref,
+    grad_input_ref,
+    grad_prev_ref,
+    grad_weight_ref,
+    grad_small_ref,
+    grad_attended,
+    grad_projected,
+    mask,
+):
+    tokens, features = input_ref.shape
+    head_dim = features // HEADS
+    score_scale = head_dim ** (-0.5)
+    part = weight_ref.shape[2]
+    slots = EXPERTS * CAP
+    routes = routes_ref[...]
+    moe_low = moe_ref[...]
+    moe_in = moe_low.astype(jnp.float32)
+    grad = grad_ref[...].astype(jnp.float32)
+    probs, mix_first, mix_second, hots, chosen = routing_terms(
+        moe_low, small_ref, prev_ref[...], routes
+    )
+    picks = slot_hots(hots, routes)
+    out_rows = back_ref[:, 0].reshape(slots, features)
+    drow_rows = back_ref[:, 1].reshape(slots, features)
+    given = [dot_nn(pick, out_rows) for pick in picks]
+    vectors = small_ref[ROW_VECTORS : ROW_VECTORS + NC, :].astype(jnp.float32)
+    is_copy = [(routes[:, k : k + 1] == EXPERTS + 1).astype(jnp.float32) for k in range(2)]
+    is_const = [
+        [(routes[:, k : k + 1] == EXPERTS + 2 + c).astype(jnp.float32) for k in range(2)]
+        for c in range(NC)
+    ]
+    const_gate = [
+        chosen[0] * is_const[c][0] + chosen[1] * is_const[c][1] for c in range(NC)
+    ]
+    firsts = [mix_first[:, c : c + 1] for c in range(NC)]
+    seconds = [mix_second[:, c : c + 1] for c in range(NC)]
+    copy_gate = chosen[0] * is_copy[0] + chosen[1] * is_copy[1]
+    for c in range(NC):
+        copy_gate = copy_gate + const_gate[c] * firsts[c]
+    moe_out = chosen[0] * given[0] + chosen[1] * given[1] + copy_gate * moe_in
+    for c in range(NC):
+        moe_out = moe_out + (const_gate[c] * seconds[c]) * vectors[c : c + 1, :]
+    hidden = hidden_ref[...]
+    result_ref[...] = (hidden + moe_out).astype(jnp.bfloat16)
+
+    norm_dot = jnp.sum(grad * moe_in, axis=1, keepdims=True)
+    vector_dot = [
+        jnp.sum(grad * vectors[c : c + 1, :], axis=1, keepdims=True) for c in range(NC)
+    ]
+    grad_probs = jnp.zeros_like(probs)
+    for k in range(2):
+        grad_chosen = jnp.sum(grad * given[k], axis=1, keepdims=True) + is_copy[k] * norm_dot
+        for c in range(NC):
+            grad_chosen = grad_chosen + is_const[c][k] * (
+                firsts[c] * norm_dot + seconds[c] * vector_dot[c]
+            )
+        grad_probs = grad_probs + grad_chosen * hots[k]
+    grad_logits = probs * (grad_probs - jnp.sum(probs * grad_probs, axis=1, keepdims=True))
+    grad_prev_ref[...] = grad_logits
+    grad_small_ref[...] = jnp.zeros_like(grad_small_ref)
+    logits_low = grad_logits.astype(jnp.bfloat16)
+    grad_small_ref[ROW_ROUTER : ROW_ROUTER + NR, :] = dot_tn(logits_low, moe_low)
+    grad_moe = (
+        copy_gate * grad
+        + dot_nn(logits_low, small_ref[ROW_ROUTER : ROW_ROUTER + NR, :])
+        + dot_nn(picks[0] + picks[1], drow_rows)
+    )
+    weight_gap = small_ref[ROW_EVEN : ROW_EVEN + NC, :].astype(jnp.float32) - small_ref[
+        ROW_ODD : ROW_ODD + NC, :
+    ].astype(jnp.float32)
+    for c in range(NC):
+        grad_gap = firsts[c] * seconds[c] * const_gate[c] * (norm_dot - vector_dot[c])
+        grad_moe = grad_moe + grad_gap * weight_gap[c : c + 1, :]
+        grad_small_ref[ROW_EVEN + c : ROW_EVEN + c + 1, :] = jnp.sum(
+            grad_gap * moe_in, axis=0, keepdims=True
+        )
+        grad_small_ref[ROW_VECTORS + c : ROW_VECTORS + c + 1, :] = jnp.sum(
+            (const_gate[c] * seconds[c]) * grad, axis=0, keepdims=True
+        )
+
+    inverse_two = lax.rsqrt(jnp.mean(hidden * hidden, axis=1, keepdims=True) + EPSILON)
+    gain_two = small_ref[ROW_GAIN_TWO : ROW_GAIN_TWO + 1, :].astype(jnp.float32)
+    scaled = grad_moe * gain_two
+    inner = jnp.mean(hidden * scaled, axis=1, keepdims=True)
+    grad_hidden = (
+        grad
+        + inverse_two * scaled
+        - hidden * (inverse_two * inverse_two * inverse_two * inner)
+    )
+    grad_small_ref[ROW_GAIN_TWO : ROW_GAIN_TWO + 1, :] = jnp.sum(
+        grad_moe * hidden * inverse_two, axis=0, keepdims=True
+    )
+    grad_input_ref[...] = grad_hidden
+    branch = grad_hidden.astype(jnp.bfloat16)
+    first = 3 * features // part
+    sums = None
+    for step in range(features // part):
+        columns = slice(step * part, (step + 1) * part)
+        grad_weight_ref[first + step] = dot_tn(attended_ref[...], branch[:, columns]).astype(
+            jnp.bfloat16
+        )
+        term = dot_nt(branch[:, columns], weight_ref[first + step])
+        sums = term if sums is None else sums + term
+    grad_attended[...] = sums.astype(jnp.bfloat16)
+    fill_mask(mask, column_ref[...], row_ref[...])
+    lane = lax.broadcasted_iota(jnp.int32, (tokens, LANES), 1)
+
+    def pair_step(pair, carry):
+        at = pl.multiple_of(pair * LANES, LANES)
+        cosine, sine = cos_ref[...], sin_ref[...]
+        query = query_ref[:, pl.ds(at, LANES)]
+        key = key_ref[:, pl.ds(at, LANES)]
+        value = value_ref[:, pl.ds(at, LANES)]
+        grad_out = grad_attended[:, pl.ds(at, LANES)]
+        sums = None
+        for head in range(LANES // head_dim):
+            keep = lane // head_dim == head
+            weights = head_probs(query, key, keep, mask[...], score_scale)
+            grad_weights = dot_nt(jnp.where(keep, grad_out, jnp.zeros_like(grad_out)), value)
+            inner_sum = jnp.sum(weights * grad_weights, axis=1, keepdims=True)
+            grad_scores = (weights * (grad_weights - inner_sum)).astype(jnp.bfloat16)
+            terms = (
+                dot_nn(grad_scores, key) * score_scale,
+                dot_tn(grad_scores, query) * score_scale,
+                dot_tn(weights.astype(jnp.bfloat16), grad_out),
+            )
+            if sums is None:
+                sums = terms
+            else:
+                sums = tuple(jnp.where(keep, new, old) for new, old in zip(terms, sums))
+        grad_query, grad_key, grad_value = sums
+        grad_query = grad_query * cosine - swap_halves(grad_query, head_dim) * sine
+        grad_key = grad_key * cosine - swap_halves(grad_key, head_dim) * sine
+        grad_projected[:, pl.ds(at, LANES)] = grad_query.astype(jnp.bfloat16)
+        grad_projected[:, pl.ds(features + at, LANES)] = grad_key.astype(jnp.bfloat16)
+        grad_projected[:, pl.ds(2 * features + at, LANES)] = grad_value.astype(jnp.bfloat16)
+        return carry
+
+    lax.fori_loop(0, features // LANES, pair_step, 0)
+    inputs = input_ref[...].astype(jnp.float32)
+    inverse_one = lax.rsqrt(jnp.mean(inputs * inputs, axis=1, keepdims=True) + EPSILON)
+    gain_one = small_ref[ROW_GAIN_ONE : ROW_GAIN_ONE + 1, :].astype(jnp.float32)
+    normed = (inputs * inverse_one * gain_one).astype(jnp.bfloat16)
+
+    def weight_step(step, total):
+        at = pl.multiple_of(step * part, LANES)
+        piece = grad_projected[:, pl.ds(at, part)]
+        grad_weight_ref[step] = dot_tn(normed, piece).astype(jnp.bfloat16)
+        return total + dot_nt(piece, weight_ref[step])
+
+    grad_normed = lax.fori_loop(
+        0, 3 * features // part, weight_step, jnp.zeros((tokens, features), jnp.float32)
+    )
+    scaled_one = grad_normed * gain_one
+    inner_one = jnp.mean(inputs * scaled_one, axis=1, keepdims=True)
+    grad_input_ref[...] = (
+        grad_input_ref[...]
+        + inverse_one * scaled_one
+        - inputs * (inverse_one * inverse_one * inverse_one * inner_one)
+    )
+    grad_small_ref[ROW_GAIN_ONE : ROW_GAIN_ONE + 1, :] = jnp.sum(
+        grad_normed * inputs * inverse_one, axis=0, keepdims=True
+    )
+
+
+def run_before(args, parts, part_width):
+    tokens, features = args[0].shape
+    low = jax.ShapeDtypeStruct((tokens, features), jnp.bfloat16)
+    return pl.pallas_call(
+        before_kernel,
+        out_shape=(
+            low,
+            low,
+            low,
+            low,
+            jax.ShapeDtypeStruct((tokens, features), jnp.float32),
+            low,
+            jax.ShapeDtypeStruct((EXPERTS, 2, CAP, features), jnp.bfloat16),
+        ),
+        scratch_shapes=[
+            pltpu.VMEM((tokens, 3 * features), jnp.float32),
+            pltpu.VMEM((tokens, tokens), jnp.float32),
+        ],
+        compiler_params=pltpu.CompilerParams(vmem_limit_bytes=VMEM_BYTES),
+        cost_estimate=pl.CostEstimate(
+            flops=2 * tokens * features * 4 * features,
+            transcendentals=HEADS * tokens * tokens,
+            bytes_accessed=20 << 20,
+        ),
+        name="before",
+    )(*args)
+
+
+def run_after(args, parts, part_width):
+    tokens, features = args[0].shape
+    return pl.pallas_call(
+        after_kernel,
+        out_shape=(
+            jax.ShapeDtypeStruct((tokens, features), jnp.bfloat16),
+            jax.ShapeDtypeStruct((tokens, features), jnp.float32),
+            jax.ShapeDtypeStruct((tokens, NR), jnp.float32),
+            jax.ShapeDtypeStruct((parts, features, part_width), jnp.bfloat16),
+            jax.ShapeDtypeStruct((SMALL_ROWS, features), jnp.float32),
+        ),
+        scratch_shapes=[
+            pltpu.VMEM((tokens, features), jnp.bfloat16),
+            pltpu.VMEM((tokens, 3 * features), jnp.bfloat16),
+            pltpu.VMEM((tokens, tokens), jnp.float32),
+        ],
+        compiler_params=pltpu.CompilerParams(vmem_limit_bytes=VMEM_BYTES),
+        cost_estimate=pl.CostEstimate(
+            flops=4 * tokens * features * 4 * features,
+            transcendentals=HEADS * tokens * tokens,
+            bytes_accessed=60 << 20,
+        ),
+        name="after",
+    )(*args)
+
+
+def expert_both(token_rows, grad_rows, gate_weight, up_weight, down_weight):
+    gate_pre = dot_nn(token_rows, gate_weight)
+    up_pre = dot_nn(token_rows, up_weight)
+    sigmoid_gate = jax.nn.sigmoid(gate_pre)
+    silu_gate = gate_pre * sigmoid_gate
+    act = (silu_gate * up_pre).astype(jnp.bfloat16)
+    grad_down = dot_tn(act, grad_rows)
+    out = dot_nn(act, down_weight).astype(jnp.bfloat16)
+    grad_act = dot_nt(grad_rows, down_weight)
+    grad_up_pre = (grad_act * silu_gate).astype(jnp.bfloat16)
+    grad_gate_pre = (
+        grad_act * up_pre * sigmoid_gate * (1.0 + gate_pre * (1.0 - sigmoid_gate))
+    ).astype(jnp.bfloat16)
+    grad_gate = dot_tn(token_rows, grad_gate_pre)
+    grad_up = dot_tn(token_rows, grad_up_pre)
+    grad_tokens = (dot_nt(grad_gate_pre, gate_weight) + dot_nt(grad_up_pre, up_weight)).astype(
+        jnp.bfloat16
+    )
+    return out, grad_tokens, grad_gate, grad_up, grad_down
+
+
+def scatter_sum(value, axis):
+    return lax.psum_scatter(
+        value.astype(jnp.bfloat16), "dp", scatter_dimension=axis, tiled=True
+    ).astype(jnp.float32)
+
+
+def local_fast(
+    layer_input,
+    prev_logits,
+    segments,
+    routes,
+    cotangent,
+    gain_attn,
+    qkv_weight,
+    out_weight,
+    gain_moe,
+    router,
+    const_w,
+    const_v,
+    exp_gate,
+    exp_up,
+    exp_down,
+):
+    tokens, features = layer_input.shape
+    parts = lax.axis_size("expert")
+    part_width = 4 * features // parts
+    mine = lax.axis_index("expert")
+    both = jnp.concatenate([qkv_weight, out_weight], axis=1)
+    small = lax.all_gather(
+        pack_small(router, const_w, gain_attn, gain_moe, const_v), "dp", axis=1, tiled=True
+    )
+    piece = lax.dynamic_slice_in_dim(both, mine * part_width, part_width, axis=1)
+    column = lax.all_gather(piece, "dp", axis=0, tiled=True)
+    weights = lax.all_gather(column, "expert", axis=0)
+    gate_full = lax.all_gather(exp_gate, "dp", axis=0, tiled=True)
+    up_full = lax.all_gather(exp_up, "dp", axis=0, tiled=True)
+    down_full = lax.all_gather(exp_down, "dp", axis=1, tiled=True)
+    cosine, sine = rotary_tables(tokens, features // HEADS)
+    common = (
+        layer_input,
+        prev_logits,
+        routes,
+        segments.reshape(tokens, 1),
+        segments.reshape(1, tokens),
+        cotangent,
+        small,
+        weights,
+        cosine,
+        sine,
+    )
+    *saved, rows = run_before(common, parts, part_width)
+    received = lax.all_to_all(rows, "expert", split_axis=0, concat_axis=0, tiled=True)
+    slots = EXPERTS * CAP
+    out, grad_tokens, grad_gate, grad_up, grad_down = expert_both(
+        received[:, 0].reshape(slots, features),
+        received[:, 1].reshape(slots, features),
+        gate_full,
+        up_full,
+        down_full,
+    )
+    back = jnp.stack(
+        [out.reshape(EXPERTS, CAP, features), grad_tokens.reshape(EXPERTS, CAP, features)], axis=1
+    )
+    returned = lax.all_to_all(back, "expert", split_axis=0, concat_axis=0, tiled=True)
+    own_down = scatter_sum(grad_down, 1)
+    own_gate = scatter_sum(grad_gate, 0)
+    own_up = scatter_sum(grad_up, 0)
+    result, grad_input, grad_prev, grad_weights, grad_small = run_after(
+        common + tuple(saved) + (returned,), parts, part_width
+    )
+    share = lax.psum_scatter(grad_weights, "expert", scatter_dimension=0, tiled=False)
+    share = lax.psum_scatter(share, "dp", scatter_dimension=0, tiled=True)
+    own_weights = lax.all_gather(share, "expert", axis=1, tiled=True).astype(jnp.float32)
+    own_small = scatter_sum(lax.psum(grad_small.astype(jnp.bfloat16), "expert"), 1)
+    grad_even = own_small[ROW_EVEN : ROW_EVEN + NC]
+    grad_const = jnp.stack([grad_even, -grad_even], axis=1).reshape(2 * NC, -1).T
+    return (
+        result,
+        grad_input,
+        grad_prev,
+        own_small[ROW_GAIN_ONE],
+        own_weights[:, : 3 * features],
+        own_weights[:, 3 * features :],
+        own_small[ROW_GAIN_TWO],
+        own_small[ROW_ROUTER : ROW_ROUTER + NR].T,
+        grad_const,
+        own_small[ROW_VECTORS : ROW_VECTORS + NC],
+        own_gate,
+        own_up,
+        own_down,
+    )
+
+
 def solution(mesh):
     placed = (
         P(("dp", "expert"), None),
@@ -539,8 +1087,9 @@
         P("dp", "expert"),
         P("expert", "dp"),
     )
+    body = local_fast if mesh.shape["expert"] == EXPERTS else local_general
     return jax.shard_map(
-        local,
+        body,
         mesh=mesh,
         in_specs=placed,
         out_specs=(

time: 806 us -> 642 us (0.80); the launches traced: 791 us -> 640 us
  matrix products: 158 us -> 35.8 us
  local copies, waits for them, and re-layouts: 70.3 us -> 20.3 us
  Pallas kernels: 0 us -> 38.2 us
  other arithmetic: 39.2 us -> 8.75 us
  blocking collectives: 67.9 us -> 96.7 us
  starting transfers between devices: 25.2 us -> 0.44 us
  waiting for transfers between devices: 412 us -> 425 us
    dot_general x108 -> x9, matrix products: 158 us -> 35.8 us  [the longest x3 14.1 us: dot_nn(): return jnp.dot(left, right, preferred_element_type=jnp.float32)]
    psum x1 -> x0, waiting for transfers between devices: 57.6 us -> none  [sum_replicas(): lax.psum(pieces[1].astype(jnp.bfloat16), 'expert').astype(jnp.float32)]
    all_to_all x0 -> x2, blocking collectives: none -> 47.8 us  [the longest x1 24.3 us: local_fast(): lax.all_to_all(back, 'expert', split_axis=0, concat_axis=0, tiled=True)]
    all_gather x5, waiting for transfers between devices: 144 us -> 188 us  [the longest x1 58 us: local_fast(): gate_full = lax.all_gather(exp_gate, 'dp', axis=0, tiled=True)]
    pallas_call x0 -> x2, Pallas kernels: none -> 38.2 us  [the longest x1 23.3 us: run_after(): pl.pallas_call(after_kernel, out_shape=(jax.ShapeDtypeStruct((tokens, fea...]
    all_to_all x4 -> x0, starting transfers between devices: 24.1 us -> none  [the longest x1 7.52 us: local(): lax.all_to_all(grad_rows.astype(jnp.bfloat16), 'expert', split_axis=0, co...]
    reduce_scatter x5, waiting for transfers between devices: 196 us -> 216 us  [the longest x3 158 us: scatter_sum(): lax.psum_scatter(value.astype(jnp.bfloat16), 'dp', scatter_dimension=axis...]
    dynamic_update_slice x12 -> x0, local copies, waits for them, and re-layouts: 15.8 us -> none  [local(): lax.map(forward_head, (head_queries, head_keys, head_values))]
  transfers between devices with their start and end apart: 18 -> 11, of which waited for: 13 -> 11; matrix products, arithmetic and copies ran while one was open for 32% -> 7% of each run, Pallas kernels for 0% -> 2%
where the time goes in v1:
time: 642 us; the launch traced here: 640 us
  waiting for transfers between devices  425 us (66%)
  blocking collectives  96.7 us (15%)
  Pallas kernels  38.2 us (6%)
  matrix products  35.8 us (6%)
  local copies, waits for them, and re-layouts  20.3 us (3%)
  between operations  14.3 us (2%)
  other arithmetic  8.75 us (1%)
    reduce_scatter x3, waiting for transfers between devices, scatter_sum(): lax.psum_scatter(value.astype(jnp.bfloat16), 'dp', scatter_dimension=axis...  158 us
    all_gather x1, waiting for transfers between devices, local_fast(): gate_full = lax.all_gather(exp_gate, 'dp', axis=0, tiled=True)  58 us
    all_gather x1, waiting for transfers between devices, local_fast(): up_full = lax.all_gather(exp_up, 'dp', axis=0, tiled=True)  57.8 us
    reduce_scatter x1, waiting for transfers between devices, local_fast(): lax.psum_scatter(grad_weights, 'expert', scatter_dimension=0, tiled=False)  53.3 us
    all_gather x1, waiting for transfers between devices, local_fast(): lax.all_gather(share, 'expert', axis=1, tiled=True).astype(jnp.float32)  24.5 us
    all_to_all x1, blocking collectives, local_fast(): lax.all_to_all(back, 'expert', split_axis=0, concat_axis=0, tiled=True)  24.3 us
    all_gather x1, waiting for transfers between devices, local_fast(): weights = lax.all_gather(column, 'expert', axis=0)  24.2 us
    all_gather x1, waiting for transfers between devices, local_fast(): down_full = lax.all_gather(exp_down, 'dp', axis=1, tiled=True)  23.6 us
  transfers between devices with their start and end apart: 11, of which 11 were waited for; matrix products, arithmetic and copies ran while one was open for 7% of the time, Pallas kernels for 2%

profile of v1, /device:TPU:9, one launch (start us, length us, event | category | flops | bytes accessed | tf_op | source)
XLA Modules:
  0.0 639.7 jit_solution(17256617353100433501)
XLA Ops:
  8.3 13.7 %all_gather.25 = bf16[768,384]{1,0:T(8,128)(2,1)} all-gather(bf16[192,384]{1,0:T(8,128)(2,1)S(1)} %fusion.1), channel_id=1, replica_groups=mesh['dp'=4,'expert'=8] {'dp'}, dimensions={0}, use_global_device_ids=true | all-gather | bytes 737280 | tf_op jit(solution)/shard_map/all_gather | solution.py:1011
  29.4 11.8 %all_gather.24 = bf16[96,768]{0,1:T(8,128)(2,1)S(1)} all-gather(bf16[96,192]{0,1:T(8,128)(2,1)S(1)} %concatenate.12), channel_id=1, replica_groups=mesh['dp'=4,'expert'=8] {'dp'}, dimensions={1}, use_global_device_ids=true | all-gather | bytes 184320 | tf_op jit(solution)/shard_map/all_gather | solution.py:1007
  42.0 24.2 %all-gather.15.cloned.1.call-done = bf16[6144,384]{1,0:T(8,128)(2,1)} async-done(((bf16[768,384]{1,0:T(8,128)(2,1)}), bf16[6144,384]{1,0:T(8,128)(2,1)}) %all-gather.15.cloned.1.call-update) | async-done | bytes 4718608 | tf_op jit(solution)/shard_map/all_gather | solution.py:1012
  66.2 14.9 %before.1 = (bf16[256,768]{1,0:T(8,128)(2,1)}, bf16[256,768]{1,0:T(8,128)(2,1)}, bf16[256,768]{1,0:T(8,128)(2,1)}, bf16[256,768]{1,0:T(8,128)(2,1)}, f32[256,768...) custom-call(bf16[256,768]{1,0:T(8,128)(2,1)} %input_ref.3, f32[256,12]{1,0:T(8,128)} %copy.75.prev_ref, ...), custom_call_target="tpu_custom_call" | custom-call | flops 1207959552 | bytes 20971520 | tf_op jit(solution)/shard_map/before/pallas_call | solution.py:907
  81.2 23.5 %all_to_all.10 = bf16[8,2,64,768]{3,2,1,0:T(8,128)(2,1)S(1)} all-to-all(bf16[8,2,64,768]{3,2,1,0:T(8,128)(2,1)} %get-tuple-element.31), channel_id=1, replica_groups=mesh['dp'=4,'expert'=8] {'expert'}, dimensions={0} | all-to-all | bytes 3145728 | tf_op jit(solution)/shard_map/all_to_all | solution.py:1030
  104.8 23.6 %all-gather.11.cloned.1.call-done = bf16[2048,768]{0,1:T(8,128)(2,1)} async-done(((bf16[2048,192]{0,1:T(8,128)(2,1)}), bf16[2048,768]{0,1:T(8,128)(2,1)}) %all-gather.11.cloned.1.call-update) | async-done | bytes 3145744 | tf_op jit(solution)/shard_map/all_gather | solution.py:1015
  128.4 5.7 fusion.8
  134.1 58.0 %all-gather.7.cloned.1.call-done = bf16[768,2048]{1,0:T(8,128)(2,1)} async-done(((bf16[192,2048]{1,0:T(8,128)(2,1)}), bf16[768,2048]{1,0:T(8,128)(2,1)}) %all-gather.7.cloned.1.call-update) | async-done | bytes 3145744 | tf_op jit(solution)/shard_map/all_gather | solution.py:1013
  192.1 5.8 fusion.7
  197.8 57.8 %all-gather.9.cloned.1.call-done = bf16[768,2048]{1,0:T(8,128)(2,1)} async-done(((bf16[192,2048]{1,0:T(8,128)(2,1)}), bf16[768,2048]{1,0:T(8,128)(2,1)}) %all-gather.9.cloned.1.call-update) | async-done | bytes 3145744 | tf_op jit(solution)/shard_map/all_gather | solution.py:1014
  255.6 6.5 %multiply_convert_fusion.2 = (bf16[512,2048]{1,0:T(8,128)(2,1)S(1)}, bf16[512,2048]{1,0:T(8,128)(2,1)S(1)}, bf16[512,2048]{1,0:T(8,128)(2,1)S(1)}) fusion(f32[512,2048]{1,0:T(8,128)} %fusion.7, f32[512,2048]{1,0:T(8,128)} %fusion.8, bf16[512,768]{1,0:T(8,128)(2,1)S(1)} %bitcast.45, bf16[768,2048]{1,0:T(8,128)(2,1)} %all-gather.9.cloned.1.call-done), kind=kOutput, calls=%fused_computation.2 | convolution fusion | flops 1626341376 | bytes 18612224 | tf_op jit(solution)/shard_map/dot_general | solution.py:538
  270.2 24.3 %all_to_all.11.back_ref = bf16[8,2,64,768]{3,2,1,0:T(8,128)(2,1)} all-to-all(bf16[8,2,64,768]{3,2,1,0:T(8,128)(2,1)S(1)} %pad_maximum_fusion), channel_id=1, replica_groups=mesh['dp'=4,'expert'=8] {'expert'}, dimensions={0} | all-to-all | bytes 3145728 | tf_op jit(solution)/shard_map/all_to_all | solution.py:1042
  294.5 23.3 %after.1 = (bf16[256,768]{1,0:T(8,128)(2,1)}, f32[256,768]{1,0:T(8,128)}, f32[256,12]{1,0:T(8,128)}, bf16[8,768,384]{2,1,0:T(8,128)(2,1)}, f32[96,768]{1,0:T(8,128)}) custom-call(bf16[256,768]{1,0:T(8,128)(2,1)} %input_ref.3, f32[256,12]{1,0:T(8,128)} %copy.75.prev_ref, s32[256,2]{1,0:T(8,128)} %copy.76.routes_ref, s32[256,1]{1,0:T(8,128)} %copy.77.column_ref, ...), custom_call_target="tpu_custom_call" | custom-call | flops 2415919104 | bytes 62914560 | tf_op jit(solution)/shard_map/after/pallas_call | solution.py:934
  317.8 53.3 %reduce-scatter.9.cloned.1.call-done = bf16[1,768,384]{2,1,0:T(8,128)(2,1)} async-done(((bf16[8,768,384]{2,1,0:T(8,128)(2,1)}), bf16[1,768,384]{2,1,0:T(8,128)(2,1)}) %reduce-scatter.9.cloned.1.call-update) | async-done | bytes 589840 | tf_op jit(solution)/shard_map/reduce_scatter | solution.py:1049
  372.1 5.1 convolution_convert_fusion
  378.8 3.5 convolution_convert_fusion.1
  384.0 3.6 convolution_convert_fusion.2
  387.6 4.3 reduce-scatter.11.cloned.1.call-done
  392.7 19.1 %reduce-scatter.19.cloned.1.call-done = bf16[192,96]{1,0:T(8,128)(2,1)} async-done(((bf16[768,96]{1,0:T(8,128)(2,1)}), bf16[192,96]{1,0:T(8,128)(2,1)}) %reduce-scatter.19.cloned.1.call-update) | async-done | bytes 36880
  412.6 23.4 %psum.8 = bf16[96,192]{1,0:T(8,128)(2,1)S(1)} all-reduce(bf16[96,192]{1,0:T(8,128)(2,1)S(1)} %copy.84), channel_id=1, replica_groups=mesh['dp'=4,'expert'=8] {'expert'}, use_global_device_ids=true, to_apply=%region_0.0 | all-reduce | flops 18432 | bytes 73728 | tf_op jit(solution)/shard_map/psum | solution.py:1052
  438.5 38.2 %reduce-scatter.17.cloned.1.call-done = bf16[2048,192]{0,1:T(8,128)(2,1)} async-done(((bf16[2048,768]{0,1:T(8,128)(2,1)}), bf16[2048,192]{0,1:T(8,128)(2,1)}) %reduce-scatter.17.cloned.1.call-update) | async-done | bytes 786448 | tf_op jit(solution)/shard_map/reduce_scatter | solution.py:980
  479.2 60.2 %reduce-scatter.15.cloned.1.call-done = bf16[192,2048]{1,0:T(8,128)(2,1)} async-done(((bf16[768,2048]{1,0:T(8,128)(2,1)}), bf16[192,2048]{1,0:T(8,128)(2,1)}) %reduce-scatter.15.cloned.1.call-update) | async-done | bytes 786448 | tf_op jit(solution)/shard_map/reduce_scatter | solution.py:980
  541.9 60.0 %reduce-scatter.13.cloned.1.call-done = bf16[192,2048]{1,0:T(8,128)(2,1)} async-done(((bf16[768,2048]{1,0:T(8,128)(2,1)}), bf16[192,2048]{1,0:T(8,128)(2,1)}) %reduce-scatter.13.cloned.1.call-update) | async-done | bytes 786448 | tf_op jit(solution)/shard_map/reduce_scatter | solution.py:980
  604.4 24.5 %all-gather.13.cloned.1.call-done = bf16[192,3072]{1,0:T(8,128)(2,1)} async-done(((bf16[192,384]{1,0:T(8,128)(2,1)}), bf16[192,3072]{1,0:T(8,128)(2,1)}) %all-gather.13.cloned.1.call-update) | async-done | bytes 1179664 | tf_op jit(solution)/shard_map/all_gather | solution.py:1051
  (104 shorter events, 37.0 us)
Async XLA Ops:
  7.2 16.9 %copy-start.6 = (bf16[192,4]{0,1:T(4,128)(2,1)S(1)}, bf16[192,4]{0,1:T(4,128)(2,1)}, u32[]{:S(2)}) copy-start(bf16[192,4]{0,1:T(4,128)(2,1)} %param.25) | copy-start | bytes 4612
  7.2 17.3 %copy-start.8 = (bf16[192]{0:T(256)(128)(2,1)S(1)}, bf16[192]{0:T(256)(128)(2,1)}, u32[]{:S(2)}) copy-start(bf16[192]{0:T(256)(128)(2,1)} %param.20) | copy-start | bytes 1156
  7.2 17.4 %copy-start.9 = (bf16[192]{0:T(256)(128)(2,1)S(1)}, bf16[192]{0:T(256)(128)(2,1)}, u32[]{:S(2)}) copy-start(bf16[192]{0:T(256)(128)(2,1)} %param.23) | copy-start | bytes 1156
  7.2 17.5 %copy-start.4 = (bf16[192,12]{0,1:T(8,128)(2,1)S(1)}, bf16[192,12]{0,1:T(8,128)(2,1)}, u32[]{:S(2)}) copy-start(bf16[192,12]{0,1:T(8,128)(2,1)} %param.24) | copy-start | bytes 13828
  7.2 17.6 %copy-start.7 = (bf16[2,192]{1,0:T(2,128)(2,1)S(1)}, bf16[2,192]{1,0:T(2,128)(2,1)}, u32[]{:S(2)}) copy-start(bf16[2,192]{1,0:T(2,128)(2,1)} %param.26) | copy-start | bytes 2308
  7.2 18.8 %copy-start.2 = (f32[256,12]{0,1:T(8,128)S(1)}, f32[256,12]{0,1:T(8,128)}, u32[]{:S(2)}) copy-start(f32[256,12]{0,1:T(8,128)} %param.16) | copy-start | bytes 36868
  7.2 19.5 %copy-start.5 = (s32[256,2]{0,1:T(2,128)S(1)}, s32[256,2]{0,1:T(2,128)}, u32[]{:S(2)}) copy-start(s32[256,2]{0,1:T(2,128)} %param.18) | copy-start | bytes 6148
  7.3 59.0 %all-gather.15.cloned.1.call-start = ((), (), s32[]{:S(2)}) async-start(), calls=%async_computation.17 | async-start | bytes 5308416 | tf_op jit(solution)/shard_map/all_gather | solution.py:1012
  7.3 20.3 %copy-start.3 = (s32[1,256]{1,0:T(1,128)S(1)}, s32[1,256]{1,0:T(1,128)}, u32[]{:S(2)}) copy-start(s32[1,256]{1,0:T(1,128)} %row_ref.3) | copy-start | bytes 3076
  22.0 106.3 %all-gather.11.cloned.1.call-start = ((), (), s32[]{:S(2)}) async-start(), calls=%async_computation.10 | async-start | bytes 3932160 | tf_op jit(solution)/shard_map/all_gather | solution.py:1015
  22.8 169.3 %all-gather.7.cloned.1.call-start = ((), (), s32[]{:S(2)}) async-start(), calls=%async_computation.8 | async-start | bytes 3932160 | tf_op jit(solution)/shard_map/all_gather | solution.py:1013
  23.5 232.1 %all-gather.9.cloned.1.call-start = ((), (), s32[]{:S(2)}) async-start(), calls=%async_computation.9 | async-start | bytes 3932160 | tf_op jit(solution)/shard_map/all_gather | solution.py:1014
  24.1 347.0 %reduce-scatter.9.cloned.1.call-start = ((), (), s32[]{:S(2)}) async-start(), calls=%async_computation.11 | async-start | bytes 5308416 | tf_op jit(solution)/shard_map/reduce_scatter | solution.py:1049
  255.6 6.6 %copy-start.11 = (bf16[768,2048]{1,0:T(8,128)(2,1)S(1)}, bf16[768,2048]{1,0:T(8,128)(2,1)}, u32[]{:S(2)}) copy-start(bf16[768,2048]{1,0:T(8,128)(2,1)} %all-gather.7.cloned.1.call-done) | copy-start | bytes 9437188
  262.2 6.0 copy-start.15
  262.2 4.1 copy-start.10
  317.7 53.4 %copy-start = (f32[96,768]{1,0:T(8,128)S(1)}, f32[96,768]{1,0:T(8,128)}, u32[]{:S(2)}) copy-start(f32[96,768]{1,0:T(8,128)} %get-tuple-element.35) | copy-start | bytes 884740
  317.8 74.2 %reduce-scatter.11.cloned.1.call-start = ((), (), s32[]{:S(2)}) async-start(), calls=%async_computation.12 | async-start | bytes 737280 | tf_op jit(solution)/shard_map/reduce_scatter | solution.py:1050
  371.1 40.6 %reduce-scatter.19.cloned.1.call-start = ((), (), s32[]{:S(2)}) async-start(), calls=%async_computation.18 | async-start | bytes 245760
  372.0 104.7 %reduce-scatter.17.cloned.1.call-start = ((), (), s32[]{:S(2)}) async-start(), calls=%async_computation.16 | async-start | bytes 3932160 | tf_op jit(solution)/shard_map/reduce_scatter | solution.py:980
  377.3 162.1 %reduce-scatter.15.cloned.1.call-start = ((), (), s32[]{:S(2)}) async-start(), calls=%async_computation.15 | async-start | bytes 3932160 | tf_op jit(solution)/shard_map/reduce_scatter | solution.py:980
  382.4 219.5 %reduce-scatter.13.cloned.1.call-start = ((), (), s32[]{:S(2)}) async-start(), calls=%async_computation.14 | async-start | bytes 3932160 | tf_op jit(solution)/shard_map/reduce_scatter | solution.py:980
  387.6 4.4 copy-start.1
  387.6 241.3 %all-gather.13.cloned.1.call-start = ((), (), s32[]{:S(2)}) async-start(), calls=%async_computation.13 | async-start | bytes 1327104 | tf_op jit(solution)/shard_map/all_gather | solution.py:1051
  (5 other events, 9.1 us)
Sparse Core Ops, SparseCore 0:
  22.1 44.0 all-gather.14
  67.8 60.4 all-gather.10
  129.9 62.0 all-gather.6
  193.5 62.0 all-gather.8
  317.9 53.1 reduce-scatter.8
  373.2 18.6 reduce-scatter.10
  394.8 16.9 reduce-scatter.18
  414.1 62.6 reduce-scatter.16
  479.1 60.3 reduce-scatter.14
  541.6 60.3 reduce-scatter.12
  603.8 25.0 all-gather.12

commit v2 on v1

--- a/solution.py
+++ b/solution.py
@@ -530,6 +530,13 @@
 ROW_GAIN_TWO = 64
 ROW_VECTORS = 80
 SMALL_ROWS = 96
+SUM_ROUTER = 0
+SUM_EVEN = 12
+SUM_GAIN_ONE = 14
+SUM_GAIN_TWO = 15
+SUM_VECTORS = 16
+SUM_ROWS = 32
+SLICES = 4
 LANES = 128
 VMEM_BYTES = 60 * 1024 * 1024
 
@@ -797,7 +804,7 @@
     grad_prev_ref[...] = grad_logits
     grad_small_ref[...] = jnp.zeros_like(grad_small_ref)
     logits_low = grad_logits.astype(jnp.bfloat16)
-    grad_small_ref[ROW_ROUTER : ROW_ROUTER + NR, :] = dot_tn(logits_low, moe_low)
+    grad_small_ref[SUM_ROUTER : SUM_ROUTER + NR, :] = dot_tn(logits_low, moe_low)
     grad_moe = (
         copy_gate * grad
         + dot_nn(logits_low, small_ref[ROW_ROUTER : ROW_ROUTER + NR, :])
@@ -809,10 +816,10 @@
     for c in range(NC):
         grad_gap = firsts[c] * seconds[c] * const_gate[c] * (norm_dot - vector_dot[c])
         grad_moe = grad_moe + grad_gap * weight_gap[c : c + 1, :]
-        grad_small_ref[ROW_EVEN + c : ROW_EVEN + c + 1, :] = jnp.sum(
+        grad_small_ref[SUM_EVEN + c : SUM_EVEN + c + 1, :] = jnp.sum(
             grad_gap * moe_in, axis=0, keepdims=True
         )
-        grad_small_ref[ROW_VECTORS + c : ROW_VECTORS + c + 1, :] = jnp.sum(
+        grad_small_ref[SUM_VECTORS + c : SUM_VECTORS + c + 1, :] = jnp.sum(
             (const_gate[c] * seconds[c]) * grad, axis=0, keepdims=True
         )
 
@@ -825,7 +832,7 @@
         + inverse_two * scaled
         - hidden * (inverse_two * inverse_two * inverse_two * inner)
     )
-    grad_small_ref[ROW_GAIN_TWO : ROW_GAIN_TWO + 1, :] = jnp.sum(
+    grad_small_ref[SUM_GAIN_TWO : SUM_GAIN_TWO + 1, :] = jnp.sum(
         grad_moe * hidden * inverse_two, axis=0, keepdims=True
     )
     grad_input_ref[...] = grad_hidden
@@ -896,7 +903,7 @@
         + inverse_one * scaled_one
         - inputs * (inverse_one * inverse_one * inverse_one * inner_one)
     )
-    grad_small_ref[ROW_GAIN_ONE : ROW_GAIN_ONE + 1, :] = jnp.sum(
+    grad_small_ref[SUM_GAIN_ONE : SUM_GAIN_ONE + 1, :] = jnp.sum(
         grad_normed * inputs * inverse_one, axis=0, keepdims=True
     )
 
@@ -938,7 +945,7 @@
             jax.ShapeDtypeStruct((tokens, features), jnp.float32),
             jax.ShapeDtypeStruct((tokens, NR), jnp.float32),
             jax.ShapeDtypeStruct((parts, features, part_width), jnp.bfloat16),
-            jax.ShapeDtypeStruct((SMALL_ROWS, features), jnp.float32),
+            jax.ShapeDtypeStruct((SUM_ROWS, features), jnp.float32),
         ),
         scratch_shapes=[
             pltpu.VMEM((tokens, features), jnp.bfloat16),
@@ -955,31 +962,575 @@
     )(*args)
 
 
-def expert_both(token_rows, grad_rows, gate_weight, up_weight, down_weight):
-    gate_pre = dot_nn(token_rows, gate_weight)
-    up_pre = dot_nn(token_rows, up_weight)
-    sigmoid_gate = jax.nn.sigmoid(gate_pre)
-    silu_gate = gate_pre * sigmoid_gate
-    act = (silu_gate * up_pre).astype(jnp.bfloat16)
-    grad_down = dot_tn(act, grad_rows)
-    out = dot_nn(act, down_weight).astype(jnp.bfloat16)
-    grad_act = dot_nt(grad_rows, down_weight)
-    grad_up_pre = (grad_act * silu_gate).astype(jnp.bfloat16)
-    grad_gate_pre = (
-        grad_act * up_pre * sigmoid_gate * (1.0 + gate_pre * (1.0 - sigmoid_gate))
+def copy_to(source, target, send_sem, recv_sem, device):
+    return pltpu.make_async_remote_copy(
+        src_ref=source,
+        dst_ref=target,
+        send_sem=send_sem,
+        recv_sem=recv_sem,
+        device_id=device,
+        device_id_type=pl.DeviceIdType.MESH,
+    )
+
+
+def neighbours():
+    depth = lax.axis_size("dp")
+    place = lax.axis_index("dp")
+    mine = lax.axis_index("expert")
+    core = mine % 2
+    across = (mine // 2) % 2
+    along = mine // 4
+    chips = [
+        ((along + step // 2) % 2) * 4 + ((across + step % 2) % 2) * 2 for step in range(4)
+    ]
+    lines = [(place + step) % depth for step in range(depth)]
+    return place, mine, core, chips, lines
+
+
+def greet(devices):
+    barrier = pltpu.get_barrier_semaphore()
+    for device in devices:
+        pl.semaphore_signal(
+            barrier, inc=1, device_id=device, device_id_type=pl.DeviceIdType.MESH
+        )
+    pl.semaphore_wait(barrier, len(devices))
+
+
+def all_peers(place, core, chips, lines):
+    own = chips[0] + core
+    partner = (place, chips[0] + 1 - core)
+    plane = [(place, chip + core) for chip in chips[1:]]
+    line = [(spot, own) for spot in lines[1:]]
+    return partner, plane, line
+
+
+def start_kernel(
+    piece_ref,
+    pack_ref,
+    weight_ref,
+    small_ref,
+    line_send,
+    line_recv,
+    pack_send,
+    pack_recv,
+    plane_send,
+    plane_recv,
+    pair_send,
+    pair_recv,
+    own_sem,
+    own_pack_sem,
+):
+    place, mine, core, chips, lines = neighbours()
+    depth = len(lines)
+    partner, plane, line = all_peers(place, core, chips, lines)
+    greet([partner] + plane + line)
+    own_copy = pltpu.make_async_copy(piece_ref, weight_ref.at[mine, place], own_sem)
+    own_pack = pltpu.make_async_copy(pack_ref, small_ref.at[place], own_pack_sem)
+    own_copy.start()
+    own_pack.start()
+    sent = []
+
+    def line_copy(step):
+        return copy_to(
+            piece_ref,
+            weight_ref.at[mine, place],
+            line_send.at[step - 1],
+            line_recv.at[depth - step - 1],
+            line[step - 1],
+        )
+
+    def pack_copy(step):
+        return copy_to(
+            pack_ref,
+            small_ref.at[place],
+            pack_send.at[step - 1],
+            pack_recv.at[depth - step - 1],
+            line[step - 1],
+        )
+
+    for step in range(1, depth):
+        copy = line_copy(step)
+        copy.start()
+        sent.append(copy)
+    for chip in (3, 1, 2):
+        copy = copy_to(
+            piece_ref,
+            weight_ref.at[mine, place],
+            plane_send.at[chip - 1, 0],
+            plane_recv.at[chip - 1, 0],
+            plane[chip - 1],
+        )
+        copy.start()
+        sent.append(copy)
+    copy = copy_to(
+        piece_ref, weight_ref.at[mine, place], pair_send.at[0, 0], pair_recv.at[0, 0], partner
+    )
+    copy.start()
+    sent.append(copy)
+    for step in range(1, depth):
+        copy = pack_copy(step)
+        copy.start()
+        sent.append(copy)
+
+    def arrived(slot, spot, semaphore):
+        here = weight_ref.at[slot, spot]
+        copy_to(here, here, own_sem, semaphore, partner).wait_recv()
+        return here
+
+    for step in range(depth):
+        spot = lines[step]
+        if step > 0:
+            here = arrived(mine, spot, line_recv.at[step - 1])
+            for chip in (3, 1, 2):
+                copy = copy_to(
+                    here,
+                    here,
+                    plane_send.at[chip - 1, step],
+                    plane_recv.at[chip - 1, step],
+                    plane[chip - 1],
+                )
+                copy.start()
+                sent.append(copy)
+            copy = copy_to(here, here, pair_send.at[0, step], pair_recv.at[0, step], partner)
+            copy.start()
+            sent.append(copy)
+    for step in range(depth):
+        spot = lines[step]
+        for chip in (1, 2, 3):
+            here = arrived(chips[chip] + core, spot, plane_recv.at[chip - 1, step])
+            copy = copy_to(
+                here, here, pair_send.at[chip, step], pair_recv.at[chip, step], partner
+            )
+            copy.start()
+            sent.append(copy)
+    for step in range(depth):
+        for chip in range(4):
+            arrived(chips[chip] + 1 - core, lines[step], pair_recv.at[chip, step])
+    for step in range(1, depth):
+        here = small_ref.at[lines[step]]
+        copy_to(here, here, own_pack_sem, pack_recv.at[step - 1], partner).wait_recv()
+    own_copy.wait()
+    own_pack.wait()
+    for copy in sent:
+        copy.wait_send()
+
+
+def gather_start(piece, pack, parts, depth):
+    dma = pltpu.SemaphoreType.DMA
+    return pl.pallas_call(
+        start_kernel,
+        out_shape=(
+            jax.ShapeDtypeStruct((parts, depth) + piece.shape, piece.dtype),
+            jax.ShapeDtypeStruct((depth,) + pack.shape, pack.dtype),
+        ),
+        in_specs=[pl.BlockSpec(memory_space=pltpu.VMEM)] * 2,
+        out_specs=[pl.BlockSpec(memory_space=pltpu.VMEM)] * 2,
+        scratch_shapes=[
+            dma((depth - 1,)),
+            dma((depth - 1,)),
+            dma((depth - 1,)),
+            dma((depth - 1,)),
+            dma((3, depth)),
+            dma((3, depth)),
+            dma((4, depth)),
+            dma((4, depth)),
+            dma,
+            dma,
+        ],
+        compiler_params=pltpu.CompilerParams(
+            collective_id=1, has_side_effects=True, vmem_limit_bytes=16 << 20
+        ),
+        cost_estimate=pl.CostEstimate(flops=0, transcendentals=0, bytes_accessed=80 << 20),
+        name="start",
+    )(piece, pack)
+
+
+def slice_kernel(first, last, *refs):
+    if first:
+        rows_ref, weight_ref, *refs = refs
+    else:
+        rows_ref, weight_ref, out_in, back_in, *refs = refs
+    if last:
+        grad_ref, both_ref, gates, ups, downs, rows_turned, grads_turned, out_sum, back_sum = refs
+    else:
+        grad_ref, out_sum, back_sum, gates, ups, downs, rows_turned, grads_turned = refs
+    depth, triple, width = weight_ref.shape
+    part = triple // 3
+    sources, _, slots, features = rows_ref.shape
+    token_rows = rows_ref[:, 0].reshape(sources * slots, features)
+    grad_rows = rows_ref[:, 1].reshape(sources * slots, features)
+    rows_turned[...] = token_rows.T
+    grads_turned[...] = grad_rows.T
+    for spot in range(depth):
+        here = slice(spot * part, (spot + 1) * part)
+        gates[here, :] = weight_ref[spot, :part]
+        ups[here, :] = weight_ref[spot, part : 2 * part]
+        downs[here, :] = weight_ref[spot, 2 * part :]
+    if first:
+        out_sum[...] = jnp.zeros_like(out_sum)
+        back_sum[...] = jnp.zeros_like(back_sum)
+    else:
+        out_sum[...] = out_in[...]
+        back_sum[...] = back_in[...]
+    chunk = 256
+
+    def one_chunk(step, carry):
+        columns = pl.ds(pl.multiple_of(step * chunk, chunk), chunk)
+        gate_weight = gates[:, columns]
+        up_weight = ups[:, columns]
+        down_weight = downs[:, columns]
+        gate_pre = dot_nn(token_rows, gate_weight)
+        up_pre = dot_nn(token_rows, up_weight)
+        grad_act = dot_nn(grad_rows, down_weight)
+        sigmoid_gate = jax.nn.sigmoid(gate_pre)
+        silu_gate = gate_pre * sigmoid_gate
+        act = (silu_gate * up_pre).astype(jnp.bfloat16)
+        grad_up_pre = (grad_act * silu_gate).astype(jnp.bfloat16)
+        grad_gate_pre = (
+            grad_act * up_pre * sigmoid_gate * (1.0 + gate_pre * (1.0 - sigmoid_gate))
+        ).astype(jnp.bfloat16)
+        turned = (
+            dot_nn(rows_turned[...], grad_gate_pre),
+            dot_nn(rows_turned[...], grad_up_pre),
+            dot_nn(grads_turned[...], act),
+        )
+        for kind, product in enumerate(turned):
+            low = product.astype(jnp.bfloat16)
+            for spot in range(depth):
+                grad_ref[spot, kind * part : (kind + 1) * part, columns] = low[
+                    spot * part : (spot + 1) * part
+                ]
+        out_sum[...] += dot_nt(act, down_weight)
+        back_sum[...] += dot_nt(grad_gate_pre, gate_weight) + dot_nt(grad_up_pre, up_weight)
+        return carry
+
+    lax.fori_loop(0, width // chunk, one_chunk, 0)
+    if last:
+        both_ref[:, 0] = out_sum[...].astype(jnp.bfloat16).reshape(sources, slots, features)
+        both_ref[:, 1] = back_sum[...].astype(jnp.bfloat16).reshape(sources, slots, features)
+
+
+def run_slice(received, weights, sums, last):
+    depth, triple, width = weights.shape
+    sources, _, slots, features = received.shape
+    rows = sources * slots
+    total = jax.ShapeDtypeStruct((rows, features), jnp.float32)
+    grads = jax.ShapeDtypeStruct(weights.shape, jnp.bfloat16)
+    low = jnp.bfloat16
+    scratch = [pltpu.VMEM((features, width), low)] * 3 + [pltpu.VMEM((features, rows), low)] * 2
+    if last:
+        out_shape = (grads, jax.ShapeDtypeStruct(received.shape, low))
+        scratch = scratch + [pltpu.VMEM((rows, features), jnp.float32)] * 2
+    else:
+        out_shape = (grads, total, total)
+
+    def body(*refs):
+        slice_kernel(not sums, last, *refs)
+
+    return pl.pallas_call(
+        body,
+        out_shape=out_shape,
+        scratch_shapes=scratch,
+        compiler_params=pltpu.CompilerParams(vmem_limit_bytes=48 << 20),
+        cost_estimate=pl.CostEstimate(
+            flops=18 * rows * features * width,
+            transcendentals=rows * width,
+            bytes_accessed=16 << 20,
+        ),
+        name="experts",
+    )(received, weights, *sums)
+
+
+def reduce_kernel(
+    grad_ref, own_ref, risen, fallen, rise_send, rise_recv, fall_send, fall_recv
+):
+    depth, rows, _ = grad_ref.shape
+    pieces = rise_send.shape[1]
+    part = rows // pieces
+    place = lax.axis_index("dp")
+    mine = lax.axis_index("expert")
+    above, below = (place + 1, mine), (place - 1, mine)
+    top = depth - 1
+    barrier = pltpu.get_barrier_semaphore()
+    for there, device in ((place > 0, below), (place < top, above)):
+
+        @pl.when(there)
+        def _():
+            pl.semaphore_signal(
+                barrier, inc=1, device_id=device, device_id_type=pl.DeviceIdType.MESH
+            )
+
+    at_end = (place == 0) | (place == top)
+    for there, count in ((at_end, 1), (jnp.logical_not(at_end), 2)):
+
+        @pl.when(there)
+        def _():
+            pl.semaphore_wait(barrier, count)
+
+    def moved(source, held, owner, piece, send, recv, device):
+        at = pl.ds(piece * part, part)
+        return copy_to(
+            source.at[owner, at],
+            held.at[owner, at],
+            send.at[owner, piece],
+            recv.at[owner, piece],
+            device,
+        )
+
+    def pass_on(held, owner, piece, send, recv, device, leads, follows):
+        at = slice(piece * part, (piece + 1) * part)
+
+        @pl.when(leads)
+        def _():
+            moved(grad_ref, held, owner, piece, send, recv, device).start()
+
+        @pl.when(follows)
+        def _():
+            moved(held, held, owner, piece, send, recv, device).wait_recv()
+            held[owner, at] = (
+                held[owner, at].astype(jnp.float32) + grad_ref[owner, at].astype(jnp.float32)
+            ).astype(jnp.bfloat16)
+            moved(held, held, owner, piece, send, recv, device).start()
+
+    for step in range(top):
+        rise, fall = top - step, step
+        for piece in range(pieces):
+            pass_on(
+                risen, rise, piece, rise_send, rise_recv, above,
+                (place == 0) & (place < rise), (place > 0) & (place < rise),
+            )
+            pass_on(
+                fallen, fall, piece, fall_send, fall_recv, below,
+                (place == top) & (place > fall), (place < top) & (place > fall),
+            )
+    for piece in range(pieces):
+        at = slice(piece * part, (piece + 1) * part)
+        own_ref[at, :] = grad_ref[place, at].astype(jnp.float32)
+
+        @pl.when(place < top)
+        def _():
+            moved(fallen, fallen, place, piece, fall_send, fall_recv, above).wait_recv()
+            own_ref[at, :] += fallen[place, at].astype(jnp.float32)
+
+        @pl.when(place > 0)
+        def _():
+            moved(risen, risen, place, piece, rise_send, rise_recv, below).wait_recv()
+            own_ref[at, :] += risen[place, at].astype(jnp.float32)
+
+    for step in range(top):
+        rise, fall = top - step, step
+        for piece in range(pieces):
+
+            @pl.when(place < rise)
+            def _():
+                moved(risen, risen, rise, piece, rise_send, rise_recv, above).wait_send()
+
+            @pl.when(place > fall)
+            def _():
+                moved(fallen, fallen, fall, piece, fall_send, fall_recv, below).wait_send()
+
+
+def reduce_line(grads):
+    depth, rows, width = grads.shape
+    pieces = 3
+    dma = pltpu.SemaphoreType.DMA
+    return pl.pallas_call(
+        reduce_kernel,
+        out_shape=jax.ShapeDtypeStruct((rows, width), jnp.float32),
+        in_specs=[pl.BlockSpec(memory_space=pltpu.VMEM)],
+        out_specs=pl.BlockSpec(memory_space=pltpu.VMEM),
+        scratch_shapes=[pltpu.VMEM(grads.shape, grads.dtype)] * 2 + [dma((depth, pieces))] * 4,
+        compiler_params=pltpu.CompilerParams(
+            collective_id=2, has_side_effects=True, vmem_limit_bytes=24 << 20
+        ),
+        cost_estimate=pl.CostEstimate(flops=0, transcendentals=0, bytes_accessed=100 << 20),
+        name="reduce",
+    )(grads)
+
+
+def tail_kernel(
+    grad_ref,
+    small_ref,
+    out_ref,
+    small_out_ref,
+    pair_held,
+    pair_sum,
+    plane_held,
+    plane_sum,
+    line_held,
+    small_pair,
+    small_pair_sum,
+    small_plane,
+    small_plane_sum,
+    small_line,
+    pair_send,
+    pair_recv,
+    plane_send,
+    plane_recv,
+    line_send,
+    line_recv,
+    give_send,
+    give_recv,
+    share_send,
+    share_recv,
+    small_send,
+    small_recv,
+):
+    place, mine, core, chips, lines = neighbours()
+    depth = len(lines)
+    partner, plane, line = all_peers(place, core, chips, lines)
+    greet([partner] + plane + line)
+    high = jnp.float32
+    sent = []
+
+    def send(*items):
+        copy = copy_to(*items)
+        copy.start()
+        sent.append(copy)
+
+    def arrived(here, semaphore):
+        copy_to(here, here, small_send.at[0], semaphore, partner).wait_recv()
+
+    send(small_ref, small_pair, small_send.at[0], small_recv.at[0], partner)
+    order = (3, 1, 2, 0)
+    for chip in order:
+        send(
+            grad_ref.at[chips[chip] + 1 - core],
+            pair_held.at[chip],
+            pair_send.at[chip],
+            pair_recv.at[chip],
+            partner,
+        )
+    arrived(small_pair, small_recv.at[0])
+    small_pair_sum[...] = (small_ref[...].astype(high) + small_pair[...].astype(high)).astype(
+        jnp.bfloat16
+    )
+    for chip in (3, 1, 2):
+        send(
+            small_pair_sum,
+            small_plane.at[chip - 1],
+            small_send.at[chip],
+            small_recv.at[chip],
+            plane[chip - 1],
+        )
+    steps = tuple(range(1, depth)) + (0,)
+    for chip in order:
+        arrived(pair_held.at[chip], pair_recv.at[chip])
+        for step in steps:
+            spot = lines[step]
+            pair_sum[chip, spot] = (
+                grad_ref[chips[chip] + core, spot].astype(high)
+                + pair_held[chip, spot].astype(high)
+            ).astype(jnp.bfloat16)
+            if chip > 0:
+                send(
+                    pair_sum.at[chip, spot],
+                    plane_held.at[chip - 1, spot],
+                    plane_send.at[chip - 1, step],
+                    plane_recv.at[chip - 1, step],
+                    plane[chip - 1],
+                )
+    for chip in (1, 2, 3):
+        arrived(small_plane.at[chip - 1], small_recv.at[chip])
+    small_plane_sum[...] = (
+        (small_pair_sum[...].astype(high) + small_plane[0].astype(high))
+        + (small_plane[1].astype(high) + small_plane[2].astype(high))
     ).astype(jnp.bfloat16)
-    grad_gate = dot_tn(token_rows, grad_gate_pre)
-    grad_up = dot_tn(token_rows, grad_up_pre)
-    grad_tokens = (dot_nt(grad_gate_pre, gate_weight) + dot_nt(grad_up_pre, up_weight)).astype(
-        jnp.bfloat16
-    )
-    return out, grad_tokens, grad_gate, grad_up, grad_down
-
-
-def scatter_sum(value, axis):
-    return lax.psum_scatter(
-        value.astype(jnp.bfloat16), "dp", scatter_dimension=axis, tiled=True
-    ).astype(jnp.float32)
+    for step in range(1, depth):
+        send(
+            small_plane_sum.at[lines[step]],
+            small_line.at[depth - step - 1],
+            small_send.at[3 + step],
+            small_recv.at[3 + depth - step],
+            line[step - 1],
+        )
+    for step in steps:
+        spot = lines[step]
+        for chip in (1, 2, 3):
+            arrived(plane_held.at[chip - 1, spot], plane_recv.at[chip - 1, step])
+        plane_sum[step] = (
+            (pair_sum[0, spot].astype(high) + plane_held[0, spot].astype(high))
+            + (plane_held[1, spot].astype(high) + plane_held[2, spot].astype(high))
+        ).astype(jnp.bfloat16)
+        if step > 0:
+            send(
+                plane_sum.at[step],
+                line_held.at[depth - step - 1],
+                line_send.at[step - 1],
+                line_recv.at[depth - step - 1],
+                line[step - 1],
+            )
+    total = plane_sum[0].astype(high)
+    for step in range(1, depth):
+        arrived(line_held.at[step - 1], line_recv.at[step - 1])
+        total = total + line_held[step - 1].astype(high)
+    out_ref[mine] = total.astype(jnp.bfloat16)
+    for chip in (3, 1, 2):
+        send(
+            out_ref.at[mine],
+            out_ref.at[mine],
+            give_send.at[chip - 1],
+            give_recv.at[chip - 1],
+            plane[chip - 1],
+        )
+    send(out_ref.at[mine], out_ref.at[mine], share_send.at[0], share_recv.at[0], partner)
+    total = small_plane_sum[place].astype(high)
+    for step in range(1, depth):
+        arrived(small_line.at[step - 1], small_recv.at[3 + step])
+        total = total + small_line[step - 1].astype(high)
+    small_out_ref[...] = total
+    for chip in (1, 2, 3):
+        here = out_ref.at[chips[chip] + core]
+        arrived(here, give_recv.at[chip - 1])
+        send(here, here, share_send.at[chip], share_recv.at[chip], partner)
+    for chip in range(4):
+        arrived(out_ref.at[chips[chip] + 1 - core], share_recv.at[chip])
+    for copy in sent:
+        copy.wait_send()
+
+
+def reduce_tail(grads, small):
+    parts, depth, rows, width = grads.shape
+    dma = pltpu.SemaphoreType.DMA
+    low = grads.dtype
+    return pl.pallas_call(
+        tail_kernel,
+        out_shape=(
+            jax.ShapeDtypeStruct((parts, rows, width), low),
+            jax.ShapeDtypeStruct(small.shape[1:], jnp.float32),
+        ),
+        in_specs=[pl.BlockSpec(memory_space=pltpu.VMEM)] * 2,
+        out_specs=[pl.BlockSpec(memory_space=pltpu.VMEM)] * 2,
+        scratch_shapes=[
+            pltpu.VMEM((4, depth, rows, width), low),
+            pltpu.VMEM((4, depth, rows, width), low),
+            pltpu.VMEM((3, depth, rows, width), low),
+            pltpu.VMEM((depth, rows, width), low),
+            pltpu.VMEM((depth - 1, rows, width), low),
+            pltpu.VMEM(small.shape, low),
+            pltpu.VMEM(small.shape, low),
+            pltpu.VMEM((3,) + small.shape, low),
+            pltpu.VMEM(small.shape, low),
+            pltpu.VMEM((depth - 1,) + small.shape[1:], low),
+            dma((4,)),
+            dma((4,)),
+            dma((3, depth)),
+            dma((3, depth)),
+            dma((depth - 1,)),
+            dma((depth - 1,)),
+            dma((3,)),
+            dma((3,)),
+            dma((4,)),
+            dma((4,)),
+            dma((3 + depth,)),
+            dma((3 + depth,)),
+        ],
+        compiler_params=pltpu.CompilerParams(
+            collective_id=3, has_side_effects=True, vmem_limit_bytes=40 << 20
+        ),
+        cost_estimate=pl.CostEstimate(flops=0, transcendentals=0, bytes_accessed=120 << 20),
+        name="tail",
+    )(grads, small)
 
 
 def local_fast(
@@ -1001,18 +1552,27 @@
 ):
     tokens, features = layer_input.shape
     parts = lax.axis_size("expert")
+    depth = lax.axis_size("dp")
+    own_rows = qkv_weight.shape[0]
     part_width = 4 * features // parts
     mine = lax.axis_index("expert")
+    hidden_units = exp_gate.shape[1]
+    width = hidden_units // SLICES
+    gathered = []
+    for step in range(SLICES):
+        columns = slice(step * width, (step + 1) * width)
+        triple = jnp.concatenate(
+            [exp_gate[:, columns], exp_up[:, columns], exp_down[columns].T], axis=0
+        )
+        gathered.append(lax.all_gather(triple, "dp", axis=0, tiled=True))
     both = jnp.concatenate([qkv_weight, out_weight], axis=1)
-    small = lax.all_gather(
-        pack_small(router, const_w, gain_attn, gain_moe, const_v), "dp", axis=1, tiled=True
-    )
     piece = lax.dynamic_slice_in_dim(both, mine * part_width, part_width, axis=1)
-    column = lax.all_gather(piece, "dp", axis=0, tiled=True)
-    weights = lax.all_gather(column, "expert", axis=0)
-    gate_full = lax.all_gather(exp_gate, "dp", axis=0, tiled=True)
-    up_full = lax.all_gather(exp_up, "dp", axis=0, tiled=True)
-    down_full = lax.all_gather(exp_down, "dp", axis=1, tiled=True)
+    pack = pack_small(router, const_w, gain_attn, gain_moe, const_v)
+    pack_width = pl.cdiv(own_rows, LANES) * LANES
+    pack = jnp.pad(pack, ((0, 0), (0, pack_width - own_rows)))
+    weights, small = gather_start(piece, pack, parts, depth)
+    weights = weights.reshape(parts, features, part_width)
+    small = small[:, :, :own_rows].transpose(1, 0, 2).reshape(SMALL_ROWS, features)
     cosine, sine = rotary_tables(tokens, features // HEADS)
     common = (
         layer_input,
@@ -1028,44 +1588,51 @@
     )
     *saved, rows = run_before(common, parts, part_width)
     received = lax.all_to_all(rows, "expert", split_axis=0, concat_axis=0, tiled=True)
-    slots = EXPERTS * CAP
-    out, grad_tokens, grad_gate, grad_up, grad_down = expert_both(
-        received[:, 0].reshape(slots, features),
-        received[:, 1].reshape(slots, features),
-        gate_full,
-        up_full,
-        down_full,
-    )
-    back = jnp.stack(
-        [out.reshape(EXPERTS, CAP, features), grad_tokens.reshape(EXPERTS, CAP, features)], axis=1
-    )
+    sums = ()
+    owned = []
+    for step in range(SLICES):
+        last = step == SLICES - 1
+        triple = gathered[step].reshape(depth, 3 * own_rows, width)
+        grads, *sums = run_slice(received, triple, tuple(sums), last)
+        if last:
+            back = sums[0]
+            share = lax.psum_scatter(grads, "dp", scatter_dimension=0, tiled=False)
+            owned.append(share.astype(jnp.float32))
+        else:
+            share = reduce_line(grads)
+            *sums, share = lax.optimization_barrier((*sums, share))
+            owned.append(share)
     returned = lax.all_to_all(back, "expert", split_axis=0, concat_axis=0, tiled=True)
-    own_down = scatter_sum(grad_down, 1)
-    own_gate = scatter_sum(grad_gate, 0)
-    own_up = scatter_sum(grad_up, 0)
     result, grad_input, grad_prev, grad_weights, grad_small = run_after(
         common + tuple(saved) + (returned,), parts, part_width
     )
-    share = lax.psum_scatter(grad_weights, "expert", scatter_dimension=0, tiled=False)
-    share = lax.psum_scatter(share, "dp", scatter_dimension=0, tiled=True)
-    own_weights = lax.all_gather(share, "expert", axis=1, tiled=True).astype(jnp.float32)
-    own_small = scatter_sum(lax.psum(grad_small.astype(jnp.bfloat16), "expert"), 1)
-    grad_even = own_small[ROW_EVEN : ROW_EVEN + NC]
+    small_parts = (
+        grad_small.astype(jnp.bfloat16).reshape(SUM_ROWS, depth, own_rows).transpose(1, 0, 2)
+    )
+    small_parts = jnp.pad(small_parts, ((0, 0), (0, 0), (0, pack_width - own_rows)))
+    own_weights, own_small = reduce_tail(
+        grad_weights.reshape(parts, depth, own_rows, part_width), small_parts
+    )
+    own_weights = own_weights.transpose(1, 0, 2).reshape(own_rows, 4 * features)
+    own_weights = own_weights.astype(jnp.float32)
+    own_small = own_small[:, :own_rows]
+    grad_even = own_small[SUM_EVEN : SUM_EVEN + NC]
     grad_const = jnp.stack([grad_even, -grad_even], axis=1).reshape(2 * NC, -1).T
+    owned = jnp.concatenate(owned, axis=1)
     return (
         result,
         grad_input,
         grad_prev,
-        own_small[ROW_GAIN_ONE],
+        own_small[SUM_GAIN_ONE],
         own_weights[:, : 3 * features],
         own_weights[:, 3 * features :],
-        own_small[ROW_GAIN_TWO],
-        own_small[ROW_ROUTER : ROW_ROUTER + NR].T,
+        own_small[SUM_GAIN_TWO],
+        own_small[SUM_ROUTER : SUM_ROUTER + NR].T,
         grad_const,
-        own_small[ROW_VECTORS : ROW_VECTORS + NC],
-        own_gate,
-        own_up,
-        own_down,
+        own_small[SUM_VECTORS : SUM_VECTORS + NC],
+        owned[:own_rows],
+        owned[own_rows : 2 * own_rows],
+        owned[2 * own_rows :].T,
     )
 
 

time: 642 us -> 489 us (0.76)
  waiting for transfers between devices: 425 us -> 0.15 us
  Pallas kernels: 38.2 us -> 371 us
  blocking collectives: 96.7 us -> 56.2 us
  matrix products: 35.8 us -> 0 us
  local copies, waits for them, and re-layouts: 20.3 us -> 37.9 us
    pallas_call x0 -> x9, Pallas kernels: none -> 333 us  [the longest x3 190 us: reduce_line(): pl.pallas_call(reduce_kernel, out_shape=jax.ShapeDtypeStruct((rows, width...]
    reduce_scatter x5 -> x1, waiting for transfers between devices: 216 us -> 0.01 us  [local_fast(): share = lax.psum_scatter(grads, 'dp', scatter_dimension=0, tiled=False)]
    all_gather x5 -> x4, waiting for transfers between devices: 188 us -> 0.06 us  [local_fast(): gathered.append(lax.all_gather(triple, 'dp', axis=0, tiled=True))]
    dot_general x9 -> x0, matrix products: 35.8 us -> none  [the longest x3 14.1 us: dot_nn(): return jnp.dot(left, right, preferred_element_type=jnp.float32)]
    all_gather x2 -> x0, blocking collectives: 25.5 us -> none  [the longest x1 13.7 us: local_fast(): column = lax.all_gather(piece, 'dp', axis=0, tiled=True)]
    psum x1 -> x0, blocking collectives: 23.4 us -> none  [local_fast(): lax.psum(grad_small.astype(jnp.bfloat16), 'expert')]
    unnamed x12 -> x5, waiting for transfers between devices: 21.1 us -> 0.08 us
    unnamed x43 -> x61, local copies, waits for them, and re-layouts: 9.58 us -> 21.9 us
  transfers between devices with their start and end apart: 11 -> 5, of which waited for: 11 -> 0; matrix products, arithmetic and copies ran while one was open for 7% -> 4% of each run, Pallas kernels for 2% -> 74%
where the time goes in v2:
time: 489 us; the launch traced here: 487 us
  Pallas kernels  371 us (76%)
  blocking collectives  56.2 us (11%)
  local copies, waits for them, and re-layouts  37.9 us (8%)
  between operations  14.3 us (3%)
  other arithmetic  7.6 us (2%)
    pallas_call x3, Pallas kernels, reduce_line(): pl.pallas_call(reduce_kernel, out_shape=jax.ShapeDtypeStruct((rows, width...  190 us
    pallas_call x1, Pallas kernels, gather_start(): pl.pallas_call(start_kernel, out_shape=(jax.ShapeDtypeStruct((parts, dept...  54.6 us
    pallas_call x1, Pallas kernels, reduce_tail(): pl.pallas_call(tail_kernel, out_shape=(jax.ShapeDtypeStruct((parts, rows,...  50.4 us
    pallas_call x4, Pallas kernels, run_slice(): pl.pallas_call(body, out_shape=out_shape, scratch_shapes=scratch, compile...  37.9 us
    all_to_all x1, blocking collectives, local_fast(): lax.all_to_all(back, 'expert', split_axis=0, concat_axis=0, tiled=True)  32.5 us
    all_to_all x1, blocking collectives, local_fast(): lax.all_to_all(rows, 'expert', split_axis=0, concat_axis=0, tiled=True)  23.8 us
    pallas_call x1, Pallas kernels, run_after(): pl.pallas_call(after_kernel, out_shape=(jax.ShapeDtypeStruct((tokens, fea...  23.3 us
    unnamed x61, local copies, waits for them, and re-layouts  21.9 us
  transfers between devices with their start and end apart: 5, of which 0 were waited for; matrix products, arithmetic and copies ran while one was open for 4% of the time, Pallas kernels for 74%

profile of v2, /device:TPU:9, one launch (start us, length us, event | category | flops | bytes accessed | tf_op | source)
XLA Modules:
  0.0 487.1 jit_solution(10374915068528985457)
XLA Ops:
  13.8 54.6 %start.1 = (bf16[8,4,192,384]{3,2,1,0:T(8,128)(2,1)S(1)}, bf16[4,96,256]{2,1,0:T(8,128)(2,1)S(1)}) custom-call(bf16[192,384]{1,0:T(8,128)(2,1)S(1)} %fusion.piece_ref, bf16[96,256]{1,0:T(8,128)(2,1)S(1)} %pad.8.pack_ref), custom_call_target="tpu_custom_call" | custom-call | bytes 83886080 | tf_op jit(solution)/shard_map/start/pallas_call | solution.py:1120
  68.4 2.2 copy-done
  75.8 14.9 %before.1 = (bf16[256,768]{1,0:T(8,128)(2,1)}, bf16[256,768]{1,0:T(8,128)(2,1)}, bf16[256,768]{1,0:T(8,128)(2,1)}, bf16[256,768]{1,0:T(8,128)(2,1)}, f32[256,768...) custom-call(bf16[256,768]{1,0:T(8,128)(2,1)} %input_ref.3, f32[256,12]{1,0:T(8,128)} %copy.40.prev_ref, ...), custom_call_target="tpu_custom_call" | custom-call | flops 1207959552 | bytes 20971520 | tf_op jit(solution)/shard_map/before/pallas_call | solution.py:914
  90.7 23.8 %all_to_all.10.refs_0_ = bf16[8,2,64,768]{3,2,1,0:T(8,128)(2,1)S(1)} all-to-all(bf16[8,2,64,768]{3,2,1,0:T(8,128)(2,1)} %get-tuple-element.57), channel_id=1, replica_groups=mesh['dp'=4,'expert'=8] {'expert'}, dimensions={0} | all-to-all | bytes 3145728 | tf_op jit(solution)/shard_map/all_to_all | solution.py:1590
  114.4 9.4 %experts.4 = (bf16[4,576,512]{2,1,0:T(8,128)(2,1)}, f32[512,768]{1,0:T(8,128)S(1)}, f32[512,768]{1,0:T(8,128)S(1)}) custom-call(bf16[8,2,64,768]{3,2,1,0:T(8,128)(2,1)S(1)} %all_to_all.10.refs_0_, bf16[4,576,512]{2,1,0:T(8,128)(2,1)} %bitcast.58), custom_call_target="tpu_custom_call" | custom-call | flops 3623878656 | bytes 16777216 | tf_op jit(solution)/shard_map/experts/pallas_call | solution.py:1230
  123.8 2.8 copy-done.4
  126.6 76.4 %reduce.3 = f32[576,512]{1,0:T(8,128)S(1)} custom-call(bf16[4,576,512]{2,1,0:T(8,128)(2,1)S(1)} %copy-done.4), custom_call_target="tpu_custom_call" | custom-call | bytes 104857600 | tf_op jit(solution)/shard_map/reduce/pallas_call | solution.py:1337
  203.1 9.8 %experts.5 = (bf16[4,576,512]{2,1,0:T(8,128)(2,1)}, f32[512,768]{1,0:T(8,128)S(1)}, f32[512,768]{1,0:T(8,128)S(1)}) custom-call(bf16[8,2,64,768]{3,2,1,0:T(8,128)(2,1)S(1)} %all_to_all.10.refs_0_, bf16[4,576,512]{2,1,0:T(8,128)(2,1)} %bitcast.59, f32[512,768]{1,0:T(8,128)} %copy-done.15, f32[512,768]{1,0:T(8,128)} %copy-done.16), custom_call_target="tpu_custom_call" | custom-call | flops 3623878656 | bytes 16777216 | tf_op jit(solution)/shard_map/experts/pallas_call | solution.py:1230
  212.9 2.9 copy-done.2
  215.8 74.2 %reduce.4 = f32[576,512]{1,0:T(8,128)S(1)} custom-call(bf16[4,576,512]{2,1,0:T(8,128)(2,1)S(1)} %copy-done.2), custom_call_target="tpu_custom_call" | custom-call | bytes 104857600 | tf_op jit(solution)/shard_map/reduce/pallas_call | solution.py:1337
  290.0 1.4 copy-done.6
  291.4 9.8 %experts.6 = (bf16[4,576,512]{2,1,0:T(8,128)(2,1)}, f32[512,768]{1,0:T(8,128)S(1)}, f32[512,768]{1,0:T(8,128)S(1)}) custom-call(bf16[8,2,64,768]{3,2,1,0:T(8,128)(2,1)S(1)} %copy-done.6, bf16[4,576,512]{2,1,0:T(8,128)(2,1)} %bitcast.60, f32[512,768]{1,0:T(8,128)} %copy-done.10, f32[512,768]{1,0:T(8,128)} %copy-done.11), custom_call_target="tpu_custom_call" | custom-call | flops 3623878656 | bytes 16777216 | tf_op jit(solution)/shard_map/experts/pallas_call | solution.py:1230
  301.2 2.8 copy-done.3
  304.0 39.1 %reduce.5 = f32[576,512]{1,0:T(8,128)S(1)} custom-call(bf16[4,576,512]{2,1,0:T(8,128)(2,1)S(1)} %copy-done.3), custom_call_target="tpu_custom_call" | custom-call | bytes 104857600 | tf_op jit(solution)/shard_map/reduce/pallas_call | solution.py:1337
  344.5 1.4 copy-done.13
  345.9 9.0 %experts.7 = (bf16[4,576,512]{2,1,0:T(8,128)(2,1)}, bf16[8,2,64,768]{3,2,1,0:T(8,128)(2,1)S(1)}) custom-call(bf16[8,2,64,768]{3,2,1,0:T(8,128)(2,1)S(1)} %copy-done.7, bf16[4,576,512]{2,1,0:T(8,128)(2,1)} %bitcast.61, f32[512,768]{1,0:T(8,128)S(1)} %copy-done.13, f32[512,768]{1,0:T(8,128)} %copy-done.14), custom_call_target="tpu_custom_call" | custom-call | flops 3623878656 | bytes 16777216 | tf_op jit(solution)/shard_map/experts/pallas_call | solution.py:1230
  356.1 32.5 %all_to_all.11.back_ref = bf16[8,2,64,768]{3,2,1,0:T(8,128)(2,1)} all-to-all(bf16[8,2,64,768]{3,2,1,0:T(8,128)(2,1)} %copy-done.8), channel_id=1, replica_groups=mesh['dp'=4,'expert'=8] {'expert'}, dimensions={0} | all-to-all | bytes 3145728 | tf_op jit(solution)/shard_map/all_to_all | solution.py:1605
  388.6 23.3 %after.1 = (bf16[256,768]{1,0:T(8,128)(2,1)}, f32[256,768]{1,0:T(8,128)}, f32[256,12]{1,0:T(8,128)}, bf16[8,768,384]{2,1,0:T(8,128)(2,1)}, f32[32,768]{1,0:T(8,128)}) custom-call(bf16[256,768]{1,0:T(8,128)(2,1)} %input_ref.3, f32[256,12]{1,0:T(8,128)} %copy.40.prev_ref, s32[256,2]{1,0:T(8,128)} %copy.41.routes_ref, s32[256,1]{1,0:T(8,128)} %copy.42.column_ref, ...), custom_call_target="tpu_custom_call" | custom-call | flops 2415919104 | bytes 62914560 | tf_op jit(solution)/shard_map/after/pallas_call | solution.py:941
  411.8 1.5 convert_element_type.22
  413.4 1.5 reshape.82
  415.8 2.3 copy-done.1
  418.1 50.4 %tail.1 = (bf16[8,192,384]{2,1,0:T(8,128)(2,1)S(1)}, f32[32,256]{1,0:T(8,128)S(1)}) custom-call(bf16[8,4,192,384]{3,2,1,0:T(8,128)(2,1)S(1)} %bitcast.45, bf16[4,32,256]{2,1,0:T(8,128)(2,1)S(1)} %pad.9.small_ref), custom_call_target="tpu_custom_call" | custom-call | bytes 125829120 | tf_op jit(solution)/shard_map/tail/pallas_call | solution.py:1496
  472.3 1.6 copy.48
  478.2 2.3 slice_bitcast_fusion
  (109 shorter events, 23.1 us)
Async XLA Ops:
  7.2 107.3 %all-gather.11.cloned.1.call-start = ((), (), s32[]{:S(2)}) async-start(), calls=%async_computation.6 | async-start | bytes 2949120 | tf_op jit(solution)/shard_map/all_gather | solution.py:1567
  9.9 193.2 %all-gather.9.cloned.1.call-start = ((), (), s32[]{:S(2)}) async-start(), calls=%async_computation.5 | async-start | bytes 2949120 | tf_op jit(solution)/shard_map/all_gather | solution.py:1567
  10.9 279.1 %all-gather.7.cloned.1.call-start = ((), (), s32[]{:S(2)}) async-start(), calls=%async_computation.4 | async-start | bytes 2949120 | tf_op jit(solution)/shard_map/all_gather | solution.py:1567
  10.9 2.0 copy-start.27
  11.0 2.0 copy-start.23
  11.0 2.0 copy-start.26
  11.9 331.2 %all-gather.5.cloned.1.call-start = ((), (), s32[]{:S(2)}) async-start(), calls=%async_computation.3 | async-start | bytes 2949120 | tf_op jit(solution)/shard_map/all_gather | solution.py:1567
  12.8 463.8 %reduce-scatter.2.cloned.1.call-start = ((), (), s32[]{:S(2)}) async-start(), calls=%async_computation.7 | async-start | bytes 2949120 | tf_op jit(solution)/shard_map/reduce_scatter | solution.py:1599
  13.8 59.6 %copy-start.21 = (f32[256,12]{0,1:T(8,128)S(1)}, f32[256,12]{0,1:T(8,128)}, u32[]{:S(2)}) copy-start(f32[256,12]{0,1:T(8,128)} %param.16) | copy-start | bytes 36868
  13.8 60.4 %copy-start.24 = (s32[256,2]{0,1:T(2,128)S(1)}, s32[256,2]{0,1:T(2,128)}, u32[]{:S(2)}) copy-start(s32[256,2]{0,1:T(2,128)} %param.18) | copy-start | bytes 6148
  13.8 61.2 %copy-start.22 = (s32[1,256]{1,0:T(1,128)S(1)}, s32[1,256]{1,0:T(1,128)}, u32[]{:S(2)}) copy-start(s32[1,256]{1,0:T(1,128)} %row_ref.3) | copy-start | bytes 3076
  68.4 2.2 copy-start
  114.4 88.7 %copy-start.5 = (bf16[8,2,64,768]{3,2,1,0:T(8,128)(2,1)}, bf16[8,2,64,768]{3,2,1,0:T(8,128)(2,1)S(1)}, u32[]{:S(2)}) copy-start(bf16[8,2,64,768]{3,2,1,0:T(8,128)(2,1)S(1)} %all_to_all.10.refs_0_) | copy-start | bytes 4718596
  123.8 79.3 %copy-start.15 = (f32[512,768]{1,0:T(8,128)}, f32[512,768]{1,0:T(8,128)S(1)}, u32[]{:S(2)}) copy-start(f32[512,768]{1,0:T(8,128)S(1)} %get-tuple-element.61.refs_2_) | copy-start | bytes 4718596
  123.8 79.3 %copy-start.16 = (f32[512,768]{1,0:T(8,128)}, f32[512,768]{1,0:T(8,128)S(1)}, u32[]{:S(2)}) copy-start(f32[512,768]{1,0:T(8,128)S(1)} %get-tuple-element.62.refs_3_) | copy-start | bytes 4718596
  123.8 2.8 copy-start.4
  212.9 77.1 %copy-start.10 = (f32[512,768]{1,0:T(8,128)}, f32[512,768]{1,0:T(8,128)S(1)}, u32[]{:S(2)}) copy-start(f32[512,768]{1,0:T(8,128)S(1)} %get-tuple-element.66.refs_2_) | copy-start | bytes 4718596
  212.9 77.1 %copy-start.11 = (f32[512,768]{1,0:T(8,128)}, f32[512,768]{1,0:T(8,128)S(1)}, u32[]{:S(2)}) copy-start(f32[512,768]{1,0:T(8,128)S(1)} %get-tuple-element.67.refs_3_) | copy-start | bytes 4718596
  212.9 2.9 copy-start.2
  301.2 41.9 %copy-start.12 = (f32[512,768]{1,0:T(8,128)}, f32[512,768]{1,0:T(8,128)S(1)}, u32[]{:S(2)}) copy-start(f32[512,768]{1,0:T(8,128)S(1)} %get-tuple-element.71.refs_2_) | copy-start | bytes 4718596
  301.2 41.9 %copy-start.14 = (f32[512,768]{1,0:T(8,128)}, f32[512,768]{1,0:T(8,128)S(1)}, u32[]{:S(2)}) copy-start(f32[512,768]{1,0:T(8,128)S(1)} %get-tuple-element.72.refs_3_) | copy-start | bytes 4718596
  301.2 2.8 copy-start.3
  415.8 2.3 copy-start.1
  468.5 2.6 copy-start.9
  (10 other events, 16.1 us)
Sparse Core Ops, SparseCore 0:
  10.1 61.7 all-gather.10
  73.5 53.2 all-gather.8
  128.9 76.5 all-gather.6
  207.5 80.4 all-gather.4
  356.2 56.2 reduce-scatter.1

commit v3 on v2

--- a/solution.py
+++ b/solution.py
@@ -536,9 +536,7 @@
 SUM_GAIN_TWO = 15
 SUM_VECTORS = 16
 SUM_ROWS = 32
-SLICES = 4
 LANES = 128
-VMEM_BYTES = 60 * 1024 * 1024
 
 
 def dot_nn(left, right):
@@ -926,7 +924,7 @@
             pltpu.VMEM((tokens, 3 * features), jnp.float32),
             pltpu.VMEM((tokens, tokens), jnp.float32),
         ],
-        compiler_params=pltpu.CompilerParams(vmem_limit_bytes=VMEM_BYTES),
+        compiler_params=pltpu.CompilerParams(vmem_limit_bytes=32 << 20),
         cost_estimate=pl.CostEstimate(
             flops=2 * tokens * features * 4 * features,
             transcendentals=HEADS * tokens * tokens,
@@ -952,7 +950,7 @@
             pltpu.VMEM((tokens, 3 * features), jnp.bfloat16),
             pltpu.VMEM((tokens, tokens), jnp.float32),
         ],
-        compiler_params=pltpu.CompilerParams(vmem_limit_bytes=VMEM_BYTES),
+        compiler_params=pltpu.CompilerParams(vmem_limit_bytes=40 << 20),
         cost_estimate=pl.CostEstimate(
             flops=4 * tokens * features * 4 * features,
             transcendentals=HEADS * tokens * tokens,
@@ -1231,7 +1229,7 @@
         body,
         out_shape=out_shape,
         scratch_shapes=scratch,
-        compiler_params=pltpu.CompilerParams(vmem_limit_bytes=48 << 20),
+        compiler_params=pltpu.CompilerParams(vmem_limit_bytes=40 << 20),
         cost_estimate=pl.CostEstimate(
             flops=18 * rows * features * width,
             transcendentals=rows * width,
@@ -1241,8 +1239,22 @@
     )(received, weights, *sums)
 
 
-def reduce_kernel(
-    grad_ref, own_ref, risen, fallen, rise_send, rise_recv, fall_send, fall_recv
+def exchange_kernel(
+    grad_ref,
+    weight_ref,
+    own_ref,
+    full_ref,
+    risen,
+    fallen,
+    rise_send,
+    rise_recv,
+    fall_send,
+    fall_recv,
+    up_send,
+    up_recv,
+    down_send,
+    down_recv,
+    local_sem,
 ):
     depth, rows, _ = grad_ref.shape
     pieces = rise_send.shape[1]
@@ -1267,6 +1279,9 @@
         def _():
             pl.semaphore_wait(barrier, count)
 
+    local = pltpu.make_async_copy(weight_ref, full_ref.at[place], local_sem)
+    local.start()
+
     def moved(source, held, owner, piece, send, recv, device):
         at = pl.ds(piece * part, part)
         return copy_to(
@@ -1277,6 +1292,33 @@
             device,
         )
 
+    def given(origin, piece, send, recv, device, source=None):
+        at = pl.ds(piece * part, part)
+        here = full_ref.at[origin, at]
+        return copy_to(
+            here if source is None else source.at[at],
+            here,
+            send.at[origin, piece],
+            recv.at[origin, piece],
+            device,
+        )
+
+    def hand_on(step, piece, up):
+        origin = place - step if up else place + step
+        ways = (up_send, up_recv, above) if up else (down_send, down_recv, below)
+        if up:
+            there = (place < top) & (origin >= 0)
+        else:
+            there = (place > 0) & (origin <= top)
+
+        @pl.when(there)
+        def _():
+            if step == 0:
+                given(origin, piece, *ways, weight_ref).start()
+            else:
+                given(origin, piece, *ways).wait_recv()
+                given(origin, piece, *ways).start()
+
     def pass_on(held, owner, piece, send, recv, device, leads, follows):
         at = slice(piece * part, (piece + 1) * part)
 
@@ -1295,6 +1337,8 @@
     for step in range(top):
         rise, fall = top - step, step
         for piece in range(pieces):
+            hand_on(step, piece, True)
+            hand_on(step, piece, False)
             pass_on(
                 risen, rise, piece, rise_send, rise_recv, above,
                 (place == 0) & (place < rise), (place > 0) & (place < rise),
@@ -1317,6 +1361,18 @@
             moved(risen, risen, place, piece, rise_send, rise_recv, below).wait_recv()
             own_ref[at, :] += risen[place, at].astype(jnp.float32)
 
+    for origin in range(depth):
+        for piece in range(pieces):
+
+            @pl.when((place == top) & (origin < top))
+            def _():
+                given(origin, piece, up_send, up_recv, below).wait_recv()
+
+            @pl.when((place == 0) & (origin > 0))
+            def _():
+                given(origin, piece, down_send, down_recv, above).wait_recv()
+
+    local.wait()
     for step in range(top):
         rise, fall = top - step, step
         for piece in range(pieces):
@@ -1329,23 +1385,36 @@
             def _():
                 moved(fallen, fallen, fall, piece, fall_send, fall_recv, below).wait_send()
 
-
-def reduce_line(grads):
+            @pl.when((place < top) & (place >= step))
+            def _():
+                given(place - step, piece, up_send, up_recv, above).wait_send()
+
+            @pl.when((place > 0) & (place + step <= top))
+            def _():
+                given(place + step, piece, down_send, down_recv, below).wait_send()
+
+
+def exchange(grads, weights):
     depth, rows, width = grads.shape
-    pieces = 3
+    pieces = 6
     dma = pltpu.SemaphoreType.DMA
     return pl.pallas_call(
-        reduce_kernel,
-        out_shape=jax.ShapeDtypeStruct((rows, width), jnp.float32),
-        in_specs=[pl.BlockSpec(memory_space=pltpu.VMEM)],
-        out_specs=pl.BlockSpec(memory_space=pltpu.VMEM),
-        scratch_shapes=[pltpu.VMEM(grads.shape, grads.dtype)] * 2 + [dma((depth, pieces))] * 4,
+        exchange_kernel,
+        out_shape=(
+            jax.ShapeDtypeStruct((rows, width), jnp.float32),
+            jax.ShapeDtypeStruct((depth,) + weights.shape, weights.dtype),
+        ),
+        in_specs=[pl.BlockSpec(memory_space=pltpu.VMEM)] * 2,
+        out_specs=[pl.BlockSpec(memory_space=pltpu.VMEM)] * 2,
+        scratch_shapes=[pltpu.VMEM(grads.shape, grads.dtype)] * 2
+        + [dma((depth, pieces))] * 8
+        + [dma],
         compiler_params=pltpu.CompilerParams(
-            collective_id=2, has_side_effects=True, vmem_limit_bytes=24 << 20
+            collective_id=2, has_side_effects=True, vmem_limit_bytes=32 << 20
         ),
-        cost_estimate=pl.CostEstimate(flops=0, transcendentals=0, bytes_accessed=100 << 20),
-        name="reduce",
-    )(grads)
+        cost_estimate=pl.CostEstimate(flops=0, transcendentals=0, bytes_accessed=250 << 20),
+        name="exchange",
+    )(grads, weights)
 
 
 def tail_kernel(
@@ -1556,15 +1625,12 @@
     own_rows = qkv_weight.shape[0]
     part_width = 4 * features // parts
     mine = lax.axis_index("expert")
-    hidden_units = exp_gate.shape[1]
-    width = hidden_units // SLICES
-    gathered = []
-    for step in range(SLICES):
-        columns = slice(step * width, (step + 1) * width)
-        triple = jnp.concatenate(
-            [exp_gate[:, columns], exp_up[:, columns], exp_down[columns].T], axis=0
-        )
-        gathered.append(lax.all_gather(triple, "dp", axis=0, tiled=True))
+    width = exp_gate.shape[1] // 2
+    halves = [
+        jnp.concatenate([exp_gate[:, half], exp_up[:, half], exp_down[half].T], axis=0)
+        for half in (slice(0, width), slice(width, 2 * width))
+    ]
+    first_half = lax.all_gather(halves[0], "dp", axis=0, tiled=True)
     both = jnp.concatenate([qkv_weight, out_weight], axis=1)
     piece = lax.dynamic_slice_in_dim(both, mine * part_width, part_width, axis=1)
     pack = pack_small(router, const_w, gain_attn, gain_moe, const_v)
@@ -1588,20 +1654,11 @@
     )
     *saved, rows = run_before(common, parts, part_width)
     received = lax.all_to_all(rows, "expert", split_axis=0, concat_axis=0, tiled=True)
-    sums = ()
-    owned = []
-    for step in range(SLICES):
-        last = step == SLICES - 1
-        triple = gathered[step].reshape(depth, 3 * own_rows, width)
-        grads, *sums = run_slice(received, triple, tuple(sums), last)
-        if last:
-            back = sums[0]
-            share = lax.psum_scatter(grads, "dp", scatter_dimension=0, tiled=False)
-            owned.append(share.astype(jnp.float32))
-        else:
-            share = reduce_line(grads)
-            *sums, share = lax.optimization_barrier((*sums, share))
-            owned.append(share)
+    first_half = first_half.reshape(depth, 3 * own_rows, width)
+    grads, *sums = run_slice(received, first_half, (), False)
+    first_own, second_half = exchange(grads, halves[1])
+    grads, back = run_slice(received, second_half, tuple(sums), True)
+    second_own = lax.psum_scatter(grads, "dp", scatter_dimension=0, tiled=False)
     returned = lax.all_to_all(back, "expert", split_axis=0, concat_axis=0, tiled=True)
     result, grad_input, grad_prev, grad_weights, grad_small = run_after(
         common + tuple(saved) + (returned,), parts, part_width
@@ -1618,7 +1675,7 @@
     own_small = own_small[:, :own_rows]
     grad_even = own_small[SUM_EVEN : SUM_EVEN + NC]
     grad_const = jnp.stack([grad_even, -grad_even], axis=1).reshape(2 * NC, -1).T
-    owned = jnp.concatenate(owned, axis=1)
+    owned = jnp.concatenate([first_own, second_own.astype(jnp.float32)], axis=1)
     return (
         result,
         grad_input,

time: 489 us -> 403 us (0.82)
  Pallas kernels: 371 us -> 292 us
  blocking collectives: 56.2 us -> 33.9 us
  waiting for transfers between devices: 0.15 us -> 16.7 us
    pallas_call x3 -> x1, Pallas kernels: 190 us -> 125 us  [exchange(): pl.pallas_call(exchange_kernel, out_shape=(jax.ShapeDtypeStruct((rows, wi...]
    all_to_all x1 -> x0, blocking collectives: 23.8 us -> none  [local_fast(): lax.all_to_all(rows, 'expert', split_axis=0, concat_axis=0, tiled=True)]
    all_to_all x0 -> x1, waiting for transfers between devices: none -> 16.4 us  [local_fast(): lax.all_to_all(rows, 'expert', split_axis=0, concat_axis=0, tiled=True)]
    pallas_call x4 -> x2, Pallas kernels: 37.9 us -> 25.6 us  [run_slice(): pl.pallas_call(body, out_shape=out_shape, scratch_shapes=scratch, compile...]
    pallas_call x1, Pallas kernels: 50.4 us -> 56.3 us  [reduce_tail(): pl.pallas_call(tail_kernel, out_shape=(jax.ShapeDtypeStruct((parts, rows,...]
    unnamed x61 -> x109, local copies, waits for them, and re-layouts: 21.9 us -> 24.6 us
  transfers between devices with their start and end apart: 5 -> 3, of which waited for: 0 -> 2; matrix products, arithmetic and copies ran while one was open for 4% -> 2% of each run, Pallas kernels for 74% -> 35%
where the time goes in v3:
time: 403 us; the launch traced here: 402 us
  Pallas kernels  292 us (72%)
  blocking collectives  33.9 us (8%)
  local copies, waits for them, and re-layouts  33.3 us (8%)
  waiting for transfers between devices  16.7 us (4%)
  between operations  14.7 us (4%)
  other arithmetic  7.09 us (2%)
  starting transfers between devices  4.15 us (1%)
    pallas_call x1, Pallas kernels, exchange(): pl.pallas_call(exchange_kernel, out_shape=(jax.ShapeDtypeStruct((rows, wi...  125 us
    pallas_call x1, Pallas kernels, reduce_tail(): pl.pallas_call(tail_kernel, out_shape=(jax.ShapeDtypeStruct((parts, rows,...  56.3 us
    pallas_call x1, Pallas kernels, gather_start(): pl.pallas_call(start_kernel, out_shape=(jax.ShapeDtypeStruct((parts, dept...  52.5 us
    all_to_all x1, blocking collectives, local_fast(): lax.all_to_all(back, 'expert', split_axis=0, concat_axis=0, tiled=True)  33.9 us
    pallas_call x2, Pallas kernels, run_slice(): pl.pallas_call(body, out_shape=out_shape, scratch_shapes=scratch, compile...  25.6 us
    unnamed x109, local copies, waits for them, and re-layouts  24.6 us
    pallas_call x1, Pallas kernels, run_after(): pl.pallas_call(after_kernel, out_shape=(jax.ShapeDtypeStruct((tokens, fea...  20.5 us
    all_to_all x1, waiting for transfers between devices, local_fast(): lax.all_to_all(rows, 'expert', split_axis=0, concat_axis=0, tiled=True)  16.4 us
  transfers between devices with their start and end apart: 3, of which 2 were waited for; matrix products, arithmetic and copies ran while one was open for 2% of the time, Pallas kernels for 35%

profile of v3, /device:TPU:9, one launch (start us, length us, event | category | flops | bytes accessed | tf_op | source)
XLA Modules:
  0.0 402.3 jit_solution(5484436110064202148)
XLA Ops:
  7.2 2.1 slice_bitcast_fusion
  10.2 1.1 pad_maximum_fusion.1
  13.3 52.5 %start.1 = (bf16[8,4,192,384]{3,2,1,0:T(8,128)(2,1)S(1)}, bf16[4,96,256]{2,1,0:T(8,128)(2,1)S(1)}) custom-call(bf16[192,384]{1,0:T(8,128)(2,1)S(1)} %fusion.3.piece_ref, bf16[96,256]{1,0:T(8,128)(2,1)S(1)} %pad.8.pack_ref), custom_call_target="tpu_custom_call" | custom-call | bytes 83886080 | tf_op jit(solution)/shard_map/start/pallas_call | solution.py:1118
  65.8 2.1 copy-done
  68.4 2.4 copy-done.1
  70.8 12.1 %before.1 = (bf16[256,768]{1,0:T(8,128)(2,1)S(1)}, bf16[256,768]{1,0:T(8,128)(2,1)S(1)}, bf16[256,768]{1,0:T(8,128)(2,1)S(1)}, bf16[256,768]{1,0:T(8,128)(2,1)S(...) custom-call(bf16[256,768]{1,0:T(8,128)(2,1)S(1)} %copy-done.5, ...), custom_call_target="tpu_custom_call" | custom-call | flops 1207959552 | bytes 20971520 | tf_op jit(solution)/shard_map/before/pallas_call | solution.py:912
  87.6 4.1 %all-to-all-start = ((bf16[8,2,64,768]{3,2,1,0:T(8,128)(2,1)}), bf16[8,2,64,768]{3,2,1,0:T(8,128)(2,1)S(1)}, u32[]{:S(2)}, u32[]{:S(2)}) async-start(bf16[8,2,64,768]{3,2,1,0:T(8,128)(2,1)} %get-tuple-element.44), calls=%async_computation | async-start | bytes 3145728 | tf_op jit(solution)/shard_map/all_to_all | solution.py:1656
  91.7 1.1 pad_maximum_fusion.2.weight_ref
  92.8 16.4 %all-to-all-done.refs_0_ = bf16[8,2,64,768]{3,2,1,0:T(8,128)(2,1)S(1)} async-done(((bf16[8,2,64,768]{3,2,1,0:T(8,128)(2,1)}), bf16[8,2,64,768]{3,2,1,0:T(8,128)(2,1)S(1)}, u32[]{:S(2)}, u32[]{:S(2)}) %all-to-all-start) | async-done | bytes 1572896 | tf_op jit(solution)/shard_map/all_to_all | solution.py:1656
  109.5 2.7 copy-done.39
  112.2 11.6 %experts.2 = (bf16[4,576,1024]{2,1,0:T(8,128)(2,1)S(1)}, f32[512,768]{1,0:T(8,128)S(1)}, f32[512,768]{1,0:T(8,128)S(1)}) custom-call(bf16[8,2,64,768]{3,2,1,0:T(8,128)(2,1)S(1)} %all-to-all-done.refs_0_, bf16[4,576,1024]{2,1,0:T(8,128)(2,1)S(1)} %bitcast.40), custom_call_target="tpu_custom_call" | custom-call | flops 7247757312 | bytes 16777216 | tf_op jit(solution)/shard_map/experts/pallas_call | solution.py:1228
  123.8 125.2 %exchange.1 = (f32[576,1024]{1,0:T(8,128)S(1)}, bf16[4,576,1024]{2,1,0:T(8,128)(2,1)S(1)}) custom-call(bf16[4,576,1024]{2,1,0:T(8,128)(2,1)S(1)} %get-tuple-element.45.grad_ref, bf16[576,1024]{1,0:T(8,128)(2,1)S(1)} %pad_maximum_fusion.2.weight_ref), custom_call_target="tpu_custom_call" | custom-call | bytes 262144000 | tf_op jit(solution)/shard_map/exchange/pallas_call | solution.py:1401
  249.0 2.2 copy-done.40
  251.2 14.0 %experts.3 = (bf16[4,576,1024]{2,1,0:T(8,128)(2,1)S(1)}, bf16[8,2,64,768]{3,2,1,0:T(8,128)(2,1)S(1)}) custom-call(bf16[8,2,64,768]{3,2,1,0:T(8,128)(2,1)S(1)} %copy-done.10, bf16[4,576,1024]{2,1,0:T(8,128)(2,1)} %copy-done.40, f32[512,768]{1,0:T(8,128)S(1)} %get-tuple-element.47.refs_2_, f32[512,768]{1,0:T(8,128)S(1)} %get-tuple-element.48.refs_3_), custom_call_target="tpu_custom_call" | custom-call | flops 7247757312 | bytes 16777216 | tf_op jit(solution)/shard_map/experts/pallas_call | solution.py:1228
  265.2 2.2 copy-done.2
  267.4 1.1 copy-done.11
  268.7 33.9 %all_to_all.10.back_ref = bf16[8,2,64,768]{3,2,1,0:T(8,128)(2,1)S(1)} all-to-all(bf16[8,2,64,768]{3,2,1,0:T(8,128)(2,1)} %copy-done.11), channel_id=1, replica_groups=mesh['dp'=4,'expert'=8] {'expert'}, dimensions={0} | all-to-all | bytes 3145728 | tf_op jit(solution)/shard_map/all_to_all | solution.py:1662
  303.7 20.5 %after.1 = (bf16[256,768]{1,0:T(8,128)(2,1)}, f32[256,768]{1,0:T(8,128)}, f32[256,12]{1,0:T(8,128)S(1)}, bf16[8,768,384]{2,1,0:T(8,128)(2,1)S(1)}, f32[32,768]{1,0:T(8,128)S(1)}) custom-call(bf16[256,768]{1,0:T(8,128)(2,1)S(1)} %copy-done.6, f32[256,12]{1,0:T(8,128)S(1)} %copy-done.17, s32[256,2]{1,0:T(8,128)S(1)} %copy-done.19, s32[256,1]{1,0:T(8,128)S(1)} %copy-done.21, ...), custom_call_target="tpu_custom_call" | custom-call | flops 2415919104 | bytes 62914560 | tf_op jit(solution)/shard_map/after/pallas_call | solution.py:939
  324.3 2.2 copy-done.3
  327.3 2.4 copy-done.4
  329.6 56.3 %tail.1 = (bf16[8,192,384]{2,1,0:T(8,128)(2,1)S(1)}, f32[32,256]{1,0:T(8,128)S(1)}) custom-call(bf16[8,4,192,384]{3,2,1,0:T(8,128)(2,1)S(1)} %bitcast.38, bf16[4,32,256]{2,1,0:T(8,128)(2,1)S(1)} %pad.9.small_ref), custom_call_target="tpu_custom_call" | custom-call | bytes 125829120 | tf_op jit(solution)/shard_map/tail/pallas_call | solution.py:1565
  387.3 1.3 slice.82
  391.7 1.5 bitcast_convert_fusion
  393.2 2.3 fusion.2
  (142 shorter events, 14.1 us)
Async XLA Ops:
  7.2 102.3 %all-gather.2.cloned.1.call-start = ((), (), s32[]{:S(2)}) async-start(), calls=%async_computation.3 | async-start | bytes 5898240 | tf_op jit(solution)/shard_map/all_gather | solution.py:1633
  12.6 55.8 %copy-start.14 = (f32[256,128]{1,0:T(8,128)}, f32[256,128]{1,0:T(8,128)S(1)}, u32[]{:S(2)}) copy-start(f32[256,128]{1,0:T(8,128)S(1)} %copy.43.cos_ref) | copy-start | bytes 393220
  12.7 55.7 %copy-start.16 = (f32[256,12]{1,0:T(8,128)}, f32[256,12]{1,0:T(8,128)S(1)}, u32[]{:S(2)}) copy-start(f32[256,12]{1,0:T(8,128)S(1)} %copy.40.prev_ref) | copy-start | bytes 36868
  12.9 55.5 %copy-start.18 = (s32[256,2]{1,0:T(8,128)}, s32[256,2]{1,0:T(8,128)S(1)}, u32[]{:S(2)}) copy-start(s32[256,2]{1,0:T(8,128)S(1)} %copy.41.routes_ref) | copy-start | bytes 6148
  13.0 69.9 %copy-start.20 = (s32[256,1]{1,0:T(8,128)}, s32[256,1]{1,0:T(8,128)S(1)}, u32[]{:S(2)}) copy-start(s32[256,1]{1,0:T(8,128)S(1)} %copy.42.column_ref) | copy-start | bytes 3076
  13.0 55.4 %copy-start.5 = (bf16[256,768]{1,0:T(8,128)(2,1)S(1)}, bf16[256,768]{1,0:T(8,128)(2,1)}, u32[]{:S(2)}) copy-start(bf16[256,768]{1,0:T(8,128)(2,1)} %input_ref.3) | copy-start | bytes 1179652
  13.0 55.4 %copy-start.7 = (bf16[256,768]{1,0:T(8,128)(2,1)S(1)}, bf16[256,768]{1,0:T(8,128)(2,1)}, u32[]{:S(2)}) copy-start(bf16[256,768]{1,0:T(8,128)(2,1)} %grad_ref.3) | copy-start | bytes 1179652
  13.2 69.8 %copy-start.22 = (f32[256,128]{1,0:T(8,128)}, f32[256,128]{1,0:T(8,128)S(1)}, u32[]{:S(2)}) copy-start(f32[256,128]{1,0:T(8,128)S(1)} %copy.44.sin_ref) | copy-start | bytes 393220
  87.6 21.7 %all-to-all-start = ((bf16[8,2,64,768]{3,2,1,0:T(8,128)(2,1)}), bf16[8,2,64,768]{3,2,1,0:T(8,128)(2,1)S(1)}, u32[]{:S(2)}, u32[]{:S(2)}) async-start(bf16[8,2,64,768]{3,2,1,0:T(8,128)(2,1)} %get-tuple-element.44), calls=%async_computation | async-start | bytes 3145728 | tf_op jit(solution)/shard_map/all_to_all | solution.py:1656
  91.7 300.0 %reduce-scatter.2.cloned.1.call-start = ((), (), s32[]{:S(2)}) async-start(), calls=%async_computation.4 | async-start | bytes 5898240 | tf_op jit(solution)/shard_map/reduce_scatter | solution.py:1661
  123.8 127.4 %copy-start.10 = (bf16[8,2,64,768]{3,2,1,0:T(8,128)(2,1)S(1)}, bf16[8,2,64,768]{3,2,1,0:T(8,128)(2,1)}, u32[]{:S(2)}) copy-start(bf16[8,2,64,768]{3,2,1,0:T(8,128)(2,1)} %copy-done.9) | copy-start | bytes 4718596
  268.6 34.1 %copy-start.29 = (bf16[256,768]{1,0:T(8,128)(2,1)S(1)}, bf16[256,768]{1,0:T(8,128)(2,1)}, u32[]{:S(2)}) copy-start(bf16[256,768]{1,0:T(8,128)(2,1)} %copy-done.28) | copy-start | bytes 1179652
  268.6 34.1 %copy-start.31 = (bf16[256,768]{1,0:T(8,128)(2,1)S(1)}, bf16[256,768]{1,0:T(8,128)(2,1)}, u32[]{:S(2)}) copy-start(bf16[256,768]{1,0:T(8,128)(2,1)} %copy-done.30) | copy-start | bytes 1179652
  268.6 34.1 %copy-start.33 = (bf16[256,768]{1,0:T(8,128)(2,1)S(1)}, bf16[256,768]{1,0:T(8,128)(2,1)}, u32[]{:S(2)}) copy-start(bf16[256,768]{1,0:T(8,128)(2,1)} %copy-done.32) | copy-start | bytes 1179652
  268.6 34.1 %copy-start.6 = (bf16[256,768]{1,0:T(8,128)(2,1)S(1)}, bf16[256,768]{1,0:T(8,128)(2,1)}, u32[]{:S(2)}) copy-start(bf16[256,768]{1,0:T(8,128)(2,1)} %input_ref.3) | copy-start | bytes 1179652
  268.6 34.1 %copy-start.8 = (bf16[256,768]{1,0:T(8,128)(2,1)S(1)}, bf16[256,768]{1,0:T(8,128)(2,1)}, u32[]{:S(2)}) copy-start(bf16[256,768]{1,0:T(8,128)(2,1)} %grad_ref.3) | copy-start | bytes 1179652
  268.6 34.1 %copy-start.13 = (bf16[96,768]{1,0:T(8,128)(2,1)S(1)}, bf16[96,768]{1,0:T(8,128)(2,1)}, u32[]{:S(2)}) copy-start(bf16[96,768]{1,0:T(8,128)(2,1)} %copy-done.12) | copy-start | bytes 442372
  268.6 34.1 %copy-start.15 = (f32[256,128]{1,0:T(8,128)S(1)}, f32[256,128]{1,0:T(8,128)}, u32[]{:S(2)}) copy-start(f32[256,128]{1,0:T(8,128)} %copy-done.14) | copy-start | bytes 393220
  268.6 34.1 %copy-start.17 = (f32[256,12]{1,0:T(8,128)S(1)}, f32[256,12]{1,0:T(8,128)}, u32[]{:S(2)}) copy-start(f32[256,12]{1,0:T(8,128)} %copy-done.16) | copy-start | bytes 36868
  268.6 34.1 %copy-start.19 = (s32[256,2]{1,0:T(8,128)S(1)}, s32[256,2]{1,0:T(8,128)}, u32[]{:S(2)}) copy-start(s32[256,2]{1,0:T(8,128)} %copy-done.18) | copy-start | bytes 6148
  268.7 34.1 %copy-start.21 = (s32[256,1]{1,0:T(8,128)S(1)}, s32[256,1]{1,0:T(8,128)}, u32[]{:S(2)}) copy-start(s32[256,1]{1,0:T(8,128)} %copy-done.20) | copy-start | bytes 3076
  268.7 34.1 %copy-start.23 = (f32[256,128]{1,0:T(8,128)S(1)}, f32[256,128]{1,0:T(8,128)}, u32[]{:S(2)}) copy-start(f32[256,128]{1,0:T(8,128)} %copy-done.22) | copy-start | bytes 393220
  268.7 34.1 %copy-start.25 = (f32[256,768]{1,0:T(8,128)S(1)}, f32[256,768]{1,0:T(8,128)}, u32[]{:S(2)}) copy-start(f32[256,768]{1,0:T(8,128)} %copy-done.24) | copy-start | bytes 2359300
  268.7 34.1 %copy-start.27 = (bf16[256,768]{1,0:T(8,128)(2,1)S(1)}, bf16[256,768]{1,0:T(8,128)(2,1)}, u32[]{:S(2)}) copy-start(bf16[256,768]{1,0:T(8,128)(2,1)} %copy-done.26) | copy-start | bytes 1179652
  (32 other events, 76.3 us)
Sparse Core Ops, SparseCore 0:
  11.5 97.9 all-gather.1
  268.7 102.4 reduce-scatter.1

commit v4 on v3

--- a/solution.py
+++ b/solution.py
@@ -924,7 +924,7 @@
             pltpu.VMEM((tokens, 3 * features), jnp.float32),
             pltpu.VMEM((tokens, tokens), jnp.float32),
         ],
-        compiler_params=pltpu.CompilerParams(vmem_limit_bytes=32 << 20),
+        compiler_params=pltpu.CompilerParams(vmem_limit_bytes=60 << 20),
         cost_estimate=pl.CostEstimate(
             flops=2 * tokens * features * 4 * features,
             transcendentals=HEADS * tokens * tokens,
@@ -950,7 +950,7 @@
             pltpu.VMEM((tokens, 3 * features), jnp.bfloat16),
             pltpu.VMEM((tokens, tokens), jnp.float32),
         ],
-        compiler_params=pltpu.CompilerParams(vmem_limit_bytes=40 << 20),
+        compiler_params=pltpu.CompilerParams(vmem_limit_bytes=60 << 20),
         cost_estimate=pl.CostEstimate(
             flops=4 * tokens * features * 4 * features,
             transcendentals=HEADS * tokens * tokens,
@@ -1122,7 +1122,7 @@
             jax.ShapeDtypeStruct((depth,) + pack.shape, pack.dtype),
         ),
         in_specs=[pl.BlockSpec(memory_space=pltpu.VMEM)] * 2,
-        out_specs=[pl.BlockSpec(memory_space=pltpu.VMEM)] * 2,
+        out_specs=[pl.BlockSpec(memory_space=pl.ANY)] * 2,
         scratch_shapes=[
             dma((depth - 1,)),
             dma((depth - 1,)),
@@ -1136,7 +1136,7 @@
             dma,
         ],
         compiler_params=pltpu.CompilerParams(
-            collective_id=1, has_side_effects=True, vmem_limit_bytes=16 << 20
+            collective_id=1, has_side_effects=True, vmem_limit_bytes=60 << 20
         ),
         cost_estimate=pl.CostEstimate(flops=0, transcendentals=0, bytes_accessed=80 << 20),
         name="start",
@@ -1319,14 +1319,21 @@
                 given(origin, piece, *ways).wait_recv()
                 given(origin, piece, *ways).start()
 
-    def pass_on(held, owner, piece, send, recv, device, leads, follows):
-        at = slice(piece * part, (piece + 1) * part)
-
-        @pl.when(leads)
+    rising = (risen, rise_send, rise_recv, above)
+    falling = (fallen, fall_send, fall_recv, below)
+
+    def lead(there, way, owner, piece):
+        held, send, recv, device = way
+
+        @pl.when(there)
         def _():
             moved(grad_ref, held, owner, piece, send, recv, device).start()
 
-        @pl.when(follows)
+    def follow(there, way, owner, piece):
+        held, send, recv, device = way
+        at = slice(piece * part, (piece + 1) * part)
+
+        @pl.when(there)
         def _():
             moved(held, held, owner, piece, send, recv, device).wait_recv()
             held[owner, at] = (
@@ -1334,19 +1341,32 @@
             ).astype(jnp.bfloat16)
             moved(held, held, owner, piece, send, recv, device).start()
 
-    for step in range(top):
-        rise, fall = top - step, step
-        for piece in range(pieces):
-            hand_on(step, piece, True)
-            hand_on(step, piece, False)
-            pass_on(
-                risen, rise, piece, rise_send, rise_recv, above,
-                (place == 0) & (place < rise), (place > 0) & (place < rise),
-            )
-            pass_on(
-                fallen, fall, piece, fall_send, fall_recv, below,
-                (place == top) & (place > fall), (place < top) & (place > fall),
-            )
+    bottom, lower, upper, peak = (place == spot for spot in range(depth))
+    for step in range(pieces + 1):
+        if step < pieces:
+            lead(bottom, rising, 3, step)
+            lead(peak, falling, 0, step)
+            for piece in (0, 1) if step == 0 else (step + 1,):
+                if piece < pieces:
+                    hand_on(0, piece, True)
+                    hand_on(0, piece, False)
+            follow(lower, rising, 3, step)
+            follow(upper, falling, 0, step)
+        if step > 0:
+            follow(lower, falling, 0, step - 1)
+            follow(upper, rising, 3, step - 1)
+    for step in range(pieces + 1):
+        if step < pieces:
+            for owner in (2, 1):
+                lead(bottom, rising, owner, step)
+                lead(peak, falling, top - owner, step)
+            hand_on(1, step, True)
+            hand_on(1, step, False)
+            follow(lower, rising, 2, step)
+            follow(upper, falling, 1, step)
+        if step > 0:
+            hand_on(2, step - 1, True)
+            hand_on(2, step - 1, False)
     for piece in range(pieces):
         at = slice(piece * part, (piece + 1) * part)
         own_ref[at, :] = grad_ref[place, at].astype(jnp.float32)
@@ -1405,7 +1425,10 @@
             jax.ShapeDtypeStruct((depth,) + weights.shape, weights.dtype),
         ),
         in_specs=[pl.BlockSpec(memory_space=pltpu.VMEM)] * 2,
-        out_specs=[pl.BlockSpec(memory_space=pltpu.VMEM)] * 2,
+        out_specs=[
+            pl.BlockSpec(memory_space=pltpu.VMEM),
+            pl.BlockSpec(memory_space=pl.ANY),
+        ],
         scratch_shapes=[pltpu.VMEM(grads.shape, grads.dtype)] * 2
         + [dma((depth, pieces))] * 8
         + [dma],
@@ -1444,9 +1467,18 @@
     share_recv,
     small_send,
     small_recv,
+    local_sem,
 ):
     place, mine, core, chips, lines = neighbours()
     depth = len(lines)
+    local = [
+        pltpu.make_async_copy(
+            grad_ref.at[chips[chip] + core], pair_sum.at[chip], local_sem.at[chip]
+        )
+        for chip in range(4)
+    ]
+    for copy in local:
+        copy.start()
     partner, plane, line = all_peers(place, core, chips, lines)
     greet([partner] + plane + line)
     high = jnp.float32
@@ -1484,12 +1516,12 @@
         )
     steps = tuple(range(1, depth)) + (0,)
     for chip in order:
+        local[chip].wait()
         arrived(pair_held.at[chip], pair_recv.at[chip])
         for step in steps:
             spot = lines[step]
             pair_sum[chip, spot] = (
-                grad_ref[chips[chip] + core, spot].astype(high)
-                + pair_held[chip, spot].astype(high)
+                pair_sum[chip, spot].astype(high) + pair_held[chip, spot].astype(high)
             ).astype(jnp.bfloat16)
             if chip > 0:
                 send(
@@ -1568,7 +1600,10 @@
             jax.ShapeDtypeStruct((parts, rows, width), low),
             jax.ShapeDtypeStruct(small.shape[1:], jnp.float32),
         ),
-        in_specs=[pl.BlockSpec(memory_space=pltpu.VMEM)] * 2,
+        in_specs=[
+            pl.BlockSpec(memory_space=pl.ANY),
+            pl.BlockSpec(memory_space=pltpu.VMEM),
+        ],
         out_specs=[pl.BlockSpec(memory_space=pltpu.VMEM)] * 2,
         scratch_shapes=[
             pltpu.VMEM((4, depth, rows, width), low),
@@ -1593,9 +1628,10 @@
             dma((4,)),
             dma((3 + depth,)),
             dma((3 + depth,)),
+            dma((4,)),
         ],
         compiler_params=pltpu.CompilerParams(
-            collective_id=3, has_side_effects=True, vmem_limit_bytes=40 << 20
+            collective_id=3, has_side_effects=True, vmem_limit_bytes=60 << 20
         ),
         cost_estimate=pl.CostEstimate(flops=0, transcendentals=0, bytes_accessed=120 << 20),
         name="tail",
@@ -1711,7 +1747,8 @@
         P("dp", "expert"),
         P("expert", "dp"),
     )
-    body = local_fast if mesh.shape["expert"] == EXPERTS else local_general
+    fast = mesh.shape["expert"] == EXPERTS and mesh.shape["dp"] == 4
+    body = local_fast if fast else local_general
     return jax.shard_map(
         body,
         mesh=mesh,

time: 403 us -> 393 us (0.975)
  local copies, waits for them, and re-layouts: 33.3 us -> 22.9 us
  blocking collectives: 33.9 us -> 26.3 us
  Pallas kernels: 292 us -> 297 us
    unnamed x109 -> x43, local copies, waits for them, and re-layouts: 24.6 us -> 10.1 us
    pallas_call x1, Pallas kernels: 125 us -> 115 us  [exchange(): pl.pallas_call(exchange_kernel, out_shape=(jax.ShapeDtypeStruct((rows, wi...]
    all_to_all x1, blocking collectives: 33.9 us -> 26.3 us  [local_fast(): lax.all_to_all(back, 'expert', split_axis=0, concat_axis=0, tiled=True)]
    pallas_call x1, Pallas kernels: 52.5 us -> 57.5 us  [gather_start(): pl.pallas_call(start_kernel, out_shape=(jax.ShapeDtypeStruct((parts, dept...]
    pallas_call x1, Pallas kernels: 56.3 us -> 61.1 us  [reduce_tail(): pl.pallas_call(tail_kernel, out_shape=(jax.ShapeDtypeStruct((parts, rows,...]
  transfers between devices with their start and end apart: 3 -> 3, of which waited for: 2 -> 2; matrix products, arithmetic and copies ran while one was open for 2% -> 5% of each run, Pallas kernels for 35% -> 40%
where the time goes in v4:
time: 393 us; the launch traced here: 392 us
  Pallas kernels  297 us (76%)
  blocking collectives  26.3 us (7%)
  local copies, waits for them, and re-layouts  22.9 us (6%)
  waiting for transfers between devices  17.4 us (4%)
  between operations  14.4 us (4%)
  other arithmetic  9.85 us (3%)
  starting transfers between devices  4.01 us (1%)
    pallas_call x1, Pallas kernels, exchange(): pl.pallas_call(exchange_kernel, out_shape=(jax.ShapeDtypeStruct((rows, wi...  115 us
    pallas_call x1, Pallas kernels, reduce_tail(): pl.pallas_call(tail_kernel, out_shape=(jax.ShapeDtypeStruct((parts, rows,...  61.1 us
    pallas_call x1, Pallas kernels, gather_start(): pl.pallas_call(start_kernel, out_shape=(jax.ShapeDtypeStruct((parts, dept...  57.5 us
    all_to_all x1, blocking collectives, local_fast(): lax.all_to_all(back, 'expert', split_axis=0, concat_axis=0, tiled=True)  26.3 us
    pallas_call x2, Pallas kernels, run_slice(): pl.pallas_call(body, out_shape=out_shape, scratch_shapes=scratch, compile...  25.5 us
    pallas_call x1, Pallas kernels, run_after(): pl.pallas_call(after_kernel, out_shape=(jax.ShapeDtypeStruct((tokens, fea...  23.2 us
    all_to_all x1, waiting for transfers between devices, local_fast(): lax.all_to_all(rows, 'expert', split_axis=0, concat_axis=0, tiled=True)  16.5 us
    pallas_call x1, Pallas kernels, run_before(): pl.pallas_call(before_kernel, out_shape=(low, low, low, low, jax.ShapeDty...  15 us
  transfers between devices with their start and end apart: 3, of which 2 were waited for; matrix products, arithmetic and copies ran while one was open for 5% of the time, Pallas kernels for 40%

profile of v4, /device:TPU:9, one launch (start us, length us, event | category | flops | bytes accessed | tf_op | source)
XLA Modules:
  0.0 392.1 jit_solution(10458517872442141695)
XLA Ops:
  7.2 2.0 slice_bitcast_fusion
  9.5 1.1 pad_maximum_fusion.1
  17.0 57.5 %start.1 = (bf16[8,4,192,384]{3,2,1,0:T(8,128)(2,1)}, bf16[4,96,256]{2,1,0:T(8,128)(2,1)}) custom-call(bf16[192,384]{1,0:T(8,128)(2,1)} %fusion.3.piece_ref, bf16[96,256]{1,0:T(8,128)(2,1)} %pad.8.pack_ref), custom_call_target="tpu_custom_call" | custom-call | bytes 83886080 | tf_op jit(solution)/shard_map/start/pallas_call | solution.py:1118
  74.4 0.9 slice_bitcast_fusion.2
  76.4 15.0 %before.1 = (bf16[256,768]{1,0:T(8,128)(2,1)}, bf16[256,768]{1,0:T(8,128)(2,1)}, bf16[256,768]{1,0:T(8,128)(2,1)}, bf16[256,768]{1,0:T(8,128)(2,1)}, f32[256,768...) custom-call(bf16[256,768]{1,0:T(8,128)(2,1)} %input_ref.3, f32[256,12]{1,0:T(8,128)} %copy.40.prev_ref, ...), custom_call_target="tpu_custom_call" | custom-call | flops 1207959552 | bytes 20971520 | tf_op jit(solution)/shard_map/before/pallas_call | solution.py:912
  91.3 4.0 %all-to-all-start = ((bf16[8,2,64,768]{3,2,1,0:T(8,128)(2,1)}), bf16[8,2,64,768]{3,2,1,0:T(8,128)(2,1)S(1)}, u32[]{:S(2)}, u32[]{:S(2)}) async-start(bf16[8,2,64,768]{3,2,1,0:T(8,128)(2,1)} %get-tuple-element.44), calls=%async_computation | async-start | bytes 3145728 | tf_op jit(solution)/shard_map/all_to_all | solution.py:1692
  95.3 1.1 pad_maximum_fusion.2.weight_ref
  96.4 16.5 %all-to-all-done.refs_0_ = bf16[8,2,64,768]{3,2,1,0:T(8,128)(2,1)S(1)} async-done(((bf16[8,2,64,768]{3,2,1,0:T(8,128)(2,1)}), bf16[8,2,64,768]{3,2,1,0:T(8,128)(2,1)S(1)}, u32[]{:S(2)}, u32[]{:S(2)}) %all-to-all-start) | async-done | bytes 1572896 | tf_op jit(solution)/shard_map/all_to_all | solution.py:1692
  113.7 2.3 copy-done.4
  116.1 11.5 %experts.2 = (bf16[4,576,1024]{2,1,0:T(8,128)(2,1)S(1)}, f32[512,768]{1,0:T(8,128)S(1)}, f32[512,768]{1,0:T(8,128)S(1)}) custom-call(bf16[8,2,64,768]{3,2,1,0:T(8,128)(2,1)S(1)} %all-to-all-done.refs_0_, bf16[4,576,1024]{2,1,0:T(8,128)(2,1)S(1)} %bitcast.36), custom_call_target="tpu_custom_call" | custom-call | flops 7247757312 | bytes 16777216 | tf_op jit(solution)/shard_map/experts/pallas_call | solution.py:1228
  127.6 115.1 %exchange.1 = (f32[576,1024]{1,0:T(8,128)S(1)}, bf16[4,576,1024]{2,1,0:T(8,128)(2,1)S(1)}) custom-call(bf16[4,576,1024]{2,1,0:T(8,128)(2,1)S(1)} %get-tuple-element.45.grad_ref, bf16[576,1024]{1,0:T(8,128)(2,1)S(1)} %pad_maximum_fusion.2.weight_ref), custom_call_target="tpu_custom_call" | custom-call | bytes 262144000 | tf_op jit(solution)/shard_map/exchange/pallas_call | solution.py:1421
  242.7 2.1 copy-done.5
  244.8 14.0 %experts.3 = (bf16[4,576,1024]{2,1,0:T(8,128)(2,1)S(1)}, bf16[8,2,64,768]{3,2,1,0:T(8,128)(2,1)S(1)}) custom-call(bf16[8,2,64,768]{3,2,1,0:T(8,128)(2,1)S(1)} %copy-done.2, bf16[4,576,1024]{2,1,0:T(8,128)(2,1)} %copy-done.5, f32[512,768]{1,0:T(8,128)S(1)} %get-tuple-element.47.refs_2_, f32[512,768]{1,0:T(8,128)S(1)} %get-tuple-element.48.refs_3_), custom_call_target="tpu_custom_call" | custom-call | flops 7247757312 | bytes 16777216 | tf_op jit(solution)/shard_map/experts/pallas_call | solution.py:1228
  258.9 2.1 copy-done
  261.0 1.1 copy-done.3
  262.2 26.3 %all_to_all.10.back_ref = bf16[8,2,64,768]{3,2,1,0:T(8,128)(2,1)} all-to-all(bf16[8,2,64,768]{3,2,1,0:T(8,128)(2,1)} %copy-done.3), channel_id=1, replica_groups=mesh['dp'=4,'expert'=8] {'expert'}, dimensions={0} | all-to-all | bytes 3145728 | tf_op jit(solution)/shard_map/all_to_all | solution.py:1698
  288.4 23.2 %after.1 = (bf16[256,768]{1,0:T(8,128)(2,1)}, f32[256,768]{1,0:T(8,128)}, f32[256,12]{1,0:T(8,128)}, bf16[8,768,384]{2,1,0:T(8,128)(2,1)}, f32[32,768]{1,0:T(8,128)}) custom-call(bf16[256,768]{1,0:T(8,128)(2,1)} %input_ref.3, f32[256,12]{1,0:T(8,128)} %copy.40.prev_ref, s32[256,2]{1,0:T(8,128)} %copy.41.routes_ref, s32[256,1]{1,0:T(8,128)} %copy.42.column_ref, ...), custom_call_target="tpu_custom_call" | custom-call | flops 2415919104 | bytes 62914560 | tf_op jit(solution)/shard_map/after/pallas_call | solution.py:939
  311.7 0.9 convert_element_type.22
  313.3 61.1 %tail.1 = (bf16[8,192,384]{2,1,0:T(8,128)(2,1)}, f32[32,256]{1,0:T(8,128)}) custom-call(bf16[8,4,192,384]{3,2,1,0:T(8,128)(2,1)} %bitcast.41, bf16[4,32,256]{2,1,0:T(8,128)(2,1)} %pad.9.small_ref), custom_call_target="tpu_custom_call" | custom-call | bytes 125829120 | tf_op jit(solution)/shard_map/tail/pallas_call | solution.py:1597
  374.4 1.4 convert_bitcast_fusion
  376.1 0.9 slice.83
  377.0 1.3 slice.82
  381.4 1.5 bitcast_convert_fusion
  383.0 2.3 fusion.2
  (76 shorter events, 12.5 us)
Async XLA Ops:
  7.2 2.1 copy-start.8
  7.2 2.1 copy-start.7
  7.2 106.5 %all-gather.2.cloned.1.call-start = ((), (), s32[]{:S(2)}) async-start(), calls=%async_computation.3 | async-start | bytes 5898240 | tf_op jit(solution)/shard_map/all_gather | solution.py:1669
  9.4 1.2 copy-start.16
  9.4 1.3 copy-start.18
  9.5 1.3 copy-start.19
  9.5 1.3 copy-start.14
  9.5 1.3 copy-start.17
  10.6 2.5 copy-start.11
  10.6 3.3 copy-start.15
  10.6 4.1 %copy-start.13 = (s32[1,256]{1,0:T(1,128)S(1)}, s32[1,256]{1,0:T(1,128)}, u32[]{:S(2)}) copy-start(s32[1,256]{1,0:T(1,128)} %row_ref.3) | copy-start | bytes 3076
  10.6 5.6 %copy-start.6 = (bf16[192,2304]{1,0:T(8,128)(2,1)S(1)}, bf16[192,2304]{1,0:T(8,128)(2,1)}, u32[]{:S(2)}) copy-start(bf16[192,2304]{1,0:T(8,128)(2,1)} %param.21) | copy-start | bytes 2654212
  10.6 5.6 %copy-start.9 = (bf16[192,768]{1,0:T(8,128)(2,1)S(1)}, bf16[192,768]{1,0:T(8,128)(2,1)}, u32[]{:S(2)}) copy-start(bf16[192,768]{1,0:T(8,128)(2,1)} %param.22) | copy-start | bytes 884740
  91.3 21.5 %all-to-all-start = ((bf16[8,2,64,768]{3,2,1,0:T(8,128)(2,1)}), bf16[8,2,64,768]{3,2,1,0:T(8,128)(2,1)S(1)}, u32[]{:S(2)}, u32[]{:S(2)}) async-start(bf16[8,2,64,768]{3,2,1,0:T(8,128)(2,1)} %get-tuple-element.44), calls=%async_computation | async-start | bytes 3145728 | tf_op jit(solution)/shard_map/all_to_all | solution.py:1692
  95.3 286.1 %reduce-scatter.2.cloned.1.call-start = ((), (), s32[]{:S(2)}) async-start(), calls=%async_computation.4 | async-start | bytes 5898240 | tf_op jit(solution)/shard_map/reduce_scatter | solution.py:1697
  112.9 14.7 %copy-start.1 = (bf16[8,2,64,768]{3,2,1,0:T(8,128)(2,1)}, bf16[8,2,64,768]{3,2,1,0:T(8,128)(2,1)S(1)}, u32[]{:S(2)}) copy-start(bf16[8,2,64,768]{3,2,1,0:T(8,128)(2,1)S(1)} %all-to-all-done.refs_0_) | copy-start | bytes 4718596
  113.7 2.3 copy-start.4
  127.6 117.2 %copy-start.2 = (bf16[8,2,64,768]{3,2,1,0:T(8,128)(2,1)S(1)}, bf16[8,2,64,768]{3,2,1,0:T(8,128)(2,1)}, u32[]{:S(2)}) copy-start(bf16[8,2,64,768]{3,2,1,0:T(8,128)(2,1)} %copy-done.1) | copy-start | bytes 4718596
  242.7 2.1 copy-start.5
  258.9 2.1 copy-start
  261.0 1.1 copy-start.3
  377.0 1.3 copy-start.10
  377.0 2.0 copy-start.12
Sparse Core Ops, SparseCore 0:
  10.8 102.9 all-gather.1
  262.3 96.8 reduce-scatter.1

commit v5 on v4

--- a/solution.py
+++ b/solution.py
@@ -1638,6 +1638,49 @@
     )(grads, small)
 
 
+def swap_kernel(rows_ref, out_ref, send, recv, local_sem):
+    place, mine, core, chips, lines = neighbours()
+    sides = (core, 1 - core)
+    others = [(chip, side) for chip in (3, 1, 2, 0) for side in (1, 0) if chip + side > 0]
+    local = pltpu.make_async_copy(rows_ref.at[mine], out_ref.at[mine], local_sem)
+    local.start()
+    greet([(place, chips[chip] + sides[side]) for chip, side in others])
+    copies = []
+    for chip, side in others:
+        target = chips[chip] + sides[side]
+        copy = copy_to(
+            rows_ref.at[target],
+            out_ref.at[mine],
+            send.at[chip, side],
+            recv.at[chip, side],
+            (place, target),
+        )
+        copy.start()
+        copies.append(copy)
+    for chip, side in others:
+        here = out_ref.at[chips[chip] + sides[side]]
+        copy_to(here, here, local_sem, recv.at[chip, side], (place, mine)).wait_recv()
+    local.wait()
+    for copy in copies:
+        copy.wait_send()
+
+
+def swap_rows(rows):
+    dma = pltpu.SemaphoreType.DMA
+    return pl.pallas_call(
+        swap_kernel,
+        out_shape=jax.ShapeDtypeStruct(rows.shape, rows.dtype),
+        in_specs=[pl.BlockSpec(memory_space=pl.ANY)],
+        out_specs=pl.BlockSpec(memory_space=pl.ANY),
+        scratch_shapes=[dma((4, 2)), dma((4, 2)), dma],
+        compiler_params=pltpu.CompilerParams(
+            collective_id=4, has_side_effects=True, vmem_limit_bytes=4 << 20
+        ),
+        cost_estimate=pl.CostEstimate(flops=0, transcendentals=0, bytes_accessed=50 << 20),
+        name="swap",
+    )(rows)
+
+
 def local_fast(
     layer_input,
     prev_logits,
@@ -1661,12 +1704,16 @@
     own_rows = qkv_weight.shape[0]
     part_width = 4 * features // parts
     mine = lax.axis_index("expert")
-    width = exp_gate.shape[1] // 2
-    halves = [
-        jnp.concatenate([exp_gate[:, half], exp_up[:, half], exp_down[half].T], axis=0)
-        for half in (slice(0, width), slice(width, 2 * width))
+    hidden_units = exp_gate.shape[1]
+    edges = (0, 3 * hidden_units // 8, 5 * hidden_units // 8, hidden_units)
+    triples = [
+        jnp.concatenate([exp_gate[:, span], exp_up[:, span], exp_down[span].T], axis=0)
+        for span in (slice(low, high) for low, high in zip(edges, edges[1:]))
     ]
-    first_half = lax.all_gather(halves[0], "dp", axis=0, tiled=True)
+    gathered = [
+        lax.all_gather(triple, "dp", axis=0, tiled=True).reshape((depth,) + triple.shape)
+        for triple in triples[:2]
+    ]
     both = jnp.concatenate([qkv_weight, out_weight], axis=1)
     piece = lax.dynamic_slice_in_dim(both, mine * part_width, part_width, axis=1)
     pack = pack_small(router, const_w, gain_attn, gain_moe, const_v)
@@ -1689,13 +1736,17 @@
         sine,
     )
     *saved, rows = run_before(common, parts, part_width)
-    received = lax.all_to_all(rows, "expert", split_axis=0, concat_axis=0, tiled=True)
-    first_half = first_half.reshape(depth, 3 * own_rows, width)
-    grads, *sums = run_slice(received, first_half, (), False)
-    first_own, second_half = exchange(grads, halves[1])
-    grads, back = run_slice(received, second_half, tuple(sums), True)
-    second_own = lax.psum_scatter(grads, "dp", scatter_dimension=0, tiled=False)
-    returned = lax.all_to_all(back, "expert", split_axis=0, concat_axis=0, tiled=True)
+    received = swap_rows(rows)
+    grads, *sums = run_slice(received, gathered[0], (), False)
+    own_first, gathered_last = exchange(grads, triples[2])
+    *sums, own_first, gathered_last = lax.optimization_barrier(
+        (*sums, own_first, gathered_last)
+    )
+    grads, *sums = run_slice(received, gathered[1], tuple(sums), False)
+    own_second = lax.psum_scatter(grads, "dp", scatter_dimension=0, tiled=False)
+    grads, back = run_slice(received, gathered_last, tuple(sums), True)
+    own_last = lax.psum_scatter(grads, "dp", scatter_dimension=0, tiled=False)
+    returned = swap_rows(back)
     result, grad_input, grad_prev, grad_weights, grad_small = run_after(
         common + tuple(saved) + (returned,), parts, part_width
     )
@@ -1711,7 +1762,9 @@
     own_small = own_small[:, :own_rows]
     grad_even = own_small[SUM_EVEN : SUM_EVEN + NC]
     grad_const = jnp.stack([grad_even, -grad_even], axis=1).reshape(2 * NC, -1).T
-    owned = jnp.concatenate([first_own, second_own.astype(jnp.float32)], axis=1)
+    owned = jnp.concatenate(
+        [own_first, own_second.astype(jnp.float32), own_last.astype(jnp.float32)], axis=1
+    )
     return (
         result,
         grad_input,

time: 393 us -> 409 us (1.041)
  Pallas kernels: 297 us -> 340 us
  blocking collectives: 26.3 us -> 0 us
  local copies, waits for them, and re-layouts: 22.9 us -> 43.7 us
  waiting for transfers between devices: 17.4 us -> 0.09 us
    pallas_call x0 -> x2, Pallas kernels: none -> 44.6 us  [swap_rows(): pl.pallas_call(swap_kernel, out_shape=jax.ShapeDtypeStruct(rows.shape, ro...]
    all_to_all x1 -> x0, blocking collectives: 26.3 us -> none  [local_fast(): lax.all_to_all(back, 'expert', split_axis=0, concat_axis=0, tiled=True)]
    unnamed x43 -> x67, local copies, waits for them, and re-layouts: 10.1 us -> 27.4 us
    all_to_all x1 -> x0, waiting for transfers between devices: 16.5 us -> none  [local_fast(): lax.all_to_all(rows, 'expert', split_axis=0, concat_axis=0, tiled=True)]
    pallas_call x1, Pallas kernels: 115 us -> 100 us  [exchange(): pl.pallas_call(exchange_kernel, out_shape=(jax.ShapeDtypeStruct((rows, wi...]
    pallas_call x1, Pallas kernels: 61.1 us -> 70.9 us  [reduce_tail(): pl.pallas_call(tail_kernel, out_shape=(jax.ShapeDtypeStruct((parts, rows,...]
    pallas_call x2 -> x3, Pallas kernels: 25.5 us -> 26 us  [run_slice(): pl.pallas_call(body, out_shape=out_shape, scratch_shapes=scratch, compile...]
  transfers between devices with their start and end apart: 3 -> 4, of which waited for: 2 -> 0; matrix products, arithmetic and copies ran while one was open for 5% -> 5% of each run, Pallas kernels for 40% -> 82%
where the time goes in v5:
time: 409 us; the launch traced here: 408 us
  Pallas kernels  340 us (83%)
  local copies, waits for them, and re-layouts  43.7 us (11%)
  between operations  14.2 us (3%)
  other arithmetic  9.89 us (2%)
    pallas_call x1, Pallas kernels, exchange(): pl.pallas_call(exchange_kernel, out_shape=(jax.ShapeDtypeStruct((rows, wi...  100 us
    pallas_call x1, Pallas kernels, reduce_tail(): pl.pallas_call(tail_kernel, out_shape=(jax.ShapeDtypeStruct((parts, rows,...  70.9 us
    pallas_call x1, Pallas kernels, gather_start(): pl.pallas_call(start_kernel, out_shape=(jax.ShapeDtypeStruct((parts, dept...  59.7 us
    pallas_call x2, Pallas kernels, swap_rows(): pl.pallas_call(swap_kernel, out_shape=jax.ShapeDtypeStruct(rows.shape, ro...  44.6 us
    unnamed x67, local copies, waits for them, and re-layouts  27.4 us
    pallas_call x3, Pallas kernels, run_slice(): pl.pallas_call(body, out_shape=out_shape, scratch_shapes=scratch, compile...  26 us
    pallas_call x1, Pallas kernels, run_after(): pl.pallas_call(after_kernel, out_shape=(jax.ShapeDtypeStruct((tokens, fea...  23.3 us
    pallas_call x1, Pallas kernels, run_before(): pl.pallas_call(before_kernel, out_shape=(low, low, low, low, jax.ShapeDty...  14.9 us
  transfers between devices with their start and end apart: 4, of which 0 were waited for; matrix products, arithmetic and copies ran while one was open for 5% of the time, Pallas kernels for 82%

profile of v5, /device:TPU:9, one launch (start us, length us, event | category | flops | bytes accessed | tf_op | source)
XLA Modules:
  0.0 407.9 jit_solution(4144216647327101476)
XLA Ops:
  19.0 59.7 %start.1 = (bf16[8,4,192,384]{3,2,1,0:T(8,128)(2,1)}, bf16[4,96,256]{2,1,0:T(8,128)(2,1)}) custom-call(bf16[192,384]{1,0:T(8,128)(2,1)} %fusion.piece_ref, bf16[96,256]{1,0:T(8,128)(2,1)} %pad.8.pack_ref), custom_call_target="tpu_custom_call" | custom-call | bytes 83886080 | tf_op jit(solution)/shard_map/start/pallas_call | solution.py:1118
  80.7 14.9 %before.1 = (bf16[256,768]{1,0:T(8,128)(2,1)}, bf16[256,768]{1,0:T(8,128)(2,1)}, bf16[256,768]{1,0:T(8,128)(2,1)}, bf16[256,768]{1,0:T(8,128)(2,1)}, f32[256,768...) custom-call(bf16[256,768]{1,0:T(8,128)(2,1)} %input_ref.3, f32[256,12]{1,0:T(8,128)} %copy.40.prev_ref, ...), custom_call_target="tpu_custom_call" | custom-call | flops 1207959552 | bytes 20971520 | tf_op jit(solution)/shard_map/before/pallas_call | solution.py:912
  95.6 1.4 copy-done.6
  97.0 20.5 %swap.2.refs_0_ = bf16[8,2,64,768]{3,2,1,0:T(8,128)(2,1)S(1)} custom-call(bf16[8,2,64,768]{3,2,1,0:T(8,128)(2,1)S(1)} %copy-done.6), custom_call_target="tpu_custom_call" | custom-call | bytes 52428800 | tf_op jit(solution)/shard_map/swap/pallas_call | solution.py:1670
  117.7 2.5 copy-done.7
  120.2 8.8 %experts.3 = (bf16[4,576,768]{2,1,0:T(8,128)(2,1)S(1)}, f32[512,768]{1,0:T(8,128)S(1)}, f32[512,768]{1,0:T(8,128)S(1)}) custom-call(bf16[8,2,64,768]{3,2,1,0:T(8,128)(2,1)S(1)} %swap.2.refs_0_, bf16[4,576,768]{2,1,0:T(8,128)(2,1)S(1)} %bitcast.42), custom_call_target="tpu_custom_call" | custom-call | flops 5435817984 | bytes 16777216 | tf_op jit(solution)/shard_map/experts/pallas_call | solution.py:1228
  130.2 100.4 %exchange.1 = (f32[576,768]{1,0:T(8,128)S(1)}, bf16[4,576,768]{2,1,0:T(8,128)(2,1)S(1)}) custom-call(bf16[4,576,768]{2,1,0:T(8,128)(2,1)S(1)} %get-tuple-element.54.grad_ref, bf16[576,768]{1,0:T(8,128)(2,1)S(1)} %pad_maximum_fusion.2.weight_ref), custom_call_target="tpu_custom_call" | custom-call | bytes 262144000 | tf_op jit(solution)/shard_map/exchange/pallas_call | solution.py:1421
  230.6 1.8 copy-done.8
  232.5 1.4 copy-done.2
  233.9 1.7 copy-done.10
  235.5 1.4 copy-done.16
  236.9 1.4 copy-done.18
  238.4 7.1 %experts.4 = (bf16[4,576,512]{2,1,0:T(8,128)(2,1)}, f32[512,768]{1,0:T(8,128)S(1)}, f32[512,768]{1,0:T(8,128)S(1)}) custom-call(bf16[8,2,64,768]{3,2,1,0:T(8,128)(2,1)S(1)} %copy-done.2, bf16[4,576,512]{2,1,0:T(8,128)(2,1)S(1)} %bitcast.43, f32[512,768]{1,0:T(8,128)S(1)} %copy-done.16, f32[512,768]{1,0:T(8,128)S(1)} %copy-done.18), custom_call_target="tpu_custom_call" | custom-call | flops 3623878656 | bytes 16777216 | tf_op jit(solution)/shard_map/experts/pallas_call | solution.py:1228
  247.8 1.4 copy-done.3
  249.2 2.0 copy-done.9
  251.2 1.4 copy-done.12
  252.6 1.4 copy-done.14
  254.0 10.0 %experts.5 = (bf16[4,576,768]{2,1,0:T(8,128)(2,1)}, bf16[8,2,64,768]{3,2,1,0:T(8,128)(2,1)S(1)}) custom-call(bf16[8,2,64,768]{3,2,1,0:T(8,128)(2,1)S(1)} %copy-done.3, bf16[4,576,768]{2,1,0:T(8,128)(2,1)S(1)} %copy-done.9, f32[512,768]{1,0:T(8,128)S(1)} %copy-done.12, f32[512,768]{1,0:T(8,128)S(1)} %copy-done.14), custom_call_target="tpu_custom_call" | custom-call | flops 5435817984 | bytes 16777216 | tf_op jit(solution)/shard_map/experts/pallas_call | solution.py:1228
  266.6 24.1 %swap.3.back_ref = bf16[8,2,64,768]{3,2,1,0:T(8,128)(2,1)S(1)} custom-call(bf16[8,2,64,768]{3,2,1,0:T(8,128)(2,1)S(1)} %copy-done.5), custom_call_target="tpu_custom_call" | custom-call | bytes 52428800 | tf_op jit(solution)/shard_map/swap/pallas_call | solution.py:1670
  291.9 23.3 %after.1 = (bf16[256,768]{1,0:T(8,128)(2,1)}, f32[256,768]{1,0:T(8,128)}, f32[256,12]{1,0:T(8,128)}, bf16[8,768,384]{2,1,0:T(8,128)(2,1)}, f32[32,768]{1,0:T(8,128)}) custom-call(bf16[256,768]{1,0:T(8,128)(2,1)} %input_ref.3, f32[256,12]{1,0:T(8,128)} %copy.40.prev_ref, s32[256,2]{1,0:T(8,128)} %copy.41.routes_ref, s32[256,1]{1,0:T(8,128)} %copy.42.column_ref, ...), custom_call_target="tpu_custom_call" | custom-call | flops 2415919104 | bytes 62914560 | tf_op jit(solution)/shard_map/after/pallas_call | solution.py:939
  316.8 70.9 %tail.1 = (bf16[8,192,384]{2,1,0:T(8,128)(2,1)}, f32[32,256]{1,0:T(8,128)}) custom-call(bf16[8,4,192,384]{3,2,1,0:T(8,128)(2,1)} %bitcast.48, bf16[4,32,256]{2,1,0:T(8,128)(2,1)} %pad.9.small_ref), custom_call_target="tpu_custom_call" | custom-call | bytes 125829120 | tf_op jit(solution)/shard_map/tail/pallas_call | solution.py:1597
  387.7 1.4 convert_bitcast_fusion
  394.7 2.2 bitcast_convert_fusion.1
  399.0 2.3 slice_bitcast_fusion
  (114 shorter events, 30.1 us)
Async XLA Ops:
  7.2 110.5 %all-gather.3.cloned.1.call-start = ((), (), s32[]{:S(2)}) async-start(), calls=%async_computation.2 | async-start | bytes 4423680 | tf_op jit(solution)/shard_map/all_gather | solution.py:1714
  9.6 2.1 slice-start
  9.7 2.1 slice-start.1
  10.6 2.1 copy-start.28
  10.6 2.1 copy-start.30
  10.6 2.1 copy-start.31
  10.6 2.2 copy-start.26
  10.6 2.2 copy-start.29
  10.7 221.8 %all-gather.5.cloned.1.call-start = ((), (), s32[]{:S(2)}) async-start(), calls=%async_computation.3 | async-start | bytes 2949120 | tf_op jit(solution)/shard_map/all_gather | solution.py:1714
  10.7 4.4 %copy-start.23 = (f32[256,12]{0,1:T(8,128)S(1)}, f32[256,12]{0,1:T(8,128)}, u32[]{:S(2)}) copy-start(f32[256,12]{0,1:T(8,128)} %param.16) | copy-start | bytes 36868
  10.7 5.2 %copy-start.27 = (s32[256,2]{0,1:T(2,128)S(1)}, s32[256,2]{0,1:T(2,128)}, u32[]{:S(2)}) copy-start(s32[256,2]{0,1:T(2,128)} %param.18) | copy-start | bytes 6148
  10.8 6.0 %copy-start.25 = (s32[1,256]{1,0:T(1,128)S(1)}, s32[1,256]{1,0:T(1,128)}, u32[]{:S(2)}) copy-start(s32[1,256]{1,0:T(1,128)} %row_ref.3) | copy-start | bytes 3076
  11.7 6.5 %copy-start.20 = (bf16[192,2304]{1,0:T(8,128)(2,1)S(1)}, bf16[192,2304]{1,0:T(8,128)(2,1)}, u32[]{:S(2)}) copy-start(bf16[192,2304]{1,0:T(8,128)(2,1)} %param.21) | copy-start | bytes 2654212
  11.8 6.5 %copy-start.21 = (bf16[192,768]{1,0:T(8,128)(2,1)S(1)}, bf16[192,768]{1,0:T(8,128)(2,1)}, u32[]{:S(2)}) copy-start(bf16[192,768]{1,0:T(8,128)(2,1)} %param.22) | copy-start | bytes 884740
  12.7 382.1 %reduce-scatter.3.cloned.1.call-start = ((), (), s32[]{:S(2)}) async-start(), calls=%async_computation.4 | async-start | bytes 2949120 | tf_op jit(solution)/shard_map/reduce_scatter | solution.py:1746
  117.6 11.5 %copy-start.1 = (bf16[8,2,64,768]{3,2,1,0:T(8,128)(2,1)}, bf16[8,2,64,768]{3,2,1,0:T(8,128)(2,1)S(1)}, u32[]{:S(2)}) copy-start(bf16[8,2,64,768]{3,2,1,0:T(8,128)(2,1)S(1)} %swap.2.refs_0_) | copy-start | bytes 4718596
  117.7 2.5 copy-start.7
  130.2 100.4 %copy-start.15 = (f32[512,768]{1,0:T(8,128)}, f32[512,768]{1,0:T(8,128)S(1)}, u32[]{:S(2)}) copy-start(f32[512,768]{1,0:T(8,128)S(1)} %get-tuple-element.58.refs_2_) | copy-start | bytes 4718596
  230.6 1.8 copy-start.8
  233.9 1.7 copy-start.10
  247.8 149.2 %reduce-scatter.5.cloned.1.call-start = ((), (), s32[]{:S(2)}) async-start(), calls=%async_computation.5 | async-start | bytes 4423680 | tf_op jit(solution)/shard_map/reduce_scatter | solution.py:1748
  249.2 2.0 copy-start.9
  390.3 2.0 copy-start.24
  397.0 1.5 copy-start.19
  (14 other events, 18.3 us)
Sparse Core Ops, SparseCore 0:
  10.8 84.0 all-gather.2
  97.1 70.8 all-gather.4
  247.9 50.5 reduce-scatter.2
  300.7 80.2 reduce-scatter.4

commit v6 on v5

--- a/solution.py
+++ b/solution.py
@@ -1002,174 +1002,166 @@
     return partner, plane, line
 
 
-def start_kernel(
-    piece_ref,
-    pack_ref,
-    weight_ref,
-    small_ref,
-    line_send,
-    line_recv,
-    pack_send,
-    pack_recv,
-    plane_send,
-    plane_recv,
-    pair_send,
-    pair_recv,
-    own_sem,
-    own_pack_sem,
-):
+def line_kernel(piece_ref, pack_ref, column_ref, small_ref, send, recv, local_sem):
     place, mine, core, chips, lines = neighbours()
     depth = len(lines)
-    partner, plane, line = all_peers(place, core, chips, lines)
-    greet([partner] + plane + line)
-    own_copy = pltpu.make_async_copy(piece_ref, weight_ref.at[mine, place], own_sem)
-    own_pack = pltpu.make_async_copy(pack_ref, small_ref.at[place], own_pack_sem)
-    own_copy.start()
-    own_pack.start()
+    _, _, line = all_peers(place, core, chips, lines)
+    pairs = ((piece_ref, column_ref), (pack_ref, small_ref))
+    local = [
+        pltpu.make_async_copy(source, target.at[place], local_sem.at[kind])
+        for kind, (source, target) in enumerate(pairs)
+    ]
+    for copy in local:
+        copy.start()
+    greet(line)
     sent = []
-
-    def line_copy(step):
-        return copy_to(
-            piece_ref,
-            weight_ref.at[mine, place],
-            line_send.at[step - 1],
-            line_recv.at[depth - step - 1],
-            line[step - 1],
-        )
-
-    def pack_copy(step):
-        return copy_to(
-            pack_ref,
-            small_ref.at[place],
-            pack_send.at[step - 1],
-            pack_recv.at[depth - step - 1],
-            line[step - 1],
-        )
-
-    for step in range(1, depth):
-        copy = line_copy(step)
-        copy.start()
-        sent.append(copy)
-    for chip in (3, 1, 2):
-        copy = copy_to(
-            piece_ref,
-            weight_ref.at[mine, place],
-            plane_send.at[chip - 1, 0],
-            plane_recv.at[chip - 1, 0],
-            plane[chip - 1],
-        )
-        copy.start()
-        sent.append(copy)
-    copy = copy_to(
-        piece_ref, weight_ref.at[mine, place], pair_send.at[0, 0], pair_recv.at[0, 0], partner
-    )
-    copy.start()
-    sent.append(copy)
-    for step in range(1, depth):
-        copy = pack_copy(step)
-        copy.start()
-        sent.append(copy)
-
-    def arrived(slot, spot, semaphore):
-        here = weight_ref.at[slot, spot]
-        copy_to(here, here, own_sem, semaphore, partner).wait_recv()
-        return here
-
-    for step in range(depth):
-        spot = lines[step]
-        if step > 0:
-            here = arrived(mine, spot, line_recv.at[step - 1])
-            for chip in (3, 1, 2):
-                copy = copy_to(
-                    here,
-                    here,
-                    plane_send.at[chip - 1, step],
-                    plane_recv.at[chip - 1, step],
-                    plane[chip - 1],
-                )
-                copy.start()
-                sent.append(copy)
-            copy = copy_to(here, here, pair_send.at[0, step], pair_recv.at[0, step], partner)
-            copy.start()
-            sent.append(copy)
-    for step in range(depth):
-        spot = lines[step]
-        for chip in (1, 2, 3):
-            here = arrived(chips[chip] + core, spot, plane_recv.at[chip - 1, step])
+    for kind, (source, target) in enumerate(pairs):
+        for step in range(1, depth):
             copy = copy_to(
-                here, here, pair_send.at[chip, step], pair_recv.at[chip, step], partner
+                source,
+                target.at[place],
+                send.at[kind, step - 1],
+                recv.at[kind, depth - step - 1],
+                line[step - 1],
             )
             copy.start()
             sent.append(copy)
-    for step in range(depth):
-        for chip in range(4):
-            arrived(chips[chip] + 1 - core, lines[step], pair_recv.at[chip, step])
-    for step in range(1, depth):
-        here = small_ref.at[lines[step]]
-        copy_to(here, here, own_pack_sem, pack_recv.at[step - 1], partner).wait_recv()
-    own_copy.wait()
-    own_pack.wait()
+    for kind, (_, target) in enumerate(pairs):
+        for step in range(1, depth):
+            here = target.at[lines[step]]
+            copy_to(here, here, local_sem.at[0], recv.at[kind, step - 1], line[0]).wait_recv()
+    for copy in local:
+        copy.wait()
     for copy in sent:
         copy.wait_send()
 
 
-def gather_start(piece, pack, parts, depth):
+def gather_line(piece, pack, depth):
     dma = pltpu.SemaphoreType.DMA
     return pl.pallas_call(
-        start_kernel,
+        line_kernel,
         out_shape=(
-            jax.ShapeDtypeStruct((parts, depth) + piece.shape, piece.dtype),
+            jax.ShapeDtypeStruct((depth,) + piece.shape, piece.dtype),
             jax.ShapeDtypeStruct((depth,) + pack.shape, pack.dtype),
         ),
         in_specs=[pl.BlockSpec(memory_space=pltpu.VMEM)] * 2,
-        out_specs=[pl.BlockSpec(memory_space=pl.ANY)] * 2,
-        scratch_shapes=[
-            dma((depth - 1,)),
-            dma((depth - 1,)),
-            dma((depth - 1,)),
-            dma((depth - 1,)),
-            dma((3, depth)),
-            dma((3, depth)),
-            dma((4, depth)),
-            dma((4, depth)),
-            dma,
-            dma,
-        ],
+        out_specs=[pl.BlockSpec(memory_space=pltpu.VMEM)] * 2,
+        scratch_shapes=[dma((2, depth - 1)), dma((2, depth - 1)), dma((2,))],
         compiler_params=pltpu.CompilerParams(
-            collective_id=1, has_side_effects=True, vmem_limit_bytes=60 << 20
+            collective_id=1, has_side_effects=True, vmem_limit_bytes=4 << 20
         ),
-        cost_estimate=pl.CostEstimate(flops=0, transcendentals=0, bytes_accessed=80 << 20),
-        name="start",
+        cost_estimate=pl.CostEstimate(flops=0, transcendentals=0, bytes_accessed=30 << 20),
+        name="line",
     )(piece, pack)
 
 
-def slice_kernel(first, last, *refs):
+def plane_kernel(
+    column_ref, weight_ref, plane_send, plane_recv, pair_send, pair_recv, local_sem
+):
+    place, mine, core, chips, lines = neighbours()
+    depth = column_ref.shape[0]
+    partner, plane, _ = all_peers(place, core, chips, lines)
+    local = pltpu.make_async_copy(column_ref, weight_ref.at[mine], local_sem)
+    local.start()
+    greet([partner] + plane)
+    sent = []
+
+    def send(*items):
+        copy = copy_to(*items)
+        copy.start()
+        sent.append(copy)
+
+    def arrived(here, semaphore):
+        copy_to(here, here, local_sem, semaphore, partner).wait_recv()
+
+    for spot in range(depth):
+        for chip in (3, 1, 2):
+            send(
+                column_ref.at[spot],
+                weight_ref.at[mine, spot],
+                plane_send.at[chip - 1, spot],
+                plane_recv.at[chip - 1, spot],
+                plane[chip - 1],
+            )
+    for spot in range(depth):
+        send(
+            column_ref.at[spot],
+            weight_ref.at[mine, spot],
+            pair_send.at[0, spot],
+            pair_recv.at[0, spot],
+            partner,
+        )
+    for spot in range(depth):
+        for chip in (1, 2, 3):
+            here = weight_ref.at[chips[chip] + core, spot]
+            arrived(here, plane_recv.at[chip - 1, spot])
+            send(here, here, pair_send.at[chip, spot], pair_recv.at[chip, spot], partner)
+    for spot in range(depth):
+        for chip in range(4):
+            arrived(weight_ref.at[chips[chip] + 1 - core, spot], pair_recv.at[chip, spot])
+    local.wait()
+    for copy in sent:
+        copy.wait_send()
+
+
+def gather_plane(column, parts):
+    depth = column.shape[0]
+    dma = pltpu.SemaphoreType.DMA
+    return pl.pallas_call(
+        plane_kernel,
+        out_shape=jax.ShapeDtypeStruct((parts,) + column.shape, column.dtype),
+        in_specs=[pl.BlockSpec(memory_space=pltpu.VMEM)],
+        out_specs=pl.BlockSpec(memory_space=pl.ANY),
+        scratch_shapes=[dma((3, depth)), dma((3, depth)), dma((4, depth)), dma((4, depth)), dma],
+        compiler_params=pltpu.CompilerParams(
+            collective_id=5, has_side_effects=True, vmem_limit_bytes=60 << 20
+        ),
+        cost_estimate=pl.CostEstimate(flops=0, transcendentals=0, bytes_accessed=60 << 20),
+        name="plane",
+    )(column)
+
+
+def slice_kernel(count, first, *refs):
+    weight_refs, refs = refs[1 : 1 + count], refs[:1] + refs[1 + count :]
     if first:
-        rows_ref, weight_ref, *refs = refs
+        rows_ref, grad_ref, out_sum, back_sum, *refs = refs
+        gates, ups, downs, rows_turned, grads_turned, load_sem = refs
+        carried = []
     else:
-        rows_ref, weight_ref, out_in, back_in, *refs = refs
-    if last:
-        grad_ref, both_ref, gates, ups, downs, rows_turned, grads_turned, out_sum, back_sum = refs
-    else:
-        grad_ref, out_sum, back_sum, gates, ups, downs, rows_turned, grads_turned = refs
-    depth, triple, width = weight_ref.shape
+        rows_ref, out_in, back_in, grad_ref, both_ref, *refs = refs
+        gates, ups, downs, rows_turned, grads_turned, load_sem, *refs = refs
+        out_sum, back_sum, out_before, back_before, carry_sem = refs
+        carried = [
+            pltpu.make_async_copy(out_in, out_before, carry_sem.at[0]),
+            pltpu.make_async_copy(back_in, back_before, carry_sem.at[1]),
+        ]
+    depth, triple, width = grad_ref.shape
     part = triple // 3
     sources, _, slots, features = rows_ref.shape
+    loads = []
+    at = 0
+    for index, weight_ref in enumerate(weight_refs):
+        span = weight_ref.shape[2]
+        for spot in range(depth):
+            for kind, held in enumerate((gates, ups, downs)):
+                loads.append(
+                    pltpu.make_async_copy(
+                        weight_ref.at[spot, pl.ds(kind * part, part)],
+                        held.at[pl.ds(spot * part, part), pl.ds(at, span)],
+                        load_sem.at[index, spot, kind],
+                    )
+                )
+        at += span
+    for copy in loads + carried:
+        copy.start()
     token_rows = rows_ref[:, 0].reshape(sources * slots, features)
     grad_rows = rows_ref[:, 1].reshape(sources * slots, features)
     rows_turned[...] = token_rows.T
     grads_turned[...] = grad_rows.T
-    for spot in range(depth):
-        here = slice(spot * part, (spot + 1) * part)
-        gates[here, :] = weight_ref[spot, :part]
-        ups[here, :] = weight_ref[spot, part : 2 * part]
-        downs[here, :] = weight_ref[spot, 2 * part :]
-    if first:
-        out_sum[...] = jnp.zeros_like(out_sum)
-        back_sum[...] = jnp.zeros_like(back_sum)
-    else:
-        out_sum[...] = out_in[...]
-        back_sum[...] = back_in[...]
+    out_sum[...] = jnp.zeros_like(out_sum)
+    back_sum[...] = jnp.zeros_like(back_sum)
+    for copy in loads:
+        copy.wait()
     chunk = 256
 
     def one_chunk(step, carry):
@@ -1203,40 +1195,48 @@
         return carry
 
     lax.fori_loop(0, width // chunk, one_chunk, 0)
-    if last:
-        both_ref[:, 0] = out_sum[...].astype(jnp.bfloat16).reshape(sources, slots, features)
-        both_ref[:, 1] = back_sum[...].astype(jnp.bfloat16).reshape(sources, slots, features)
-
-
-def run_slice(received, weights, sums, last):
-    depth, triple, width = weights.shape
+    for copy in carried:
+        copy.wait()
+    if not first:
+        totals = (out_sum[...] + out_before[...], back_sum[...] + back_before[...])
+        for kind, total in enumerate(totals):
+            both_ref[:, kind] = total.astype(jnp.bfloat16).reshape(sources, slots, features)
+
+
+def run_slice(received, weights, sums):
+    depth, triple, _ = weights[0].shape
+    width = sum(weight.shape[2] for weight in weights)
     sources, _, slots, features = received.shape
     rows = sources * slots
     total = jax.ShapeDtypeStruct((rows, features), jnp.float32)
-    grads = jax.ShapeDtypeStruct(weights.shape, jnp.bfloat16)
+    grads = jax.ShapeDtypeStruct((depth, triple, width), jnp.bfloat16)
     low = jnp.bfloat16
+    dma = pltpu.SemaphoreType.DMA
     scratch = [pltpu.VMEM((features, width), low)] * 3 + [pltpu.VMEM((features, rows), low)] * 2
-    if last:
+    scratch.append(dma((len(weights), depth, 3)))
+    if sums:
         out_shape = (grads, jax.ShapeDtypeStruct(received.shape, low))
-        scratch = scratch + [pltpu.VMEM((rows, features), jnp.float32)] * 2
+        scratch += [pltpu.VMEM((rows, features), jnp.float32)] * 4 + [dma((2,))]
     else:
         out_shape = (grads, total, total)
 
     def body(*refs):
-        slice_kernel(not sums, last, *refs)
+        slice_kernel(len(weights), not sums, *refs)
 
     return pl.pallas_call(
         body,
         out_shape=out_shape,
+        in_specs=[pl.BlockSpec(memory_space=pltpu.VMEM)]
+        + [pl.BlockSpec(memory_space=pl.ANY)] * (len(weights) + len(sums)),
         scratch_shapes=scratch,
-        compiler_params=pltpu.CompilerParams(vmem_limit_bytes=40 << 20),
+        compiler_params=pltpu.CompilerParams(vmem_limit_bytes=60 << 20),
         cost_estimate=pl.CostEstimate(
             flops=18 * rows * features * width,
             transcendentals=rows * width,
             bytes_accessed=16 << 20,
         ),
         name="experts",
-    )(received, weights, *sums)
+    )(received, *weights, *sums)
 
 
 def exchange_kernel(
@@ -1433,7 +1433,7 @@
         + [dma((depth, pieces))] * 8
         + [dma],
         compiler_params=pltpu.CompilerParams(
-            collective_id=2, has_side_effects=True, vmem_limit_bytes=32 << 20
+            collective_id=2, has_side_effects=True, vmem_limit_bytes=60 << 20
         ),
         cost_estimate=pl.CostEstimate(flops=0, transcendentals=0, bytes_accessed=250 << 20),
         name="exchange",
@@ -1674,7 +1674,7 @@
         out_specs=pl.BlockSpec(memory_space=pl.ANY),
         scratch_shapes=[dma((4, 2)), dma((4, 2)), dma],
         compiler_params=pltpu.CompilerParams(
-            collective_id=4, has_side_effects=True, vmem_limit_bytes=4 << 20
+            collective_id=4, has_side_effects=True, vmem_limit_bytes=60 << 20
         ),
         cost_estimate=pl.CostEstimate(flops=0, transcendentals=0, bytes_accessed=50 << 20),
         name="swap",
@@ -1705,21 +1705,23 @@
     part_width = 4 * features // parts
     mine = lax.axis_index("expert")
     hidden_units = exp_gate.shape[1]
-    edges = (0, 3 * hidden_units // 8, 5 * hidden_units // 8, hidden_units)
+    edges = (0, 3 * hidden_units // 8, hidden_units // 2, hidden_units)
     triples = [
         jnp.concatenate([exp_gate[:, span], exp_up[:, span], exp_down[span].T], axis=0)
         for span in (slice(low, high) for low, high in zip(edges, edges[1:]))
-    ]
-    gathered = [
-        lax.all_gather(triple, "dp", axis=0, tiled=True).reshape((depth,) + triple.shape)
-        for triple in triples[:2]
     ]
     both = jnp.concatenate([qkv_weight, out_weight], axis=1)
     piece = lax.dynamic_slice_in_dim(both, mine * part_width, part_width, axis=1)
     pack = pack_small(router, const_w, gain_attn, gain_moe, const_v)
     pack_width = pl.cdiv(own_rows, LANES) * LANES
     pack = jnp.pad(pack, ((0, 0), (0, pack_width - own_rows)))
-    weights, small = gather_start(piece, pack, parts, depth)
+    column, small = gather_line(piece, pack, depth)
+    column, small, *triples[:2] = lax.optimization_barrier((column, small, *triples[:2]))
+    gathered = [
+        lax.all_gather(triple, "dp", axis=0, tiled=True).reshape((depth,) + triple.shape)
+        for triple in triples[:2]
+    ]
+    weights = gather_plane(column, parts)
     weights = weights.reshape(parts, features, part_width)
     small = small[:, :, :own_rows].transpose(1, 0, 2).reshape(SMALL_ROWS, features)
     cosine, sine = rotary_tables(tokens, features // HEADS)
@@ -1737,14 +1739,9 @@
     )
     *saved, rows = run_before(common, parts, part_width)
     received = swap_rows(rows)
-    grads, *sums = run_slice(received, gathered[0], (), False)
+    grads, *sums = run_slice(received, gathered[:1], ())
     own_first, gathered_last = exchange(grads, triples[2])
-    *sums, own_first, gathered_last = lax.optimization_barrier(
-        (*sums, own_first, gathered_last)
-    )
-    grads, *sums = run_slice(received, gathered[1], tuple(sums), False)
-    own_second = lax.psum_scatter(grads, "dp", scatter_dimension=0, tiled=False)
-    grads, back = run_slice(received, gathered_last, tuple(sums), True)
+    grads, back = run_slice(received, [gathered[1], gathered_last], tuple(sums))
     own_last = lax.psum_scatter(grads, "dp", scatter_dimension=0, tiled=False)
     returned = swap_rows(back)
     result, grad_input, grad_prev, grad_weights, grad_small = run_after(
@@ -1762,9 +1759,7 @@
     own_small = own_small[:, :own_rows]
     grad_even = own_small[SUM_EVEN : SUM_EVEN + NC]
     grad_const = jnp.stack([grad_even, -grad_even], axis=1).reshape(2 * NC, -1).T
-    owned = jnp.concatenate(
-        [own_first, own_second.astype(jnp.float32), own_last.astype(jnp.float32)], axis=1
-    )
+    owned = jnp.concatenate([own_first, own_last.astype(jnp.float32)], axis=1)
     return (
         result,
         grad_input,

time: 409 us -> 398 us (0.973)
  local copies, waits for them, and re-layouts: 43.7 us -> 14 us
  Pallas kernels: 340 us -> 358 us
    unnamed x67 -> x31, local copies, waits for them, and re-layouts: 27.4 us -> 3.31 us
    pallas_call x1, Pallas kernels: 100 us -> 115 us  [exchange(): pl.pallas_call(exchange_kernel, out_shape=(jax.ShapeDtypeStruct((rows, wi...]
  transfers between devices with their start and end apart: 4 -> 3, of which waited for: 0 -> 0; matrix products, arithmetic and copies ran while one was open for 5% -> 4% of each run, Pallas kernels for 82% -> 80%
where the time goes in v6:
time: 398 us; the launch traced here: 397 us
  Pallas kernels  358 us (90%)
  between operations  14.2 us (4%)
  local copies, waits for them, and re-layouts  14 us (4%)
  other arithmetic  10.1 us (3%)
    pallas_call x1, Pallas kernels, exchange(): pl.pallas_call(exchange_kernel, out_shape=(jax.ShapeDtypeStruct((rows, wi...  115 us
    pallas_call x1, Pallas kernels, reduce_tail(): pl.pallas_call(tail_kernel, out_shape=(jax.ShapeDtypeStruct((parts, rows,...  71.7 us
    pallas_call x2, Pallas kernels, swap_rows(): pl.pallas_call(swap_kernel, out_shape=jax.ShapeDtypeStruct(rows.shape, ro...  44.7 us
    pallas_call x2, Pallas kernels, run_slice(): pl.pallas_call(body, out_shape=out_shape, in_specs=[pl.BlockSpec(memory_s...  34.9 us
    pallas_call x1, Pallas kernels, gather_plane(): pl.pallas_call(plane_kernel, out_shape=jax.ShapeDtypeStruct((parts,) + co...  32.9 us
    pallas_call x1, Pallas kernels, run_after(): pl.pallas_call(after_kernel, out_shape=(jax.ShapeDtypeStruct((tokens, fea...  23.2 us
    pallas_call x1, Pallas kernels, gather_line(): pl.pallas_call(line_kernel, out_shape=(jax.ShapeDtypeStruct((depth,) + pi...  21 us
    pallas_call x1, Pallas kernels, run_before(): pl.pallas_call(before_kernel, out_shape=(low, low, low, low, jax.ShapeDty...  15 us
  transfers between devices with their start and end apart: 3, of which 0 were waited for; matrix products, arithmetic and copies ran while one was open for 4% of the time, Pallas kernels for 80%

profile of v6, /device:TPU:9, one launch (start us, length us, event | category | flops | bytes accessed | tf_op | source)
XLA Modules:
  0.0 397.3 jit_solution(630280232768368300)
XLA Ops:
  7.3 0.8 slice.73
  9.8 21.0 %line.1 = (bf16[4,192,384]{2,1,0:T(8,128)(2,1)S(1)}, bf16[4,96,256]{2,1,0:T(8,128)(2,1)S(1)}) custom-call(bf16[192,384]{1,0:T(8,128)(2,1)S(1)} %fusion.3.piece_ref, bf16[96,256]{1,0:T(8,128)(2,1)S(1)} %pad.8.pack_ref), custom_call_target="tpu_custom_call" | custom-call | bytes 31457280 | tf_op jit(solution)/shard_map/line/pallas_call | solution.py:1041
  30.8 0.8 copy-done
  32.4 1.0 pad_maximum_fusion.2
  35.2 0.8 copy.40.prev_ref
  36.0 0.8 copy.41.routes_ref
  36.8 0.8 copy.42.column_ref
  38.5 0.8 reshape.69.small_ref
  39.3 32.9 %plane.1 = bf16[8,4,192,384]{3,2,1,0:T(8,128)(2,1)} custom-call(bf16[4,192,384]{2,1,0:T(8,128)(2,1)} %copy-done), custom_call_target="tpu_custom_call" | custom-call | bytes 62914560 | tf_op jit(solution)/shard_map/plane/pallas_call | solution.py:1110
  72.2 15.0 %before.1 = (bf16[256,768]{1,0:T(8,128)(2,1)}, bf16[256,768]{1,0:T(8,128)(2,1)}, bf16[256,768]{1,0:T(8,128)(2,1)}, bf16[256,768]{1,0:T(8,128)(2,1)}, f32[256,768...) custom-call(bf16[256,768]{1,0:T(8,128)(2,1)} %input_ref.3, f32[256,12]{1,0:T(8,128)} %copy.40.prev_ref, ...), custom_call_target="tpu_custom_call" | custom-call | flops 1207959552 | bytes 20971520 | tf_op jit(solution)/shard_map/before/pallas_call | solution.py:912
  87.3 20.9 %swap.2.refs_0_ = bf16[8,2,64,768]{3,2,1,0:T(8,128)(2,1)} custom-call(bf16[8,2,64,768]{3,2,1,0:T(8,128)(2,1)} %get-tuple-element.50.rows_ref), custom_call_target="tpu_custom_call" | custom-call | bytes 52428800 | tf_op jit(solution)/shard_map/swap/pallas_call | solution.py:1670
  108.2 1.1 pad_maximum_fusion.1.weight_ref
  109.3 13.7 %experts.2 = (bf16[4,576,768]{2,1,0:T(8,128)(2,1)}, f32[512,768]{1,0:T(8,128)}, f32[512,768]{1,0:T(8,128)}) custom-call(bf16[8,2,64,768]{3,2,1,0:T(8,128)(2,1)} %swap.2.refs_0_, bf16[4,576,768]{2,1,0:T(8,128)(2,1)} %bitcast.54), custom_call_target="tpu_custom_call" | custom-call | flops 5435817984 | bytes 16777216 | tf_op jit(solution)/shard_map/experts/pallas_call | solution.py:1226
  123.0 114.6 %exchange.1 = (f32[576,768]{1,0:T(8,128)}, bf16[4,576,1024]{2,1,0:T(8,128)(2,1)}) custom-call(bf16[4,576,768]{2,1,0:T(8,128)(2,1)} %get-tuple-element.53.grad_ref, bf16[576,1024]{1,0:T(8,128)(2,1)} %pad_maximum_fusion.1.weight_ref), custom_call_target="tpu_custom_call" | custom-call | bytes 262144000 | tf_op jit(solution)/shard_map/exchange/pallas_call | solution.py:1421
  237.7 21.2 %experts.3 = (bf16[4,576,1280]{2,1,0:T(8,128)(2,1)}, bf16[8,2,64,768]{3,2,1,0:T(8,128)(2,1)}) custom-call(bf16[8,2,64,768]{3,2,1,0:T(8,128)(2,1)} %swap.2.refs_0_, bf16[4,576,256]{2,1,0:T(8,128)(2,1)} %bitcast.55, bf16[4,576,1024]{2,1,0:T(8,128)(2,1)} %get-tuple-element.54.refs_2_, f32[512,768]{1,0:T(8,128)} %get-tuple-element.55.refs_3_, ...), custom_call_target="tpu_custom_call" | custom-call | flops 9059696640 | bytes 16777216 | tf_op jit(solution)/shard_map/experts/pallas_call | solution.py:1226
  259.0 23.9 %swap.3.back_ref = bf16[8,2,64,768]{3,2,1,0:T(8,128)(2,1)} custom-call(bf16[8,2,64,768]{3,2,1,0:T(8,128)(2,1)} %get-tuple-element.57.rows_ref), custom_call_target="tpu_custom_call" | custom-call | bytes 52428800 | tf_op jit(solution)/shard_map/swap/pallas_call | solution.py:1670
  282.8 23.2 %after.1 = (bf16[256,768]{1,0:T(8,128)(2,1)}, f32[256,768]{1,0:T(8,128)}, f32[256,12]{1,0:T(8,128)}, bf16[8,768,384]{2,1,0:T(8,128)(2,1)}, f32[32,768]{1,0:T(8,128)}) custom-call(bf16[256,768]{1,0:T(8,128)(2,1)} %input_ref.3, f32[256,12]{1,0:T(8,128)} %copy.40.prev_ref, s32[256,2]{1,0:T(8,128)} %copy.41.routes_ref, s32[256,1]{1,0:T(8,128)} %copy.42.column_ref, ...), custom_call_target="tpu_custom_call" | custom-call | flops 2415919104 | bytes 62914560 | tf_op jit(solution)/shard_map/after/pallas_call | solution.py:939
  306.1 0.9 convert_element_type.22
  307.7 71.7 %tail.1 = (bf16[8,192,384]{2,1,0:T(8,128)(2,1)}, f32[32,256]{1,0:T(8,128)}) custom-call(bf16[8,4,192,384]{3,2,1,0:T(8,128)(2,1)} %bitcast.43, bf16[4,32,256]{2,1,0:T(8,128)(2,1)} %pad.9.small_ref), custom_call_target="tpu_custom_call" | custom-call | bytes 125829120 | tf_op jit(solution)/shard_map/tail/pallas_call | solution.py:1597
  379.5 1.5 convert_bitcast_fusion
  381.2 0.9 slice.95
  382.1 1.3 slice.94
  386.5 1.7 bitcast_convert_fusion
  388.4 2.4 fusion.2
  (81 shorter events, 9.4 us)
Async XLA Ops:
  7.2 1.7 copy-start.3
  7.2 1.7 copy-start.12
  7.2 1.7 copy-start.13
  7.2 1.8 copy-start.11
  7.2 1.8 copy-start.9
  7.2 2.5 copy-start.4
  7.2 2.5 copy-start.2
  7.3 102.0 %all-gather.5.cloned.1.call-start = ((), (), s32[]{:S(2)}) async-start(), calls=%async_computation.2 | async-start | bytes 4423680 | tf_op jit(solution)/shard_map/all_gather | solution.py:1721
  8.8 22.8 %slice-start = ((bf16[192,2048]{1,0:T(8,128)(2,1)}), bf16[192,256]{1,0:T(8,128)(2,1)S(1)}, s32[]{:S(2)}) async-start(bf16[192,2048]{1,0:T(8,128)(2,1)} %param.27), calls=%async_computation.4 | async-start | bytes 196608 | tf_op jit(solution)/shard_map/slice | solution.py:1710
  8.8 22.8 %slice-start.3 = ((bf16[192,2048]{1,0:T(8,128)(2,1)}), bf16[192,256]{1,0:T(8,128)(2,1)S(1)}, s32[]{:S(2)}) async-start(bf16[192,2048]{1,0:T(8,128)(2,1)} %param.28), calls=%async_computation.7 | async-start | bytes 196608 | tf_op jit(solution)/shard_map/slice | solution.py:1710
  8.8 23.5 %slice-start.1 = ((bf16[192,2048]{1,0:T(8,128)(2,1)}), bf16[192,768]{1,0:T(8,128)(2,1)S(1)}, s32[]{:S(2)}) async-start(bf16[192,2048]{1,0:T(8,128)(2,1)} %param.27), calls=%async_computation.5 | async-start | bytes 589824 | tf_op jit(solution)/shard_map/slice | solution.py:1710
  8.9 23.5 %slice-start.4 = ((bf16[192,2048]{1,0:T(8,128)(2,1)}), bf16[192,768]{1,0:T(8,128)(2,1)S(1)}, s32[]{:S(2)}) async-start(bf16[192,2048]{1,0:T(8,128)(2,1)} %param.28), calls=%async_computation.8 | async-start | bytes 589824 | tf_op jit(solution)/shard_map/slice | solution.py:1710
  30.8 0.8 copy-start
  33.3 1.9 copy-start.6
  33.3 2.6 copy-start.10
  33.4 3.4 copy-start.8
  33.4 204.3 %all-gather.3.cloned.1.call-start = ((), (), s32[]{:S(2)}) async-start(), calls=%async_computation.1 | async-start | bytes 1474560 | tf_op jit(solution)/shard_map/all_gather | solution.py:1721
  34.1 352.4 %reduce-scatter.2.cloned.1.call-start = ((), (), s32[]{:S(2)}) async-start(), calls=%async_computation.3 | async-start | bytes 7372800 | tf_op jit(solution)/shard_map/reduce_scatter | solution.py:1745
  87.3 20.9 %slice-start.2 = ((bf16[192,2048]{1,0:T(8,128)(2,1)}), bf16[192,1024]{1,0:T(8,128)(2,1)S(1)}, s32[]{:S(2)}) async-start(bf16[192,2048]{1,0:T(8,128)(2,1)} %param.27), calls=%async_computation.6 | async-start | bytes 786432 | tf_op jit(solution)/shard_map/slice | solution.py:1710
  87.3 20.9 %slice-start.5 = ((bf16[192,2048]{1,0:T(8,128)(2,1)}), bf16[192,1024]{1,0:T(8,128)(2,1)S(1)}, s32[]{:S(2)}) async-start(bf16[192,2048]{1,0:T(8,128)(2,1)} %param.28), calls=%async_computation.9 | async-start | bytes 786432 | tf_op jit(solution)/shard_map/slice | solution.py:1710
  382.1 1.3 copy-start.5
  382.1 2.0 copy-start.7
  386.5 1.9 copy-start.1
Sparse Core Ops, SparseCore 0:
  33.5 68.1 all-gather.4
  103.8 36.9 all-gather.2
  259.1 121.4 reduce-scatter.1

commit v7 on v6

--- a/solution.py
+++ b/solution.py
@@ -1002,123 +1002,193 @@
     return partner, plane, line
 
 
-def line_kernel(piece_ref, pack_ref, column_ref, small_ref, send, recv, local_sem):
+def start_kernel(
+    piece_ref,
+    pack_ref,
+    weight_ref,
+    small_ref,
+    line_send,
+    line_recv,
+    pack_send,
+    pack_recv,
+    plane_send,
+    plane_recv,
+    pair_send,
+    pair_recv,
+    local_sem,
+):
     place, mine, core, chips, lines = neighbours()
     depth = len(lines)
-    _, _, line = all_peers(place, core, chips, lines)
-    pairs = ((piece_ref, column_ref), (pack_ref, small_ref))
+    top = depth - 1
+    partner, plane, _ = all_peers(place, core, chips, lines)
+    above, below = (place + 1, mine), (place - 1, mine)
     local = [
-        pltpu.make_async_copy(source, target.at[place], local_sem.at[kind])
-        for kind, (source, target) in enumerate(pairs)
+        pltpu.make_async_copy(piece_ref, weight_ref.at[mine, place], local_sem.at[0]),
+        pltpu.make_async_copy(pack_ref, small_ref.at[place], local_sem.at[1]),
     ]
     for copy in local:
         copy.start()
-    greet(line)
-    sent = []
-    for kind, (source, target) in enumerate(pairs):
-        for step in range(1, depth):
-            copy = copy_to(
-                source,
-                target.at[place],
-                send.at[kind, step - 1],
-                recv.at[kind, depth - step - 1],
-                line[step - 1],
-            )
-            copy.start()
-            sent.append(copy)
-    for kind, (_, target) in enumerate(pairs):
-        for step in range(1, depth):
-            here = target.at[lines[step]]
-            copy_to(here, here, local_sem.at[0], recv.at[kind, step - 1], line[0]).wait_recv()
+    barrier = pltpu.get_barrier_semaphore()
+    mesh_id = pl.DeviceIdType.MESH
+    for device in [partner] + plane:
+        pl.semaphore_signal(barrier, inc=1, device_id=device, device_id_type=mesh_id)
+    for there, device in ((place > 0, below), (place < top, above)):
+
+        @pl.when(there)
+        def _():
+            pl.semaphore_signal(barrier, inc=1, device_id=device, device_id_type=mesh_id)
+
+    at_end = (place == 0) | (place == top)
+    for there, count in ((at_end, 5), (jnp.logical_not(at_end), 6)):
+
+        @pl.when(there)
+        def _():
+            pl.semaphore_wait(barrier, count)
+
+    def along(up, origin, first=False):
+        here = weight_ref.at[mine, origin]
+        way = 0 if up else 1
+        return copy_to(
+            piece_ref if first else here,
+            here,
+            line_send.at[way, origin],
+            line_recv.at[origin],
+            above if up else below,
+        )
+
+    def along_pack(up, origin, first=False):
+        here = small_ref.at[origin]
+        way = 0 if up else 1
+        return copy_to(
+            pack_ref if first else here,
+            here,
+            pack_send.at[way, origin],
+            pack_recv.at[origin],
+            above if up else below,
+        )
+
+    def over_plane(chip, origin, source):
+        return copy_to(
+            source,
+            weight_ref.at[mine, origin],
+            plane_send.at[chip - 1, origin],
+            plane_recv.at[chip - 1, origin],
+            plane[chip - 1],
+        )
+
+    def to_partner(chip, origin, source):
+        return copy_to(
+            source,
+            weight_ref.at[chips[chip] + core, origin],
+            pair_send.at[chip, origin],
+            pair_recv.at[chip, origin],
+            partner,
+        )
+
+    def arrived(here, semaphore):
+        copy_to(here, here, local_sem.at[0], semaphore, partner).wait_recv()
+
+    def spread(origin, source):
+        for chip in (3, 1, 2):
+            over_plane(chip, origin, source).start()
+        to_partner(0, origin, source).start()
+
+    goes_on = ((True, place < top), (False, place > 0))
+    for up, there in goes_on:
+
+        @pl.when(there)
+        def _():
+            along(up, place, True).start()
+
+    spread(place, piece_ref)
+    for up, there in goes_on:
+
+        @pl.when(there)
+        def _():
+            along_pack(up, place, True).start()
+
+    for step in range(1, depth):
+        for up, further in goes_on:
+            origin = place - step if up else place + step
+            came = origin >= 0 if up else origin <= top
+
+            @pl.when(came & further)
+            def _():
+                along(up, origin).wait_recv()
+                along(up, origin).start()
+                spread(origin, weight_ref.at[mine, origin])
+
+            @pl.when(came & jnp.logical_not(further))
+            def _():
+                along(up, origin).wait_recv()
+                spread(origin, weight_ref.at[mine, origin])
+
+    for step in range(1, depth):
+        for up, further in goes_on:
+            origin = place - step if up else place + step
+            came = origin >= 0 if up else origin <= top
+
+            @pl.when(came & further)
+            def _():
+                along_pack(up, origin).wait_recv()
+                along_pack(up, origin).start()
+
+            @pl.when(came & jnp.logical_not(further))
+            def _():
+                along_pack(up, origin).wait_recv()
+
+    for origin in range(depth):
+        for chip in (1, 2, 3):
+            here = weight_ref.at[chips[chip] + core, origin]
+            arrived(here, plane_recv.at[chip - 1, origin])
+            to_partner(chip, origin, here).start()
+    for origin in range(depth):
+        for chip in range(4):
+            arrived(weight_ref.at[chips[chip] + 1 - core, origin], pair_recv.at[chip, origin])
     for copy in local:
         copy.wait()
-    for copy in sent:
-        copy.wait_send()
-
-
-def gather_line(piece, pack, depth):
+    for origin in range(depth):
+        here = weight_ref.at[mine, origin]
+        for chip in (1, 2, 3):
+            over_plane(chip, origin, here).wait_send()
+        for chip in range(4):
+            to_partner(chip, origin, here).wait_send()
+        for up, further in goes_on:
+            passed = (origin <= place) if up else (origin >= place)
+
+            @pl.when(further & passed)
+            def _():
+                along(up, origin).wait_send()
+                along_pack(up, origin).wait_send()
+
+
+def gather_start(piece, pack, parts, depth):
     dma = pltpu.SemaphoreType.DMA
     return pl.pallas_call(
-        line_kernel,
+        start_kernel,
         out_shape=(
-            jax.ShapeDtypeStruct((depth,) + piece.shape, piece.dtype),
+            jax.ShapeDtypeStruct((parts, depth) + piece.shape, piece.dtype),
             jax.ShapeDtypeStruct((depth,) + pack.shape, pack.dtype),
         ),
         in_specs=[pl.BlockSpec(memory_space=pltpu.VMEM)] * 2,
-        out_specs=[pl.BlockSpec(memory_space=pltpu.VMEM)] * 2,
-        scratch_shapes=[dma((2, depth - 1)), dma((2, depth - 1)), dma((2,))],
+        out_specs=[pl.BlockSpec(memory_space=pl.ANY)] * 2,
+        scratch_shapes=[
+            dma((2, depth)),
+            dma((depth,)),
+            dma((2, depth)),
+            dma((depth,)),
+            dma((3, depth)),
+            dma((3, depth)),
+            dma((4, depth)),
+            dma((4, depth)),
+            dma((2,)),
+        ],
         compiler_params=pltpu.CompilerParams(
-            collective_id=1, has_side_effects=True, vmem_limit_bytes=4 << 20
+            collective_id=1, has_side_effects=True, vmem_limit_bytes=60 << 20
         ),
-        cost_estimate=pl.CostEstimate(flops=0, transcendentals=0, bytes_accessed=30 << 20),
-        name="line",
+        cost_estimate=pl.CostEstimate(flops=0, transcendentals=0, bytes_accessed=80 << 20),
+        name="start",
     )(piece, pack)
-
-
-def plane_kernel(
-    column_ref, weight_ref, plane_send, plane_recv, pair_send, pair_recv, local_sem
-):
-    place, mine, core, chips, lines = neighbours()
-    depth = column_ref.shape[0]
-    partner, plane, _ = all_peers(place, core, chips, lines)
-    local = pltpu.make_async_copy(column_ref, weight_ref.at[mine], local_sem)
-    local.start()
-    greet([partner] + plane)
-    sent = []
-
-    def send(*items):
-        copy = copy_to(*items)
-        copy.start()
-        sent.append(copy)
-
-    def arrived(here, semaphore):
-        copy_to(here, here, local_sem, semaphore, partner).wait_recv()
-
-    for spot in range(depth):
-        for chip in (3, 1, 2):
-            send(
-                column_ref.at[spot],
-                weight_ref.at[mine, spot],
-                plane_send.at[chip - 1, spot],
-                plane_recv.at[chip - 1, spot],
-                plane[chip - 1],
-            )
-    for spot in range(depth):
-        send(
-            column_ref.at[spot],
-            weight_ref.at[mine, spot],
-            pair_send.at[0, spot],
-            pair_recv.at[0, spot],
-            partner,
-        )
-    for spot in range(depth):
-        for chip in (1, 2, 3):
-            here = weight_ref.at[chips[chip] + core, spot]
-            arrived(here, plane_recv.at[chip - 1, spot])
-            send(here, here, pair_send.at[chip, spot], pair_recv.at[chip, spot], partner)
-    for spot in range(depth):
-        for chip in range(4):
-            arrived(weight_ref.at[chips[chip] + 1 - core, spot], pair_recv.at[chip, spot])
-    local.wait()
-    for copy in sent:
-        copy.wait_send()
-
-
-def gather_plane(column, parts):
-    depth = column.shape[0]
-    dma = pltpu.SemaphoreType.DMA
-    return pl.pallas_call(
-        plane_kernel,
-        out_shape=jax.ShapeDtypeStruct((parts,) + column.shape, column.dtype),
-        in_specs=[pl.BlockSpec(memory_space=pltpu.VMEM)],
-        out_specs=pl.BlockSpec(memory_space=pl.ANY),
-        scratch_shapes=[dma((3, depth)), dma((3, depth)), dma((4, depth)), dma((4, depth)), dma],
-        compiler_params=pltpu.CompilerParams(
-            collective_id=5, has_side_effects=True, vmem_limit_bytes=60 << 20
-        ),
-        cost_estimate=pl.CostEstimate(flops=0, transcendentals=0, bytes_accessed=60 << 20),
-        name="plane",
-    )(column)
 
 
 def slice_kernel(count, first, *refs):
@@ -1710,18 +1780,16 @@
         jnp.concatenate([exp_gate[:, span], exp_up[:, span], exp_down[span].T], axis=0)
         for span in (slice(low, high) for low, high in zip(edges, edges[1:]))
     ]
+    gathered = [
+        lax.all_gather(triple, "dp", axis=0, tiled=True).reshape((depth,) + triple.shape)
+        for triple in triples[:2]
+    ]
     both = jnp.concatenate([qkv_weight, out_weight], axis=1)
     piece = lax.dynamic_slice_in_dim(both, mine * part_width, part_width, axis=1)
     pack = pack_small(router, const_w, gain_attn, gain_moe, const_v)
     pack_width = pl.cdiv(own_rows, LANES) * LANES
     pack = jnp.pad(pack, ((0, 0), (0, pack_width - own_rows)))
-    column, small = gather_line(piece, pack, depth)
-    column, small, *triples[:2] = lax.optimization_barrier((column, small, *triples[:2]))
-    gathered = [
-        lax.all_gather(triple, "dp", axis=0, tiled=True).reshape((depth,) + triple.shape)
-        for triple in triples[:2]
-    ]
-    weights = gather_plane(column, parts)
+    weights, small = gather_start(piece, pack, parts, depth)
     weights = weights.reshape(parts, features, part_width)
     small = small[:, :, :own_rows].transpose(1, 0, 2).reshape(SMALL_ROWS, features)
     cosine, sine = rotary_tables(tokens, features // HEADS)

time: 398 us -> 393 us (0.987)
  Pallas kernels: 358 us -> 353 us
    pallas_call x2 -> x1, Pallas kernels: 53.9 us -> 46.1 us  [gather_start(): pl.pallas_call(start_kernel, out_shape=(jax.ShapeDtypeStruct((parts, dept...]
    pallas_call x2, Pallas kernels: 44.7 us -> 51.6 us  [swap_rows(): pl.pallas_call(swap_kernel, out_shape=jax.ShapeDtypeStruct(rows.shape, ro...]
    pallas_call x1, Pallas kernels: 115 us -> 111 us  [exchange(): pl.pallas_call(exchange_kernel, out_shape=(jax.ShapeDtypeStruct((rows, wi...]
  transfers between devices with their start and end apart: 3 -> 3, of which waited for: 0 -> 0; matrix products, arithmetic and copies ran while one was open for 4% -> 5% of each run, Pallas kernels for 80% -> 84%
where the time goes in v7:
time: 393 us; the launch traced here: 392 us
  Pallas kernels  353 us (90%)
  local copies, waits for them, and re-layouts  14.6 us (4%)
  between operations  14.1 us (4%)
  other arithmetic  10.8 us (3%)
    pallas_call x1, Pallas kernels, exchange(): pl.pallas_call(exchange_kernel, out_shape=(jax.ShapeDtypeStruct((rows, wi...  111 us
    pallas_call x1, Pallas kernels, reduce_tail(): pl.pallas_call(tail_kernel, out_shape=(jax.ShapeDtypeStruct((parts, rows,...  71.2 us
    pallas_call x2, Pallas kernels, swap_rows(): pl.pallas_call(swap_kernel, out_shape=jax.ShapeDtypeStruct(rows.shape, ro...  51.6 us
    pallas_call x1, Pallas kernels, gather_start(): pl.pallas_call(start_kernel, out_shape=(jax.ShapeDtypeStruct((parts, dept...  46.1 us
    pallas_call x2, Pallas kernels, run_slice(): pl.pallas_call(body, out_shape=out_shape, in_specs=[pl.BlockSpec(memory_s...  34.9 us
    pallas_call x1, Pallas kernels, run_after(): pl.pallas_call(after_kernel, out_shape=(jax.ShapeDtypeStruct((tokens, fea...  23.2 us
    pallas_call x1, Pallas kernels, run_before(): pl.pallas_call(before_kernel, out_shape=(low, low, low, low, jax.ShapeDty...  14.9 us
  transfers between devices with their start and end apart: 3, of which 0 were waited for; matrix products, arithmetic and copies ran while one was open for 5% of the time, Pallas kernels for 84%

profile of v7, /device:TPU:9, one launch (start us, length us, event | category | flops | bytes accessed | tf_op | source)
XLA Modules:
  0.0 392.3 jit_solution(10200868516244990562)
XLA Ops:
  7.2 1.0 slice_bitcast_fusion.1
  8.3 1.0 pad_maximum_fusion.2
  12.3 0.8 copy.43.cos_ref
  13.1 0.8 copy.40.prev_ref
  13.9 0.8 copy.41.routes_ref
  14.7 0.8 copy.42.column_ref
  17.0 46.1 %start.1 = (bf16[8,4,192,384]{3,2,1,0:T(8,128)(2,1)}, bf16[4,96,256]{2,1,0:T(8,128)(2,1)}) custom-call(bf16[192,384]{1,0:T(8,128)(2,1)} %fusion.3.piece_ref, bf16[96,256]{1,0:T(8,128)(2,1)} %pad.8.pack_ref), custom_call_target="tpu_custom_call" | custom-call | bytes 83886080 | tf_op jit(solution)/shard_map/start/pallas_call | solution.py:1167
  63.1 0.9 slice_bitcast_fusion.2
  64.2 0.9 reshape.69.small_ref
  65.1 14.9 %before.1 = (bf16[256,768]{1,0:T(8,128)(2,1)}, bf16[256,768]{1,0:T(8,128)(2,1)}, bf16[256,768]{1,0:T(8,128)(2,1)}, bf16[256,768]{1,0:T(8,128)(2,1)}, f32[256,768...) custom-call(bf16[256,768]{1,0:T(8,128)(2,1)} %input_ref.3, f32[256,12]{1,0:T(8,128)} %copy.40.prev_ref, ...), custom_call_target="tpu_custom_call" | custom-call | flops 1207959552 | bytes 20971520 | tf_op jit(solution)/shard_map/before/pallas_call | solution.py:912
  80.0 24.6 %swap.2.refs_0_ = bf16[8,2,64,768]{3,2,1,0:T(8,128)(2,1)} custom-call(bf16[8,2,64,768]{3,2,1,0:T(8,128)(2,1)} %get-tuple-element.44.rows_ref), custom_call_target="tpu_custom_call" | custom-call | bytes 52428800 | tf_op jit(solution)/shard_map/swap/pallas_call | solution.py:1740
  104.6 1.1 pad_maximum_fusion.1.weight_ref
  105.7 13.6 %experts.2 = (bf16[4,576,768]{2,1,0:T(8,128)(2,1)}, f32[512,768]{1,0:T(8,128)}, f32[512,768]{1,0:T(8,128)}) custom-call(bf16[8,2,64,768]{3,2,1,0:T(8,128)(2,1)} %swap.2.refs_0_, bf16[4,576,768]{2,1,0:T(8,128)(2,1)} %bitcast.54), custom_call_target="tpu_custom_call" | custom-call | flops 5435817984 | bytes 16777216 | tf_op jit(solution)/shard_map/experts/pallas_call | solution.py:1296
  119.4 110.6 %exchange.1 = (f32[576,768]{1,0:T(8,128)}, bf16[4,576,1024]{2,1,0:T(8,128)(2,1)}) custom-call(bf16[4,576,768]{2,1,0:T(8,128)(2,1)} %get-tuple-element.45.grad_ref, bf16[576,1024]{1,0:T(8,128)(2,1)} %pad_maximum_fusion.1.weight_ref), custom_call_target="tpu_custom_call" | custom-call | bytes 262144000 | tf_op jit(solution)/shard_map/exchange/pallas_call | solution.py:1491
  230.0 21.3 %experts.3 = (bf16[4,576,1280]{2,1,0:T(8,128)(2,1)}, bf16[8,2,64,768]{3,2,1,0:T(8,128)(2,1)}) custom-call(bf16[8,2,64,768]{3,2,1,0:T(8,128)(2,1)} %swap.2.refs_0_, bf16[4,576,256]{2,1,0:T(8,128)(2,1)} %bitcast.55, bf16[4,576,1024]{2,1,0:T(8,128)(2,1)} %get-tuple-element.46.refs_2_, f32[512,768]{1,0:T(8,128)} %get-tuple-element.47.refs_3_, ...), custom_call_target="tpu_custom_call" | custom-call | flops 9059696640 | bytes 16777216 | tf_op jit(solution)/shard_map/experts/pallas_call | solution.py:1296
  251.3 27.0 %swap.3.back_ref = bf16[8,2,64,768]{3,2,1,0:T(8,128)(2,1)} custom-call(bf16[8,2,64,768]{3,2,1,0:T(8,128)(2,1)} %get-tuple-element.49.rows_ref), custom_call_target="tpu_custom_call" | custom-call | bytes 52428800 | tf_op jit(solution)/shard_map/swap/pallas_call | solution.py:1740
  278.3 23.2 %after.1 = (bf16[256,768]{1,0:T(8,128)(2,1)}, f32[256,768]{1,0:T(8,128)}, f32[256,12]{1,0:T(8,128)}, bf16[8,768,384]{2,1,0:T(8,128)(2,1)}, f32[32,768]{1,0:T(8,128)}) custom-call(bf16[256,768]{1,0:T(8,128)(2,1)} %input_ref.3, f32[256,12]{1,0:T(8,128)} %copy.40.prev_ref, s32[256,2]{1,0:T(8,128)} %copy.41.routes_ref, s32[256,1]{1,0:T(8,128)} %copy.42.column_ref, ...), custom_call_target="tpu_custom_call" | custom-call | flops 2415919104 | bytes 62914560 | tf_op jit(solution)/shard_map/after/pallas_call | solution.py:939
  301.5 0.9 convert_element_type.22
  303.2 71.2 %tail.1 = (bf16[8,192,384]{2,1,0:T(8,128)(2,1)}, f32[32,256]{1,0:T(8,128)}) custom-call(bf16[8,4,192,384]{3,2,1,0:T(8,128)(2,1)} %bitcast.43, bf16[4,32,256]{2,1,0:T(8,128)(2,1)} %pad.9.small_ref), custom_call_target="tpu_custom_call" | custom-call | bytes 125829120 | tf_op jit(solution)/shard_map/tail/pallas_call | solution.py:1667
  374.4 1.5 convert_bitcast_fusion
  376.2 0.9 slice.95
  377.0 1.3 slice.94
  381.5 1.7 bitcast_convert_fusion
  383.4 2.4 fusion.2
  (80 shorter events, 8.9 us)
Async XLA Ops:
  7.2 1.1 slice-start
  7.2 1.1 slice-start.3
  7.2 98.5 %all-gather.5.cloned.1.call-start = ((), (), s32[]{:S(2)}) async-start(), calls=%async_computation.2 | async-start | bytes 4423680 | tf_op jit(solution)/shard_map/all_gather | solution.py:1784
  8.3 1.5 copy-start.2
  8.3 1.5 slice-start.1
  8.3 1.5 slice-start.4
  9.3 1.3 copy-start.10
  9.3 1.4 copy-start.12
  9.4 1.4 copy-start.13
  9.4 1.4 copy-start.8
  9.4 1.4 copy-start.11
  9.4 220.6 %all-gather.3.cloned.1.call-start = ((), (), s32[]{:S(2)}) async-start(), calls=%async_computation.1 | async-start | bytes 1474560 | tf_op jit(solution)/shard_map/all_gather | solution.py:1784
  10.6 2.6 copy-start.5
  10.6 3.3 copy-start.9
  10.6 4.1 %copy-start.7 = (s32[1,256]{1,0:T(1,128)S(1)}, s32[1,256]{1,0:T(1,128)}, u32[]{:S(2)}) copy-start(s32[1,256]{1,0:T(1,128)} %row_ref.3) | copy-start | bytes 3076
  10.6 370.9 %reduce-scatter.2.cloned.1.call-start = ((), (), s32[]{:S(2)}) async-start(), calls=%async_computation.3 | async-start | bytes 7372800 | tf_op jit(solution)/shard_map/reduce_scatter | solution.py:1813
  10.7 5.5 %copy-start.1 = (bf16[192,2304]{1,0:T(8,128)(2,1)S(1)}, bf16[192,2304]{1,0:T(8,128)(2,1)}, u32[]{:S(2)}) copy-start(bf16[192,2304]{1,0:T(8,128)(2,1)} %param.21) | copy-start | bytes 2654212
  10.7 5.5 %copy-start.3 = (bf16[192,768]{1,0:T(8,128)(2,1)S(1)}, bf16[192,768]{1,0:T(8,128)(2,1)}, u32[]{:S(2)}) copy-start(bf16[192,768]{1,0:T(8,128)(2,1)} %param.22) | copy-start | bytes 884740
  80.0 24.6 %slice-start.2 = ((bf16[192,2048]{1,0:T(8,128)(2,1)}), bf16[192,1024]{1,0:T(8,128)(2,1)S(1)}, s32[]{:S(2)}) async-start(bf16[192,2048]{1,0:T(8,128)(2,1)} %param.27), calls=%async_computation.6 | async-start | bytes 786432 | tf_op jit(solution)/shard_map/slice | solution.py:1780
  80.0 24.6 %slice-start.5 = ((bf16[192,2048]{1,0:T(8,128)(2,1)}), bf16[192,1024]{1,0:T(8,128)(2,1)S(1)}, s32[]{:S(2)}) async-start(bf16[192,2048]{1,0:T(8,128)(2,1)} %param.28), calls=%async_computation.9 | async-start | bytes 786432 | tf_op jit(solution)/shard_map/slice | solution.py:1780
  377.0 1.3 copy-start.4
  377.0 2.0 copy-start.6
  381.4 1.9 copy-start
Sparse Core Ops, SparseCore 0:
  10.2 79.7 all-gather.4
  92.1 30.8 all-gather.2
  251.4 124.1 reduce-scatter.1

commit v8 on v7

--- a/solution.py
+++ b/solution.py
@@ -1486,7 +1486,7 @@
 
 def exchange(grads, weights):
     depth, rows, width = grads.shape
-    pieces = 6
+    pieces = 9
     dma = pltpu.SemaphoreType.DMA
     return pl.pallas_call(
         exchange_kernel,
@@ -1775,15 +1775,14 @@
     part_width = 4 * features // parts
     mine = lax.axis_index("expert")
     hidden_units = exp_gate.shape[1]
-    edges = (0, 3 * hidden_units // 8, hidden_units // 2, hidden_units)
+    edges = (0, hidden_units // 2, hidden_units)
     triples = [
         jnp.concatenate([exp_gate[:, span], exp_up[:, span], exp_down[span].T], axis=0)
         for span in (slice(low, high) for low, high in zip(edges, edges[1:]))
     ]
-    gathered = [
-        lax.all_gather(triple, "dp", axis=0, tiled=True).reshape((depth,) + triple.shape)
-        for triple in triples[:2]
-    ]
+    gathered_first = lax.all_gather(triples[0], "dp", axis=0, tiled=True).reshape(
+        (depth,) + triples[0].shape
+    )
     both = jnp.concatenate([qkv_weight, out_weight], axis=1)
     piece = lax.dynamic_slice_in_dim(both, mine * part_width, part_width, axis=1)
     pack = pack_small(router, const_w, gain_attn, gain_moe, const_v)
@@ -1807,9 +1806,9 @@
     )
     *saved, rows = run_before(common, parts, part_width)
     received = swap_rows(rows)
-    grads, *sums = run_slice(received, gathered[:1], ())
-    own_first, gathered_last = exchange(grads, triples[2])
-    grads, back = run_slice(received, [gathered[1], gathered_last], tuple(sums))
+    grads, *sums = run_slice(received, [gathered_first], ())
+    own_first, gathered_last = exchange(grads, triples[1])
+    grads, back = run_slice(received, [gathered_last], tuple(sums))
     own_last = lax.psum_scatter(grads, "dp", scatter_dimension=0, tiled=False)
     returned = swap_rows(back)
     result, grad_input, grad_prev, grad_weights, grad_small = run_after(

time: 393 us -> 391 us (level)
  Pallas kernels: 353 us -> 347 us
  waiting for transfers between devices: 0.07 us -> 4.74 us
    pallas_call x1, Pallas kernels: 71.2 us -> 65.9 us  [reduce_tail(): pl.pallas_call(tail_kernel, out_shape=(jax.ShapeDtypeStruct((parts, rows,...]
    pallas_call x1, Pallas kernels: 111 us -> 115 us  [exchange(): pl.pallas_call(exchange_kernel, out_shape=(jax.ShapeDtypeStruct((rows, wi...]
    all_gather x2 -> x1, waiting for transfers between devices: 0.02 us -> 4.71 us  [local_fast(): lax.all_gather(triples[0], 'dp', axis=0, tiled=True)]
    pallas_call x2, Pallas kernels: 51.6 us -> 47.2 us  [swap_rows(): pl.pallas_call(swap_kernel, out_shape=jax.ShapeDtypeStruct(rows.shape, ro...]
  transfers between devices with their start and end apart: 3 -> 2, of which waited for: 0 -> 1; matrix products, arithmetic and copies ran while one was open for 5% -> 5% of each run, Pallas kernels for 84% -> 50%
where the time goes in v8:
time: 391 us
  Pallas kernels  347 us (89%)
  local copies, waits for them, and re-layouts  15 us (4%)
  between operations  14.4 us (4%)
  other arithmetic  10 us (3%)
  waiting for transfers between devices  4.74 us (1%)
    pallas_call x1, Pallas kernels, exchange(): pl.pallas_call(exchange_kernel, out_shape=(jax.ShapeDtypeStruct((rows, wi...  115 us
    pallas_call x1, Pallas kernels, reduce_tail(): pl.pallas_call(tail_kernel, out_shape=(jax.ShapeDtypeStruct((parts, rows,...  65.9 us
    pallas_call x2, Pallas kernels, swap_rows(): pl.pallas_call(swap_kernel, out_shape=jax.ShapeDtypeStruct(rows.shape, ro...  47.2 us
    pallas_call x1, Pallas kernels, gather_start(): pl.pallas_call(start_kernel, out_shape=(jax.ShapeDtypeStruct((parts, dept...  45.3 us
    pallas_call x2, Pallas kernels, run_slice(): pl.pallas_call(body, out_shape=out_shape, in_specs=[pl.BlockSpec(memory_s...  34.5 us
    pallas_call x1, Pallas kernels, run_after(): pl.pallas_call(after_kernel, out_shape=(jax.ShapeDtypeStruct((tokens, fea...  23.3 us
    pallas_call x1, Pallas kernels, run_before(): pl.pallas_call(before_kernel, out_shape=(low, low, low, low, jax.ShapeDty...  15 us
  transfers between devices with their start and end apart: 2, of which 1 were waited for; matrix products, arithmetic and copies ran while one was open for 5% of the time, Pallas kernels for 50%

profile of v8, /device:TPU:9, one launch (start us, length us, event | category | flops | bytes accessed | tf_op | source)
XLA Modules:
  0.0 390.7 jit_solution(9767071094164622903)
XLA Ops:
  7.2 1.3 slice_bitcast_fusion
  9.0 1.1 pad_maximum_fusion.1
  12.6 0.8 copy.40.prev_ref
  13.4 0.8 copy.41.routes_ref
  14.2 0.8 copy.42.column_ref
  16.5 45.3 %start.1 = (bf16[8,4,192,384]{3,2,1,0:T(8,128)(2,1)}, bf16[4,96,256]{2,1,0:T(8,128)(2,1)}) custom-call(bf16[192,384]{1,0:T(8,128)(2,1)} %fusion.3.piece_ref, bf16[96,256]{1,0:T(8,128)(2,1)} %pad.8.pack_ref), custom_call_target="tpu_custom_call" | custom-call | bytes 83886080 | tf_op jit(solution)/shard_map/start/pallas_call | solution.py:1167
  61.8 0.9 slice_bitcast_fusion.2
  63.0 0.9 reshape.66.small_ref
  63.8 15.0 %before.1 = (bf16[256,768]{1,0:T(8,128)(2,1)}, bf16[256,768]{1,0:T(8,128)(2,1)}, bf16[256,768]{1,0:T(8,128)(2,1)}, bf16[256,768]{1,0:T(8,128)(2,1)}, f32[256,768...) custom-call(bf16[256,768]{1,0:T(8,128)(2,1)} %input_ref.3, f32[256,12]{1,0:T(8,128)} %copy.40.prev_ref, ...), custom_call_target="tpu_custom_call" | custom-call | flops 1207959552 | bytes 20971520 | tf_op jit(solution)/shard_map/before/pallas_call | solution.py:912
  78.8 24.0 %swap.2.refs_0_ = bf16[8,2,64,768]{3,2,1,0:T(8,128)(2,1)} custom-call(bf16[8,2,64,768]{3,2,1,0:T(8,128)(2,1)} %get-tuple-element.44.rows_ref), custom_call_target="tpu_custom_call" | custom-call | bytes 52428800 | tf_op jit(solution)/shard_map/swap/pallas_call | solution.py:1740
  102.8 1.1 pad_maximum_fusion.2.weight_ref
  103.9 4.7 %all-gather.2.cloned.1.call-done = bf16[2304,1024]{1,0:T(8,128)(2,1)} async-done(((bf16[576,1024]{1,0:T(8,128)(2,1)}), bf16[2304,1024]{1,0:T(8,128)(2,1)}) %all-gather.2.cloned.1.call-update) | async-done | bytes 4718608 | tf_op jit(solution)/shard_map/all_gather | solution.py:1783
  108.6 16.9 %experts.2 = (bf16[4,576,1024]{2,1,0:T(8,128)(2,1)}, f32[512,768]{1,0:T(8,128)}, f32[512,768]{1,0:T(8,128)}) custom-call(bf16[8,2,64,768]{3,2,1,0:T(8,128)(2,1)} %swap.2.refs_0_, bf16[4,576,1024]{2,1,0:T(8,128)(2,1)} %bitcast.51), custom_call_target="tpu_custom_call" | custom-call | flops 7247757312 | bytes 16777216 | tf_op jit(solution)/shard_map/experts/pallas_call | solution.py:1296
  125.5 115.3 %exchange.1 = (f32[576,1024]{1,0:T(8,128)}, bf16[4,576,1024]{2,1,0:T(8,128)(2,1)}) custom-call(bf16[4,576,1024]{2,1,0:T(8,128)(2,1)} %get-tuple-element.45.grad_ref, bf16[576,1024]{1,0:T(8,128)(2,1)} %pad_maximum_fusion.2.weight_ref), custom_call_target="tpu_custom_call" | custom-call | bytes 262144000 | tf_op jit(solution)/shard_map/exchange/pallas_call | solution.py:1491
  240.8 17.6 %experts.3 = (bf16[4,576,1024]{2,1,0:T(8,128)(2,1)}, bf16[8,2,64,768]{3,2,1,0:T(8,128)(2,1)}) custom-call(bf16[8,2,64,768]{3,2,1,0:T(8,128)(2,1)} %swap.2.refs_0_, bf16[4,576,1024]{2,1,0:T(8,128)(2,1)} %get-tuple-element.46.refs_1_, f32[512,768]{1,0:T(8,128)} %get-tuple-element.47.refs_2_, f32[512,768]{1,0:T(8,128)} %get-tuple-element.48.refs_3_), custom_call_target="tpu_custom_call" | custom-call | flops 7247757312 | bytes 16777216 | tf_op jit(solution)/shard_map/experts/pallas_call | solution.py:1296
  258.5 23.2 %swap.3.back_ref = bf16[8,2,64,768]{3,2,1,0:T(8,128)(2,1)} custom-call(bf16[8,2,64,768]{3,2,1,0:T(8,128)(2,1)} %get-tuple-element.49.rows_ref), custom_call_target="tpu_custom_call" | custom-call | bytes 52428800 | tf_op jit(solution)/shard_map/swap/pallas_call | solution.py:1740
  281.7 23.3 %after.1 = (bf16[256,768]{1,0:T(8,128)(2,1)}, f32[256,768]{1,0:T(8,128)}, f32[256,12]{1,0:T(8,128)}, bf16[8,768,384]{2,1,0:T(8,128)(2,1)}, f32[32,768]{1,0:T(8,128)}) custom-call(bf16[256,768]{1,0:T(8,128)(2,1)} %input_ref.3, f32[256,12]{1,0:T(8,128)} %copy.40.prev_ref, s32[256,2]{1,0:T(8,128)} %copy.41.routes_ref, s32[256,1]{1,0:T(8,128)} %copy.42.column_ref, ...), custom_call_target="tpu_custom_call" | custom-call | flops 2415919104 | bytes 62914560 | tf_op jit(solution)/shard_map/after/pallas_call | solution.py:939
  305.0 0.9 convert_element_type.22
  306.7 65.9 %tail.1 = (bf16[8,192,384]{2,1,0:T(8,128)(2,1)}, f32[32,256]{1,0:T(8,128)}) custom-call(bf16[8,4,192,384]{3,2,1,0:T(8,128)(2,1)} %bitcast.40, bf16[4,32,256]{2,1,0:T(8,128)(2,1)} %pad.9.small_ref), custom_call_target="tpu_custom_call" | custom-call | bytes 125829120 | tf_op jit(solution)/shard_map/tail/pallas_call | solution.py:1667
  372.6 1.4 convert_bitcast_fusion
  374.3 0.9 slice.83
  375.2 1.3 slice.82
  379.6 1.7 bitcast_convert_fusion
  381.6 2.3 fusion.2
  (65 shorter events, 9.0 us)
Async XLA Ops:
  7.2 1.4 copy-start.3
  7.2 1.6 copy-start.2
  7.2 101.4 %all-gather.2.cloned.1.call-start = ((), (), s32[]{:S(2)}) async-start(), calls=%async_computation.1 | async-start | bytes 5898240 | tf_op jit(solution)/shard_map/all_gather | solution.py:1783
  8.9 1.3 copy-start.11
  9.0 1.3 copy-start.13
  9.0 1.3 copy-start.14
  9.0 1.4 copy-start.9
  9.0 1.4 copy-start.12
  10.1 2.5 copy-start.6
  10.1 3.3 copy-start.10
  10.1 4.1 %copy-start.8 = (s32[1,256]{1,0:T(1,128)S(1)}, s32[1,256]{1,0:T(1,128)}, u32[]{:S(2)}) copy-start(s32[1,256]{1,0:T(1,128)} %row_ref.3) | copy-start | bytes 3076
  10.1 5.7 %copy-start.1 = (bf16[192,2304]{1,0:T(8,128)(2,1)S(1)}, bf16[192,2304]{1,0:T(8,128)(2,1)}, u32[]{:S(2)}) copy-start(bf16[192,2304]{1,0:T(8,128)(2,1)} %param.21) | copy-start | bytes 2654212
  10.1 5.7 %copy-start.4 = (bf16[192,768]{1,0:T(8,128)(2,1)S(1)}, bf16[192,768]{1,0:T(8,128)(2,1)}, u32[]{:S(2)}) copy-start(bf16[192,768]{1,0:T(8,128)(2,1)} %param.22) | copy-start | bytes 884740
  10.2 369.4 %reduce-scatter.2.cloned.1.call-start = ((), (), s32[]{:S(2)}) async-start(), calls=%async_computation.2 | async-start | bytes 5898240 | tf_op jit(solution)/shard_map/reduce_scatter | solution.py:1812
  375.2 1.3 copy-start.5
  375.2 2.0 copy-start.7
  379.6 2.0 copy-start
Sparse Core Ops, SparseCore 0:
  10.3 98.2 all-gather.1
  258.6 101.3 reduce-scatter.1

commit v9 on v8

--- a/solution.py
+++ b/solution.py
@@ -1171,7 +1171,7 @@
             jax.ShapeDtypeStruct((depth,) + pack.shape, pack.dtype),
         ),
         in_specs=[pl.BlockSpec(memory_space=pltpu.VMEM)] * 2,
-        out_specs=[pl.BlockSpec(memory_space=pl.ANY)] * 2,
+        out_specs=[pl.BlockSpec(memory_space=pltpu.VMEM)] * 2,
         scratch_shapes=[
             dma((2, depth)),
             dma((depth,)),
@@ -1486,7 +1486,7 @@
 
 def exchange(grads, weights):
     depth, rows, width = grads.shape
-    pieces = 9
+    pieces = 6
     dma = pltpu.SemaphoreType.DMA
     return pl.pallas_call(
         exchange_kernel,
@@ -1497,7 +1497,7 @@
         in_specs=[pl.BlockSpec(memory_space=pltpu.VMEM)] * 2,
         out_specs=[
             pl.BlockSpec(memory_space=pltpu.VMEM),
-            pl.BlockSpec(memory_space=pl.ANY),
+            pl.BlockSpec(memory_space=pltpu.VMEM),
         ],
         scratch_shapes=[pltpu.VMEM(grads.shape, grads.dtype)] * 2
         + [dma((depth, pieces))] * 8
@@ -1671,7 +1671,7 @@
             jax.ShapeDtypeStruct(small.shape[1:], jnp.float32),
         ),
         in_specs=[
-            pl.BlockSpec(memory_space=pl.ANY),
+            pl.BlockSpec(memory_space=pltpu.VMEM),
             pl.BlockSpec(memory_space=pltpu.VMEM),
         ],
         out_specs=[pl.BlockSpec(memory_space=pltpu.VMEM)] * 2,
@@ -1740,8 +1740,8 @@
     return pl.pallas_call(
         swap_kernel,
         out_shape=jax.ShapeDtypeStruct(rows.shape, rows.dtype),
-        in_specs=[pl.BlockSpec(memory_space=pl.ANY)],
-        out_specs=pl.BlockSpec(memory_space=pl.ANY),
+        in_specs=[pl.BlockSpec(memory_space=pltpu.VMEM)],
+        out_specs=pl.BlockSpec(memory_space=pltpu.VMEM),
         scratch_shapes=[dma((4, 2)), dma((4, 2)), dma],
         compiler_params=pltpu.CompilerParams(
             collective_id=4, has_side_effects=True, vmem_limit_bytes=60 << 20

time: 391 us -> 398 us (1.018)
  Pallas kernels: 347 us -> 358 us
  waiting for transfers between devices: 4.74 us -> 0.04 us
    pallas_call x2, Pallas kernels: 47.2 us -> 54.8 us  [swap_rows(): pl.pallas_call(swap_kernel, out_shape=jax.ShapeDtypeStruct(rows.shape, ro...]
    pallas_call x1, Pallas kernels: 115 us -> 121 us  [exchange(): pl.pallas_call(exchange_kernel, out_shape=(jax.ShapeDtypeStruct((rows, wi...]
    all_gather x1, waiting for transfers between devices: 4.71 us -> 0.01 us  [local_fast(): lax.all_gather(triples[0], 'dp', axis=0, tiled=True)]
  transfers between devices with their start and end apart: 2 -> 2, of which waited for: 1 -> 0; matrix products, arithmetic and copies ran while one was open for 5% -> 4% of each run, Pallas kernels for 50% -> 51%
where the time goes in v9:
time: 398 us; the launch traced here: 397 us
  Pallas kernels  358 us (90%)
  local copies, waits for them, and re-layouts  15 us (4%)
  between operations  14.4 us (4%)
  other arithmetic  10 us (3%)
    pallas_call x1, Pallas kernels, exchange(): pl.pallas_call(exchange_kernel, out_shape=(jax.ShapeDtypeStruct((rows, wi...  121 us
    pallas_call x1, Pallas kernels, reduce_tail(): pl.pallas_call(tail_kernel, out_shape=(jax.ShapeDtypeStruct((parts, rows,...  62.2 us
    pallas_call x2, Pallas kernels, swap_rows(): pl.pallas_call(swap_kernel, out_shape=jax.ShapeDtypeStruct(rows.shape, ro...  54.8 us
    pallas_call x1, Pallas kernels, gather_start(): pl.pallas_call(start_kernel, out_shape=(jax.ShapeDtypeStruct((parts, dept...  46.9 us
    pallas_call x2, Pallas kernels, run_slice(): pl.pallas_call(body, out_shape=out_shape, in_specs=[pl.BlockSpec(memory_s...  34.5 us
    pallas_call x1, Pallas kernels, run_after(): pl.pallas_call(after_kernel, out_shape=(jax.ShapeDtypeStruct((tokens, fea...  23.2 us
    pallas_call x1, Pallas kernels, run_before(): pl.pallas_call(before_kernel, out_shape=(low, low, low, low, jax.ShapeDty...  14.9 us
  transfers between devices with their start and end apart: 2, of which 0 were waited for; matrix products, arithmetic and copies ran while one was open for 4% of the time, Pallas kernels for 51%

profile of v9, /device:TPU:9, one launch (start us, length us, event | category | flops | bytes accessed | tf_op | source)
XLA Modules:
  0.0 397.4 jit_solution(9125936777745209185)
XLA Ops:
  7.2 1.3 slice_bitcast_fusion
  9.0 1.1 pad_maximum_fusion.1
  11.9 0.7 copy.43.cos_ref
  12.6 0.8 copy.40.prev_ref
  13.4 0.8 copy.41.routes_ref
  14.2 0.8 copy.42.column_ref
  16.5 46.9 %start.1 = (bf16[8,4,192,384]{3,2,1,0:T(8,128)(2,1)}, bf16[4,96,256]{2,1,0:T(8,128)(2,1)}) custom-call(bf16[192,384]{1,0:T(8,128)(2,1)} %fusion.3.piece_ref, bf16[96,256]{1,0:T(8,128)(2,1)} %pad.8.pack_ref), custom_call_target="tpu_custom_call" | custom-call | bytes 83886080 | tf_op jit(solution)/shard_map/start/pallas_call | solution.py:1167
  63.4 0.9 slice_bitcast_fusion.2
  64.5 0.9 reshape.66.small_ref
  65.4 14.9 %before.1 = (bf16[256,768]{1,0:T(8,128)(2,1)}, bf16[256,768]{1,0:T(8,128)(2,1)}, bf16[256,768]{1,0:T(8,128)(2,1)}, bf16[256,768]{1,0:T(8,128)(2,1)}, f32[256,768...) custom-call(bf16[256,768]{1,0:T(8,128)(2,1)} %input_ref.3, f32[256,12]{1,0:T(8,128)} %copy.40.prev_ref, ...), custom_call_target="tpu_custom_call" | custom-call | flops 1207959552 | bytes 20971520 | tf_op jit(solution)/shard_map/before/pallas_call | solution.py:912
  80.3 28.1 %swap.2.refs_0_ = bf16[8,2,64,768]{3,2,1,0:T(8,128)(2,1)} custom-call(bf16[8,2,64,768]{3,2,1,0:T(8,128)(2,1)} %get-tuple-element.44.rows_ref), custom_call_target="tpu_custom_call" | custom-call | bytes 52428800 | tf_op jit(solution)/shard_map/swap/pallas_call | solution.py:1740
  108.4 1.1 pad_maximum_fusion.2.weight_ref
  109.5 16.9 %experts.2 = (bf16[4,576,1024]{2,1,0:T(8,128)(2,1)}, f32[512,768]{1,0:T(8,128)}, f32[512,768]{1,0:T(8,128)}) custom-call(bf16[8,2,64,768]{3,2,1,0:T(8,128)(2,1)} %swap.2.refs_0_, bf16[4,576,1024]{2,1,0:T(8,128)(2,1)} %bitcast.51), custom_call_target="tpu_custom_call" | custom-call | flops 7247757312 | bytes 16777216 | tf_op jit(solution)/shard_map/experts/pallas_call | solution.py:1296
  126.5 121.3 %exchange.1 = (f32[576,1024]{1,0:T(8,128)}, bf16[4,576,1024]{2,1,0:T(8,128)(2,1)}) custom-call(bf16[4,576,1024]{2,1,0:T(8,128)(2,1)} %get-tuple-element.45.grad_ref, bf16[576,1024]{1,0:T(8,128)(2,1)} %pad_maximum_fusion.2.weight_ref), custom_call_target="tpu_custom_call" | custom-call | bytes 262144000 | tf_op jit(solution)/shard_map/exchange/pallas_call | solution.py:1491
  247.8 17.6 %experts.3 = (bf16[4,576,1024]{2,1,0:T(8,128)(2,1)}, bf16[8,2,64,768]{3,2,1,0:T(8,128)(2,1)}) custom-call(bf16[8,2,64,768]{3,2,1,0:T(8,128)(2,1)} %swap.2.refs_0_, bf16[4,576,1024]{2,1,0:T(8,128)(2,1)} %get-tuple-element.46.refs_1_, f32[512,768]{1,0:T(8,128)} %get-tuple-element.47.refs_2_, f32[512,768]{1,0:T(8,128)} %get-tuple-element.48.refs_3_), custom_call_target="tpu_custom_call" | custom-call | flops 7247757312 | bytes 16777216 | tf_op jit(solution)/shard_map/experts/pallas_call | solution.py:1296
  265.4 26.7 %swap.3.back_ref = bf16[8,2,64,768]{3,2,1,0:T(8,128)(2,1)} custom-call(bf16[8,2,64,768]{3,2,1,0:T(8,128)(2,1)} %get-tuple-element.49.rows_ref), custom_call_target="tpu_custom_call" | custom-call | bytes 52428800 | tf_op jit(solution)/shard_map/swap/pallas_call | solution.py:1740
  292.1 23.2 %after.1 = (bf16[256,768]{1,0:T(8,128)(2,1)}, f32[256,768]{1,0:T(8,128)}, f32[256,12]{1,0:T(8,128)}, bf16[8,768,384]{2,1,0:T(8,128)(2,1)}, f32[32,768]{1,0:T(8,128)}) custom-call(bf16[256,768]{1,0:T(8,128)(2,1)} %input_ref.3, f32[256,12]{1,0:T(8,128)} %copy.40.prev_ref, s32[256,2]{1,0:T(8,128)} %copy.41.routes_ref, s32[256,1]{1,0:T(8,128)} %copy.42.column_ref, ...), custom_call_target="tpu_custom_call" | custom-call | flops 2415919104 | bytes 62914560 | tf_op jit(solution)/shard_map/after/pallas_call | solution.py:939
  315.3 0.9 convert_element_type.22
  317.0 62.2 %tail.1 = (bf16[8,192,384]{2,1,0:T(8,128)(2,1)}, f32[32,256]{1,0:T(8,128)}) custom-call(bf16[8,4,192,384]{3,2,1,0:T(8,128)(2,1)} %bitcast.40, bf16[4,32,256]{2,1,0:T(8,128)(2,1)} %pad.9.small_ref), custom_call_target="tpu_custom_call" | custom-call | bytes 125829120 | tf_op jit(solution)/shard_map/tail/pallas_call | solution.py:1667
  379.3 1.4 convert_bitcast_fusion
  381.0 0.9 slice.83
  381.8 1.3 slice.82
  386.2 1.7 bitcast_convert_fusion
  388.3 2.3 fusion.2
  (65 shorter events, 8.2 us)
Async XLA Ops:
  7.2 1.4 copy-start.3
  7.2 1.6 copy-start.2
  7.2 102.3 %all-gather.2.cloned.1.call-start = ((), (), s32[]{:S(2)}) async-start(), calls=%async_computation.1 | async-start | bytes 5898240 | tf_op jit(solution)/shard_map/all_gather | solution.py:1783
  8.9 1.3 copy-start.11
  9.0 1.3 copy-start.13
  9.0 1.3 copy-start.14
  9.0 1.4 copy-start.9
  9.0 1.4 copy-start.12
  10.1 2.5 copy-start.6
  10.1 3.3 copy-start.10
  10.1 4.1 %copy-start.8 = (s32[1,256]{1,0:T(1,128)S(1)}, s32[1,256]{1,0:T(1,128)}, u32[]{:S(2)}) copy-start(s32[1,256]{1,0:T(1,128)} %row_ref.3) | copy-start | bytes 3076
  10.1 5.7 %copy-start.1 = (bf16[192,2304]{1,0:T(8,128)(2,1)S(1)}, bf16[192,2304]{1,0:T(8,128)(2,1)}, u32[]{:S(2)}) copy-start(bf16[192,2304]{1,0:T(8,128)(2,1)} %param.21) | copy-start | bytes 2654212
  10.1 5.7 %copy-start.4 = (bf16[192,768]{1,0:T(8,128)(2,1)S(1)}, bf16[192,768]{1,0:T(8,128)(2,1)}, u32[]{:S(2)}) copy-start(bf16[192,768]{1,0:T(8,128)(2,1)} %param.22) | copy-start | bytes 884740
  10.2 376.1 %reduce-scatter.2.cloned.1.call-start = ((), (), s32[]{:S(2)}) async-start(), calls=%async_computation.2 | async-start | bytes 5898240 | tf_op jit(solution)/shard_map/reduce_scatter | solution.py:1812
  381.8 1.3 copy-start.5
  381.8 2.0 copy-start.7
  386.2 2.0 copy-start
Sparse Core Ops, SparseCore 0:
  10.3 98.4 all-gather.1
  265.5 98.7 reduce-scatter.1
